TPU v7x, 32 devices: a whole 2x2x4 slice. The times are simulated.
32 devices in a mesh: region: 8 (over y, x, core), member: 4 (over z).
Axes of the slice: x: 2, y: 2, z: 4, core: 2. Of those that a mesh axis runs over, the one named last changes fastest.
Arguments:
- controls: float32 [16, 8, 128, 512], P('member', None, 'region'), may hold values from -6 to 6
- perturbations: float32 [64, 8, 128, 512], P('member', None, 'region'), may hold values from -1.5 to 1.5
- assignment: int32 [64], replicated, may hold values from 0 to 15
- courant: float32 [4, 4, 8, 128, 512], P(None, None, 'member', 'region'), may hold values from 0.02 to 0.24
- innovation: float32 [8, 128, 512], P('member', 'region'), may hold values from -6 to 6
- obs_weight: float32 [8, 128, 512], P('member', 'region'), may hold values from 0.3 to 3
Outputs:
- gradient: float32 [16, 8, 128, 512], P('member', None, 'region')
- departure: float32 [8, 128, 512], P('member', 'region')
All inputs are finite; a program needn't handle non-finite values.
Results may differ from a plain program's by a relative error of at most 0.0001.
Values sent between devices are 32-bit elements; how exact they have to be, the bound alone decides.
No kernel may reach another device: no remote copies, remote signals or barrier semaphores. Data moves between devices by JAX's collectives and lax.ppermute only.
A program may use at most 64 MiB of HBM per device.

v0:
```python
import jax
import jax.numpy as jnp
from jax import lax
from jax.sharding import PartitionSpec as P

FIELDS = 16
PASSES = 16
STEPS = 4


def padded_2(block, sides, width):
    for axis, dim in sides:
        count = lax.axis_size(axis)
        forward = [(i, i + 1) for i in range(count - 1)]
        backward = [(target, source) for source, target in forward]
        low = lax.ppermute(
            lax.slice_in_dim(block, block.shape[dim] - width, None, axis=dim), axis, forward
        )
        high = lax.ppermute(lax.slice_in_dim(block, 0, width, axis=dim), axis, backward)
        block = jnp.concatenate([low, block, high], axis=dim)
    return block


def relax_once(extended):
    padded = jnp.pad(extended, ((0, 0), (0, 0), (1, 1), (0, 0)))
    from_west = jnp.pad(extended[..., :-1], ((0, 0), (0, 0), (0, 0), (1, 0)))
    from_east = jnp.pad(extended[..., 1:], ((0, 0), (0, 0), (0, 0), (0, 1)))
    beside_all = padded[:, :, 2:] + padded[:, :, :-2] + from_west + from_east
    return extended + 0.2 * (beside_all - 4.0 * extended)


def spread(fields, halo_depth, row_start, total_rows):
    row_count = fields.shape[2]
    global_rows = row_start - halo_depth + lax.iota(jnp.int32, row_count + 2 * halo_depth)
    inside = ((global_rows >= 0) & (global_rows < total_rows)).astype(jnp.float32)[:, None]
    for block_index in range(PASSES // halo_depth):
        extended = padded_2(fields, (("region", 2),), halo_depth)
        for repeat in range(halo_depth):
            extended = relax_once(extended) * inside
        fields = extended[:, :, halo_depth : halo_depth + row_count, :]
    return fields


def tangent_step(state, coeffs):
    padded = padded_2(state, (("region", 1),), 1)
    from_west = jnp.pad(state[..., :-1], ((0, 0), (0, 0), (1, 0)))
    from_east = jnp.pad(state[..., 1:], ((0, 0), (0, 0), (0, 1)))
    center = 1.0 - jnp.sum(coeffs, 0)
    return (
        center * state
        + coeffs[0] * padded[:, :-2]
        + coeffs[1] * padded[:, 2:]
        + coeffs[2] * from_west
        + coeffs[3] * from_east
    )


def adjoint_step(state, coeffs):
    carried = jnp.stack([coeffs[0] * state, coeffs[1] * state])
    padded = padded_2(carried, (("region", 2),), 1)
    west_part = coeffs[2] * state
    east_part = coeffs[3] * state
    from_east = jnp.pad(west_part[..., 1:], ((0, 0), (0, 0), (0, 1)))
    from_west = jnp.pad(east_part[..., :-1], ((0, 0), (0, 0), (1, 0)))
    center = 1.0 - jnp.sum(coeffs, 0)
    return center * state + padded[0, :, 2:] + padded[1, :, :-2] + from_east + from_west


def shards(controls, perturbations, assignment, courant, innovation, obs_weight):
    row_count = controls.shape[2]
    row_start = lax.axis_index("region") * row_count
    total_rows = row_count * lax.axis_size("region")
    halo_depth = 4
    highest = lax.Precision.HIGHEST
    smoothed = spread(controls, halo_depth, row_start, total_rows)
    one_hot = (assignment[:, None] == lax.iota(jnp.int32, FIELDS)[None, :]).astype(jnp.float32)
    local_members = perturbations.shape[0]
    own_hot = lax.dynamic_slice_in_dim(
        one_hot, lax.axis_index("member") * local_members, local_members, 0
    )
    all_fields = lax.all_gather(smoothed, "member", axis=0, tiled=True)
    own_sums = jnp.einsum("kl,kzxy->lzxy", own_hot, perturbations, precision=highest)
    increment = lax.psum_scatter(
        jnp.sum(all_fields * own_sums, 0), "member", scatter_dimension=0, tiled=True
    )
    state = increment
    for step in range(STEPS):
        state = tangent_step(state, courant[step])
    departure = obs_weight * (state - innovation)
    adjoint = departure
    for step in range(STEPS - 1, -1, -1):
        adjoint = adjoint_step(adjoint, courant[step])
    full_adjoint = lax.all_gather(adjoint, "member", axis=0, tiled=True)
    weighted = perturbations * full_adjoint[None]
    field_terms = lax.psum_scatter(
        jnp.einsum("kl,kzxy->lzxy", own_hot, weighted, precision=highest),
        "member",
        scatter_dimension=0,
        tiled=True,
    )
    gradient = controls + spread(field_terms, halo_depth, row_start, total_rows)
    return (gradient, departure)


def solution(mesh):
    return jax.shard_map(
        shards,
        mesh=mesh,
        in_specs=(
            P("member", None, "region", None),
            P("member", None, "region", None),
            P(),
            P(None, None, "member", "region", None),
            P("member", "region", None),
            P("member", "region", None),
        ),
        out_specs=(P("member", None, "region", None), P("member", "region", None)),
        check_vma=False,
    )
```

profile of v0, /device:TPU:19, one launch (start us, length us, event | category | flops | bytes accessed | tf_op | source)
XLA Modules:
  0.0 439.7 jit_solution(9767177885848576362)
XLA Ops:
  8.6 3.7 collective-permute-start
  15.6 5.3 %collective-permute-done.1 = f32[4,8,4,512]{3,2,1,0:T(4,128)S(1)} collective-permute-done((f32[4,8,4,512]{3,2,1,0:T(4,128)S(1)}, f32[4,8,4,512]{3,2,1,0:T(4,128)S(1)}, u32[]{:S(2)}, u32[]{:S(2)}) %collective-permute-start.1) | collective-permute-done | bytes 262176 | tf_op jit(solution)/shard_map/ppermute | solution.py:19
  29.8 2.7 collective-permute-start.3
  33.1 5.3 %collective-permute-done.3 = f32[4,8,4,512]{3,2,1,0:T(4,128)S(1)} collective-permute-done((f32[4,8,4,512]{3,2,1,0:T(4,128)S(1)}, f32[4,8,4,512]{3,2,1,0:T(4,128)S(1)}, u32[]{:S(2)}, u32[]{:S(2)}) %collective-permute-start.3) | collective-permute-done | bytes 262176 | tf_op jit(solution)/shard_map/ppermute | solution.py:19
  47.3 3.0 collective-permute-start.5
  50.6 5.3 %collective-permute-done.5 = f32[4,8,4,512]{3,2,1,0:T(4,128)S(1)} collective-permute-done((f32[4,8,4,512]{3,2,1,0:T(4,128)S(1)}, f32[4,8,4,512]{3,2,1,0:T(4,128)S(1)}, u32[]{:S(2)}, u32[]{:S(2)}) %collective-permute-start.5) | collective-permute-done | bytes 262176 | tf_op jit(solution)/shard_map/ppermute | solution.py:19
  64.8 2.6 collective-permute-start.7
  68.1 5.3 %collective-permute-done.7 = f32[4,8,4,512]{3,2,1,0:T(4,128)S(1)} collective-permute-done((f32[4,8,4,512]{3,2,1,0:T(4,128)S(1)}, f32[4,8,4,512]{3,2,1,0:T(4,128)S(1)}, u32[]{:S(2)}, u32[]{:S(2)}) %collective-permute-start.7) | collective-permute-done | bytes 262176 | tf_op jit(solution)/shard_map/ppermute | solution.py:19
  81.8 78.4 %all-gather.2.cloned.1.call-done = f32[16,8,16,512]{3,2,1,0:T(8,128)} async-done(((f32[4,8,16,512]{3,2,1,0:T(8,128)}), f32[16,8,16,512]{3,2,1,0:T(8,128)}) %all-gather.2.cloned.1.call-update) | async-done | bytes 4194320 | tf_op jit(solution)/shard_map/all_gather | solution.py:81
  160.3 10.9 %fusion.2 = f32[8,16,512]{2,1,0:T(8,128)} fusion(f32[16,8,16,512]{3,2,1,0:T(8,128)} %all-gather.2.cloned.1.call-done, f32[16,8,16,512]{3,2,1,0:T(8,128)} %param.7, s32[16]{0:T(128)S(1)} %dynamic-slice), kind=kOutput, calls=%fused_computation.3 | convolution fusion | flops 203358464 | bytes 8650816 | tf_op jit(solution)/shard_map/kl,kzxy->lzxy/dot_general | solution.py:82
  171.4 15.9 %reduce-scatter.3.cloned.1.call-done = f32[2,16,512]{2,1,0:T(8,128)} async-done(((f32[8,16,512]{2,1,0:T(8,128)}), f32[2,16,512]{2,1,0:T(8,128)}) %reduce-scatter.3.cloned.1.call-update) | async-done | bytes 65552 | tf_op jit(solution)/shard_map/reduce_scatter | solution.py:83
  188.1 6.1 %collective-permute-start.8 = (f32[2,1,512]{2,1,0:T(1,128)S(1)}, f32[2,1,512]{2,1,0:T(1,128)S(1)}, u32[]{:S(2)}, u32[]{:S(2)}) collective-permute-start(f32[2,1,512]{2,1,0:T(1,128)S(1)} %get-tuple-element.134), channel_id=1, source_target_pairs={{0,4},{4,8},{8,12},{12,16},{16,20},{20,24},{24,28},{1,5},{5,9},{9,... | collective-permute-start | bytes 12296 | tf_op jit(solution)/shard_map/ppermute | solution.py:16
  197.1 2.9 collective-permute-done.9
  205.5 3.4 collective-permute-done.11
  213.3 3.4 collective-permute-done.13
  221.2 3.4 collective-permute-done.15
  226.7 4.5 %collective-permute-start.17 = (f32[2,2,1,512]{3,2,1,0:T(1,128)S(1)}, f32[2,2,1,512]{3,2,1,0:T(1,128)S(1)}, u32[]{:S(2)}, u32[]{:S(2)}) collective-permute-start(f32[2,2,1,512]{3,2,1,0:T(1,128)S(1)} %get-tuple-element.111), channel_id=1, source_target_pairs={{0,4},{4,8},{8,12},{12,16},{16,20},{20,24},{24,28},{1,5},{5,9},{9,... | collective-permute-start | bytes 24584 | tf_op jit(solution)/shard_map/ppermute | solution.py:16
  234.3 5.1 %collective-permute-start.19 = (f32[2,2,1,512]{3,2,1,0:T(1,128)S(1)}, f32[2,2,1,512]{3,2,1,0:T(1,128)S(1)}, u32[]{:S(2)}, u32[]{:S(2)}) collective-permute-start(f32[2,2,1,512]{3,2,1,0:T(1,128)S(1)} %get-tuple-element.109), channel_id=1, source_target_pairs={{0,4},{4,8},{8,12},{12,16},{16,20},{20,24},{24,28},{1,5},{5,9},{9,... | collective-permute-start | bytes 24584 | tf_op jit(solution)/shard_map/ppermute | solution.py:16
  242.3 5.1 %collective-permute-start.21 = (f32[2,2,1,512]{3,2,1,0:T(1,128)S(1)}, f32[2,2,1,512]{3,2,1,0:T(1,128)S(1)}, u32[]{:S(2)}, u32[]{:S(2)}) collective-permute-start(f32[2,2,1,512]{3,2,1,0:T(1,128)S(1)} %get-tuple-element.107), channel_id=1, source_target_pairs={{0,4},{4,8},{8,12},{12,16},{16,20},{20,24},{24,28},{1,5},{5,9},{9,... | collective-permute-start | bytes 24584 | tf_op jit(solution)/shard_map/ppermute | solution.py:16
  250.2 5.1 %collective-permute-start.23 = (f32[2,2,1,512]{3,2,1,0:T(1,128)S(1)}, f32[2,2,1,512]{3,2,1,0:T(1,128)S(1)}, u32[]{:S(2)}, u32[]{:S(2)}) collective-permute-start(f32[2,2,1,512]{3,2,1,0:T(1,128)S(1)} %get-tuple-element.105), channel_id=1, source_target_pairs={{0,4},{4,8},{8,12},{12,16},{16,20},{20,24},{24,28},{1,5},{5,9},{9,... | collective-permute-start | bytes 24584 | tf_op jit(solution)/shard_map/ppermute | solution.py:16
  256.2 12.3 %all_gather.7 = f32[8,16,512]{2,1,0:T(8,128)S(1)} all-gather(f32[2,16,512]{2,1,0:T(8,128)S(1)} %fusion.231), channel_id=1, replica_groups=mesh['region'=8,'member'=4] {'member'}, dimensions={0}, use_global_device_ids=true | all-gather | bytes 327680 | tf_op jit(solution)/shard_map/all_gather | solution.py:93
  269.4 4.4 %fusion = f32[16,8,16,512]{3,0,2,1:T(8,128)S(1)} fusion(f32[16,8,16,512]{3,2,1,0:T(8,128)S(1)} %broadcast_multiply_fusion, s32[16]{0:T(128)S(1)} %dynamic-slice), kind=kOutput, calls=%fused_computation | convolution fusion | flops 201326848 | bytes 8388672 | tf_op jit(solution)/shard_map/kl,kzxy->lzxy/dot_general | solution.py:96
  273.9 4.5 %copy.18 = f32[16,8,16,512]{3,2,1,0:T(8,128)} copy(f32[16,8,16,512]{3,0,2,1:T(8,128)S(1)} %fusion) | data formatting | bytes 8388608 | tf_op jit(solution)/shard_map/kl,kzxy->lzxy/dot_general | solution.py:96
  278.3 80.1 %reduce-scatter.5.cloned.1.call-done = f32[4,8,16,512]{3,2,1,0:T(8,128)} async-done(((f32[16,8,16,512]{3,2,1,0:T(8,128)}), f32[4,8,16,512]{3,2,1,0:T(8,128)}) %reduce-scatter.5.cloned.1.call-update) | async-done | bytes 1048592 | tf_op jit(solution)/shard_map/reduce_scatter | solution.py:95
  359.9 3.7 collective-permute-start.24
  366.9 5.3 %collective-permute-done.25 = f32[4,8,4,512]{3,2,1,0:T(4,128)S(1)} collective-permute-done((f32[4,8,4,512]{3,2,1,0:T(4,128)S(1)}, f32[4,8,4,512]{3,2,1,0:T(4,128)S(1)}, u32[]{:S(2)}, u32[]{:S(2)}) %collective-permute-start.25) | collective-permute-done | bytes 262176 | tf_op jit(solution)/shard_map/ppermute | solution.py:19
  381.1 2.6 collective-permute-start.27
  384.4 5.3 %collective-permute-done.27 = f32[4,8,4,512]{3,2,1,0:T(4,128)S(1)} collective-permute-done((f32[4,8,4,512]{3,2,1,0:T(4,128)S(1)}, f32[4,8,4,512]{3,2,1,0:T(4,128)S(1)}, u32[]{:S(2)}, u32[]{:S(2)}) %collective-permute-start.27) | collective-permute-done | bytes 262176 | tf_op jit(solution)/shard_map/ppermute | solution.py:19
  398.6 2.6 collective-permute-start.29
  401.9 5.3 %collective-permute-done.29 = f32[4,8,4,512]{3,2,1,0:T(4,128)S(1)} collective-permute-done((f32[4,8,4,512]{3,2,1,0:T(4,128)S(1)}, f32[4,8,4,512]{3,2,1,0:T(4,128)S(1)}, u32[]{:S(2)}, u32[]{:S(2)}) %collective-permute-start.29) | collective-permute-done | bytes 262176 | tf_op jit(solution)/shard_map/ppermute | solution.py:19
  416.1 2.7 collective-permute-start.31
  419.4 5.3 %collective-permute-done.31 = f32[4,8,4,512]{3,2,1,0:T(4,128)S(1)} collective-permute-done((f32[4,8,4,512]{3,2,1,0:T(4,128)S(1)}, f32[4,8,4,512]{3,2,1,0:T(4,128)S(1)}, u32[]{:S(2)}, u32[]{:S(2)}) %collective-permute-start.31) | collective-permute-done | bytes 262176 | tf_op jit(solution)/shard_map/ppermute | solution.py:19
  (183 shorter events, 113.3 us)
Async XLA Ops:
  7.2 153.1 %all-gather.2.cloned.1.call-start = ((), (), s32[]{:S(2)}) async-start(), calls=%async_computation.2 | async-start | bytes 5242880 | tf_op jit(solution)/shard_map/all_gather | solution.py:81
  8.6 7.0 %collective-permute-start = (f32[4,8,4,512]{3,2,1,0:T(4,128)S(1)}, f32[4,8,4,512]{3,2,1,0:T(4,128)S(1)}, u32[]{:S(2)}, u32[]{:S(2)}) collective-permute-start(f32[4,8,4,512]{3,2,1,0:T(4,128)S(1)} %get-tuple-element.102), channel_id=1, source_target_pairs={{0,4},{4,8},{8,12},{12,16},{16,20},{20,24},{24,28},{1,5},{5,9},{9,... | collective-permute-start | bytes 786440 | tf_op jit(solution)/shard_map/ppermute | solution.py:16
  12.3 8.6 %collective-permute-start.1 = (f32[4,8,4,512]{3,2,1,0:T(4,128)S(1)}, f32[4,8,4,512]{3,2,1,0:T(4,128)S(1)}, u32[]{:S(2)}, u32[]{:S(2)}) collective-permute-start(f32[4,8,4,512]{3,2,1,0:T(4,128)S(1)} %get-tuple-element.103), channel_id=1, source_target_pairs={{4,0},{8,4},{12,8},{16,12},{20,16},{24,20},{28,24},{5,1},{9,5},{13... | collective-permute-start | bytes 786440 | tf_op jit(solution)/shard_map/ppermute | solution.py:19
  27.8 5.2 %collective-permute-start.2 = (f32[4,8,4,512]{3,2,1,0:T(4,128)S(1)}, f32[4,8,4,512]{3,2,1,0:T(4,128)S(1)}, u32[]{:S(2)}, u32[]{:S(2)}) collective-permute-start(f32[4,8,4,512]{3,2,1,0:T(4,128)S(1)} %get-tuple-element.82), channel_id=1, source_target_pairs={{0,4},{4,8},{8,12},{12,16},{16,20},{20,24},{24,28},{1,5},{5,9},{9,... | collective-permute-start | bytes 786440 | tf_op jit(solution)/shard_map/ppermute | solution.py:16
  29.8 8.6 %collective-permute-start.3 = (f32[4,8,4,512]{3,2,1,0:T(4,128)S(1)}, f32[4,8,4,512]{3,2,1,0:T(4,128)S(1)}, u32[]{:S(2)}, u32[]{:S(2)}) collective-permute-start(f32[4,8,4,512]{3,2,1,0:T(4,128)S(1)} %get-tuple-element.83), channel_id=1, source_target_pairs={{4,0},{8,4},{12,8},{16,12},{20,16},{24,20},{28,24},{5,1},{9,5},{13... | collective-permute-start | bytes 786440 | tf_op jit(solution)/shard_map/ppermute | solution.py:19
  45.3 5.2 %collective-permute-start.4 = (f32[4,8,4,512]{3,2,1,0:T(4,128)S(1)}, f32[4,8,4,512]{3,2,1,0:T(4,128)S(1)}, u32[]{:S(2)}, u32[]{:S(2)}) collective-permute-start(f32[4,8,4,512]{3,2,1,0:T(4,128)S(1)} %get-tuple-element.72), channel_id=1, source_target_pairs={{0,4},{4,8},{8,12},{12,16},{16,20},{20,24},{24,28},{1,5},{5,9},{9,... | collective-permute-start | bytes 786440 | tf_op jit(solution)/shard_map/ppermute | solution.py:16
  47.3 8.6 %collective-permute-start.5 = (f32[4,8,4,512]{3,2,1,0:T(4,128)S(1)}, f32[4,8,4,512]{3,2,1,0:T(4,128)S(1)}, u32[]{:S(2)}, u32[]{:S(2)}) collective-permute-start(f32[4,8,4,512]{3,2,1,0:T(4,128)S(1)} %get-tuple-element.73), channel_id=1, source_target_pairs={{4,0},{8,4},{12,8},{16,12},{20,16},{24,20},{28,24},{5,1},{9,5},{13... | collective-permute-start | bytes 786440 | tf_op jit(solution)/shard_map/ppermute | solution.py:19
  62.9 5.2 %collective-permute-start.6 = (f32[4,8,4,512]{3,2,1,0:T(4,128)S(1)}, f32[4,8,4,512]{3,2,1,0:T(4,128)S(1)}, u32[]{:S(2)}, u32[]{:S(2)}) collective-permute-start(f32[4,8,4,512]{3,2,1,0:T(4,128)S(1)} %get-tuple-element.62), channel_id=1, source_target_pairs={{0,4},{4,8},{8,12},{12,16},{16,20},{20,24},{24,28},{1,5},{5,9},{9,... | collective-permute-start | bytes 786440 | tf_op jit(solution)/shard_map/ppermute | solution.py:16
  64.8 8.6 %collective-permute-start.7 = (f32[4,8,4,512]{3,2,1,0:T(4,128)S(1)}, f32[4,8,4,512]{3,2,1,0:T(4,128)S(1)}, u32[]{:S(2)}, u32[]{:S(2)}) collective-permute-start(f32[4,8,4,512]{3,2,1,0:T(4,128)S(1)} %get-tuple-element.63), channel_id=1, source_target_pairs={{4,0},{8,4},{12,8},{16,12},{20,16},{24,20},{28,24},{5,1},{9,5},{13... | collective-permute-start | bytes 786440 | tf_op jit(solution)/shard_map/ppermute | solution.py:19
  81.5 105.8 %reduce-scatter.3.cloned.1.call-start = ((), (), s32[]{:S(2)}) async-start(), calls=%async_computation.3 | async-start | bytes 327680 | tf_op jit(solution)/shard_map/reduce_scatter | solution.py:83
  171.2 187.3 %reduce-scatter.5.cloned.1.call-start = ((), (), s32[]{:S(2)}) async-start(), calls=%async_computation.4 | async-start | bytes 5242880 | tf_op jit(solution)/shard_map/reduce_scatter | solution.py:95
  188.1 9.0 %collective-permute-start.8 = (f32[2,1,512]{2,1,0:T(1,128)S(1)}, f32[2,1,512]{2,1,0:T(1,128)S(1)}, u32[]{:S(2)}, u32[]{:S(2)}) collective-permute-start(f32[2,1,512]{2,1,0:T(1,128)S(1)} %get-tuple-element.134), channel_id=1, source_target_pairs={{0,4},{4,8},{8,12},{12,16},{16,20},{20,24},{24,28},{1,5},{5,9},{9,... | collective-permute-start | bytes 12296 | tf_op jit(solution)/shard_map/ppermute | solution.py:16
  194.1 5.8 %collective-permute-start.9 = (f32[2,1,512]{2,1,0:T(1,128)S(1)}, f32[2,1,512]{2,1,0:T(1,128)S(1)}, u32[]{:S(2)}, u32[]{:S(2)}) collective-permute-start(f32[2,1,512]{2,1,0:T(1,128)S(1)} %get-tuple-element.135), channel_id=1, source_target_pairs={{4,0},{8,4},{12,8},{16,12},{20,16},{24,20},{28,24},{5,1},{9,5},{13... | collective-permute-start | bytes 12296 | tf_op jit(solution)/shard_map/ppermute | solution.py:19
  203.0 5.8 %collective-permute-start.11 = (f32[2,1,512]{2,1,0:T(1,128)S(1)}, f32[2,1,512]{2,1,0:T(1,128)S(1)}, u32[]{:S(2)}, u32[]{:S(2)}) collective-permute-start(f32[2,1,512]{2,1,0:T(1,128)S(1)} %get-tuple-element.131), channel_id=1, source_target_pairs={{4,0},{8,4},{12,8},{16,12},{20,16},{24,20},{28,24},{5,1},{9,5},{13... | collective-permute-start | bytes 12296 | tf_op jit(solution)/shard_map/ppermute | solution.py:19
  210.9 5.8 %collective-permute-start.13 = (f32[2,1,512]{2,1,0:T(1,128)S(1)}, f32[2,1,512]{2,1,0:T(1,128)S(1)}, u32[]{:S(2)}, u32[]{:S(2)}) collective-permute-start(f32[2,1,512]{2,1,0:T(1,128)S(1)} %get-tuple-element.127), channel_id=1, source_target_pairs={{4,0},{8,4},{12,8},{16,12},{20,16},{24,20},{28,24},{5,1},{9,5},{13... | collective-permute-start | bytes 12296 | tf_op jit(solution)/shard_map/ppermute | solution.py:19
  218.8 5.8 %collective-permute-start.15 = (f32[2,1,512]{2,1,0:T(1,128)S(1)}, f32[2,1,512]{2,1,0:T(1,128)S(1)}, u32[]{:S(2)}, u32[]{:S(2)}) collective-permute-start(f32[2,1,512]{2,1,0:T(1,128)S(1)} %get-tuple-element.121), channel_id=1, source_target_pairs={{4,0},{8,4},{12,8},{16,12},{20,16},{24,20},{28,24},{5,1},{9,5},{13... | collective-permute-start | bytes 12296 | tf_op jit(solution)/shard_map/ppermute | solution.py:19
  224.8 6.6 %collective-permute-start.16 = (f32[2,2,1,512]{3,2,1,0:T(1,128)S(1)}, f32[2,2,1,512]{3,2,1,0:T(1,128)S(1)}, u32[]{:S(2)}, u32[]{:S(2)}) collective-permute-start(f32[2,2,1,512]{3,2,1,0:T(1,128)S(1)} %get-tuple-element.110), channel_id=1, source_target_pairs={{4,0},{8,4},{12,8},{16,12},{20,16},{24,20},{28,24},{5,1},{9,5},{13... | collective-permute-start | bytes 24584 | tf_op jit(solution)/shard_map/ppermute | solution.py:19
  226.7 5.3 %collective-permute-start.17 = (f32[2,2,1,512]{3,2,1,0:T(1,128)S(1)}, f32[2,2,1,512]{3,2,1,0:T(1,128)S(1)}, u32[]{:S(2)}, u32[]{:S(2)}) collective-permute-start(f32[2,2,1,512]{3,2,1,0:T(1,128)S(1)} %get-tuple-element.111), channel_id=1, source_target_pairs={{0,4},{4,8},{8,12},{12,16},{16,20},{20,24},{24,28},{1,5},{5,9},{9,... | collective-permute-start | bytes 24584 | tf_op jit(solution)/shard_map/ppermute | solution.py:16
  232.1 7.4 %collective-permute-start.18 = (f32[2,2,1,512]{3,2,1,0:T(1,128)S(1)}, f32[2,2,1,512]{3,2,1,0:T(1,128)S(1)}, u32[]{:S(2)}, u32[]{:S(2)}) collective-permute-start(f32[2,2,1,512]{3,2,1,0:T(1,128)S(1)} %get-tuple-element.108), channel_id=1, source_target_pairs={{4,0},{8,4},{12,8},{16,12},{20,16},{24,20},{28,24},{5,1},{9,5},{13... | collective-permute-start | bytes 24584 | tf_op jit(solution)/shard_map/ppermute | solution.py:19
  234.3 5.9 %collective-permute-start.19 = (f32[2,2,1,512]{3,2,1,0:T(1,128)S(1)}, f32[2,2,1,512]{3,2,1,0:T(1,128)S(1)}, u32[]{:S(2)}, u32[]{:S(2)}) collective-permute-start(f32[2,2,1,512]{3,2,1,0:T(1,128)S(1)} %get-tuple-element.109), channel_id=1, source_target_pairs={{0,4},{4,8},{8,12},{12,16},{16,20},{20,24},{24,28},{1,5},{5,9},{9,... | collective-permute-start | bytes 24584 | tf_op jit(solution)/shard_map/ppermute | solution.py:16
  240.3 7.1 %collective-permute-start.20 = (f32[2,2,1,512]{3,2,1,0:T(1,128)S(1)}, f32[2,2,1,512]{3,2,1,0:T(1,128)S(1)}, u32[]{:S(2)}, u32[]{:S(2)}) collective-permute-start(f32[2,2,1,512]{3,2,1,0:T(1,128)S(1)} %get-tuple-element.106), channel_id=1, source_target_pairs={{4,0},{8,4},{12,8},{16,12},{20,16},{24,20},{28,24},{5,1},{9,5},{13... | collective-permute-start | bytes 24584 | tf_op jit(solution)/shard_map/ppermute | solution.py:19
  242.3 5.9 %collective-permute-start.21 = (f32[2,2,1,512]{3,2,1,0:T(1,128)S(1)}, f32[2,2,1,512]{3,2,1,0:T(1,128)S(1)}, u32[]{:S(2)}, u32[]{:S(2)}) collective-permute-start(f32[2,2,1,512]{3,2,1,0:T(1,128)S(1)} %get-tuple-element.107), channel_id=1, source_target_pairs={{0,4},{4,8},{8,12},{12,16},{16,20},{20,24},{24,28},{1,5},{5,9},{9,... | collective-permute-start | bytes 24584 | tf_op jit(solution)/shard_map/ppermute | solution.py:16
  248.3 7.1 %collective-permute-start.22 = (f32[2,2,1,512]{3,2,1,0:T(1,128)S(1)}, f32[2,2,1,512]{3,2,1,0:T(1,128)S(1)}, u32[]{:S(2)}, u32[]{:S(2)}) collective-permute-start(f32[2,2,1,512]{3,2,1,0:T(1,128)S(1)} %get-tuple-element.104), channel_id=1, source_target_pairs={{4,0},{8,4},{12,8},{16,12},{20,16},{24,20},{28,24},{5,1},{9,5},{13... | collective-permute-start | bytes 24584 | tf_op jit(solution)/shard_map/ppermute | solution.py:19
  250.2 5.9 %collective-permute-start.23 = (f32[2,2,1,512]{3,2,1,0:T(1,128)S(1)}, f32[2,2,1,512]{3,2,1,0:T(1,128)S(1)}, u32[]{:S(2)}, u32[]{:S(2)}) collective-permute-start(f32[2,2,1,512]{3,2,1,0:T(1,128)S(1)} %get-tuple-element.105), channel_id=1, source_target_pairs={{0,4},{4,8},{8,12},{12,16},{16,20},{20,24},{24,28},{1,5},{5,9},{9,... | collective-permute-start | bytes 24584 | tf_op jit(solution)/shard_map/ppermute | solution.py:16
  359.9 7.0 %collective-permute-start.24 = (f32[4,8,4,512]{3,2,1,0:T(4,128)S(1)}, f32[4,8,4,512]{3,2,1,0:T(4,128)S(1)}, u32[]{:S(2)}, u32[]{:S(2)}) collective-permute-start(f32[4,8,4,512]{3,2,1,0:T(4,128)S(1)} %get-tuple-element.92), channel_id=1, source_target_pairs={{0,4},{4,8},{8,12},{12,16},{16,20},{20,24},{24,28},{1,5},{5,9},{9,... | collective-permute-start | bytes 786440 | tf_op jit(solution)/shard_map/ppermute | solution.py:16
  363.6 8.6 %collective-permute-start.25 = (f32[4,8,4,512]{3,2,1,0:T(4,128)S(1)}, f32[4,8,4,512]{3,2,1,0:T(4,128)S(1)}, u32[]{:S(2)}, u32[]{:S(2)}) collective-permute-start(f32[4,8,4,512]{3,2,1,0:T(4,128)S(1)} %get-tuple-element.93), channel_id=1, source_target_pairs={{4,0},{8,4},{12,8},{16,12},{20,16},{24,20},{28,24},{5,1},{9,5},{13... | collective-permute-start | bytes 786440 | tf_op jit(solution)/shard_map/ppermute | solution.py:19
  379.2 5.2 %collective-permute-start.26 = (f32[4,8,4,512]{3,2,1,0:T(4,128)S(1)}, f32[4,8,4,512]{3,2,1,0:T(4,128)S(1)}, u32[]{:S(2)}, u32[]{:S(2)}) collective-permute-start(f32[4,8,4,512]{3,2,1,0:T(4,128)S(1)} %get-tuple-element.44), channel_id=1, source_target_pairs={{0,4},{4,8},{8,12},{12,16},{16,20},{20,24},{24,28},{1,5},{5,9},{9,... | collective-permute-start | bytes 786440 | tf_op jit(solution)/shard_map/ppermute | solution.py:16
  381.1 8.6 %collective-permute-start.27 = (f32[4,8,4,512]{3,2,1,0:T(4,128)S(1)}, f32[4,8,4,512]{3,2,1,0:T(4,128)S(1)}, u32[]{:S(2)}, u32[]{:S(2)}) collective-permute-start(f32[4,8,4,512]{3,2,1,0:T(4,128)S(1)} %get-tuple-element.45), channel_id=1, source_target_pairs={{4,0},{8,4},{12,8},{16,12},{20,16},{24,20},{28,24},{5,1},{9,5},{13... | collective-permute-start | bytes 786440 | tf_op jit(solution)/shard_map/ppermute | solution.py:19
  396.7 5.2 %collective-permute-start.28 = (f32[4,8,4,512]{3,2,1,0:T(4,128)S(1)}, f32[4,8,4,512]{3,2,1,0:T(4,128)S(1)}, u32[]{:S(2)}, u32[]{:S(2)}) collective-permute-start(f32[4,8,4,512]{3,2,1,0:T(4,128)S(1)} %get-tuple-element.34), channel_id=1, source_target_pairs={{0,4},{4,8},{8,12},{12,16},{16,20},{20,24},{24,28},{1,5},{5,9},{9,... | collective-permute-start | bytes 786440 | tf_op jit(solution)/shard_map/ppermute | solution.py:16
  398.6 8.6 %collective-permute-start.29 = (f32[4,8,4,512]{3,2,1,0:T(4,128)S(1)}, f32[4,8,4,512]{3,2,1,0:T(4,128)S(1)}, u32[]{:S(2)}, u32[]{:S(2)}) collective-permute-start(f32[4,8,4,512]{3,2,1,0:T(4,128)S(1)} %get-tuple-element.35), channel_id=1, source_target_pairs={{4,0},{8,4},{12,8},{16,12},{20,16},{24,20},{28,24},{5,1},{9,5},{13... | collective-permute-start | bytes 786440 | tf_op jit(solution)/shard_map/ppermute | solution.py:19
  414.2 5.2 %collective-permute-start.30 = (f32[4,8,4,512]{3,2,1,0:T(4,128)S(1)}, f32[4,8,4,512]{3,2,1,0:T(4,128)S(1)}, u32[]{:S(2)}, u32[]{:S(2)}) collective-permute-start(f32[4,8,4,512]{3,2,1,0:T(4,128)S(1)} %get-tuple-element.24), channel_id=1, source_target_pairs={{0,4},{4,8},{8,12},{12,16},{16,20},{20,24},{24,28},{1,5},{5,9},{9,... | collective-permute-start | bytes 786440 | tf_op jit(solution)/shard_map/ppermute | solution.py:16
  416.1 8.6 %collective-permute-start.31 = (f32[4,8,4,512]{3,2,1,0:T(4,128)S(1)}, f32[4,8,4,512]{3,2,1,0:T(4,128)S(1)}, u32[]{:S(2)}, u32[]{:S(2)}) collective-permute-start(f32[4,8,4,512]{3,2,1,0:T(4,128)S(1)} %get-tuple-element.25), channel_id=1, source_target_pairs={{4,0},{8,4},{12,8},{16,12},{20,16},{24,20},{28,24},{5,1},{9,5},{13... | collective-permute-start | bytes 786440 | tf_op jit(solution)/shard_map/ppermute | solution.py:19
  (11 other events, 297.9 us)
Sparse Core Ops, SparseCore 0:
  81.6 78.6 all-gather.1
  171.3 15.9 reduce-scatter.2
  278.5 79.9 reduce-scatter.4
where the time goes:
time: 446 us; the launch traced here: 440 us
  waiting for transfers between devices  237 us (53%)
  starting transfers between devices  88.4 us (20%)
  other arithmetic  41.8 us (9%)
  local copies, waits for them, and re-layouts  29.7 us (7%)
  matrix products  15.3 us (3%)
  between operations  15.1 us (3%)
  blocking collectives  12.3 us (3%)
    reduce_scatter x1, waiting for transfers between devices, shards(): lax.psum_scatter(jnp.einsum('kl,kzxy->lzxy', own_hot, weighted, precision...  80.1 us
    all_gather x1, waiting for transfers between devices, shards(): all_fields = lax.all_gather(smoothed, 'member', axis=0, tiled=True)  78.4 us
    ppermute x16, waiting for transfers between devices, padded_2(): lax.ppermute(lax.slice_in_dim(block, 0, width, axis=dim), axis, backward)  55.3 us
    ppermute x16, starting transfers between devices, padded_2(): lax.ppermute(lax.slice_in_dim(block, block.shape[dim] - width, None, axis...  50.6 us
    ppermute x16, starting transfers between devices, padded_2(): lax.ppermute(lax.slice_in_dim(block, 0, width, axis=dim), axis, backward)  37.5 us
    mul x31, other arithmetic, spread(): extended = relax_once(extended) * inside  33.7 us
    slice x32, local copies, waits for them, and re-layouts, relax_once(): from_west = jnp.pad(extended[..., :-1], ((0, 0), (0, 0), (0, 0), (1, 0)))  18.4 us
    reduce_scatter x1, waiting for transfers between devices, shards(): lax.psum_scatter(jnp.sum(all_fields * own_sums, 0), 'member', scatter_dim...  15.9 us
  transfers between devices with their start and end apart: 35, of which 27 were waited for; matrix products, arithmetic and copies ran while one was open for 1% of the time, Pallas kernels for 0%

commit v1 on v0

v1 whole, which is shorter than its diff:
```python
import functools

import jax
import jax.numpy as jnp
import numpy as np
from jax import lax
from jax.experimental import pallas as pl
from jax.experimental.pallas import tpu as pltpu
from jax.sharding import PartitionSpec as P

FIELDS = 16
PASSES = 16
STEPS = 4
RATE = 0.2
STACK = 4
F32 = jnp.float32
BF16 = jnp.bfloat16


def sine_basis(n):
    k = np.arange(1, n + 1, dtype=np.float64)
    return np.sqrt(2.0 / (n + 1)) * np.sin(np.pi * np.outer(k, k) / (n + 1))


def halves(matrix):
    high = np.asarray(matrix, np.float32).astype(jnp.bfloat16)
    low = (np.asarray(matrix, np.float64) - high.astype(np.float64)).astype(jnp.bfloat16)
    return np.stack([high, low])


@functools.lru_cache(None)
def diffusion_tables(rows, cols):
    depth = PASSES
    window = rows + 2 * depth
    col_basis = sine_basis(cols)
    row_basis = sine_basis(window)
    first = np.eye(window)
    first[:depth] = 0.0
    for i in range(depth - 1):
        first[i, depth + depth - 2 - i] = -1.0
    last = np.eye(window)
    last[depth + rows :] = 0.0
    for i in range(1, depth):
        last[depth + rows + i, depth + rows - i] = -1.0
    forward = [row_basis @ first, row_basis, row_basis @ last]
    stacked = np.eye(STACK)
    forward = np.stack([halves(np.kron(stacked, m)) for m in forward])
    backward = halves(np.kron(stacked, row_basis[depth : depth + rows]))
    row_values = 2.0 * np.cos(np.pi * np.arange(1, window + 1) / (window + 1))
    col_values = 2.0 * np.cos(np.pi * np.arange(1, cols + 1) / (cols + 1))
    scale = (RATE * (1.0 + row_values[:, None] + col_values[None, :])) ** PASSES
    return halves(col_basis), forward, backward, scale.astype(np.float32)


def split(x):
    high = x.astype(BF16)
    return high, (x - high.astype(F32)).astype(BF16)


def mul(a, b):
    dot = functools.partial(jnp.dot, preferred_element_type=F32)
    return dot(a[0], b[0]) + (dot(a[1], b[0]) + dot(a[0], b[1]))


def diffuse_block(ext, col_ref, fwd_ref, bwd_ref, scale_ref, rows):
    pairs, window, cols = ext.shape
    col = (col_ref[0], col_ref[1])
    fwd = (fwd_ref[0], fwd_ref[1])
    bwd = (bwd_ref[0], bwd_ref[1])
    spectral = mul(split(ext.reshape(pairs * window, cols)), col)
    group = STACK * window
    outs = []
    for g in range(pairs // STACK):
        part = mul(fwd, split(spectral[g * group : (g + 1) * group]))
        part = (part.reshape(STACK, window, cols) * scale_ref[...][None]).reshape(group, cols)
        outs.append(mul(bwd, split(part)))
    out = mul(split(jnp.concatenate(outs, 0)), col)
    return out.reshape(pairs, rows, cols)


def smooth_kernel(top_ref, own_ref, bot_ref, col_ref, fwd_ref, bwd_ref, scale_ref, out_ref):
    ext = jnp.concatenate([top_ref[0], own_ref[0], bot_ref[0]], axis=1)
    out_ref[0] = diffuse_block(ext, col_ref, fwd_ref, bwd_ref, scale_ref, own_ref.shape[2])


def gradient_kernel(
    slot_ref, ctl_ref, top_ref, own_ref, bot_ref, atop_ref, aown_ref, abot_ref,
    col_ref, fwd_ref, bwd_ref, scale_ref, out_ref,
):
    levels = own_ref.shape[1]
    parts = []
    for z in range(levels):
        s = slot_ref[z]
        parts.append(
            jnp.concatenate(
                [top_ref[0, z] * atop_ref[s], own_ref[0, z] * aown_ref[s], bot_ref[0, z] * abot_ref[s]],
                axis=0,
            )
        )
    ext = jnp.stack(parts)
    out_ref[0] = ctl_ref[0] + diffuse_block(ext, col_ref, fwd_ref, bwd_ref, scale_ref, own_ref.shape[2])


def table_specs(tables):
    def spec(t):
        return pl.BlockSpec(t.shape, functools.partial(lambda n, *_: (0,) * n, t.ndim))

    return [spec(t) for t in tables]


def smooth(top, own, bot, tables):
    fields, levels, rows, cols = own.shape
    block = lambda a: pl.BlockSpec((1,) + a.shape[1:], lambda f: (f, 0, 0, 0))
    return pl.pallas_call(
        smooth_kernel,
        grid=(fields,),
        in_specs=[block(top), block(own), block(bot)] + table_specs(tables),
        out_specs=block(own),
        out_shape=jax.ShapeDtypeStruct(own.shape, F32),
        cost_estimate=pl.CostEstimate(flops=5 * 10**9, bytes_accessed=4 * own.size * 4, transcendentals=0),
        name="smooth",
    )(top, own, bot, *tables)


def gradient_of(slots, controls, sums, adjoints, tables):
    fields, levels, rows, cols = controls.shape
    block = lambda a: pl.BlockSpec((1,) + a.shape[1:], lambda f, s: (f, 0, 0, 0))
    whole = lambda a: pl.BlockSpec(a.shape, lambda f, s: (0, 0, 0))
    return pl.pallas_call(
        gradient_kernel,
        grid_spec=pltpu.PrefetchScalarGridSpec(
            num_scalar_prefetch=1,
            grid=(fields,),
            in_specs=[block(controls)]
            + [block(a) for a in sums]
            + [whole(a) for a in adjoints]
            + table_specs(tables),
            out_specs=block(controls),
        ),
        out_shape=jax.ShapeDtypeStruct(controls.shape, F32),
        cost_estimate=pl.CostEstimate(flops=5 * 10**9, bytes_accessed=5 * controls.size * 4, transcendentals=0),
        name="gradient",
    )(slots, controls, *sums, *adjoints, *tables)


def member_sums_kernel(assign_ref, members_ref, out_ref):
    out_ref[...] = jnp.zeros_like(out_ref)
    for k in range(members_ref.shape[0]):
        field = assign_ref[k]
        out_ref[field] = out_ref[field] + members_ref[k]


def member_sums(assignment, perturbations):
    members, levels, rows, cols = perturbations.shape
    return pl.pallas_call(
        member_sums_kernel,
        grid_spec=pltpu.PrefetchScalarGridSpec(
            num_scalar_prefetch=1,
            grid=(levels,),
            in_specs=[pl.BlockSpec((members, 1, rows, cols), lambda z, s: (0, z, 0, 0))],
            out_specs=pl.BlockSpec((FIELDS, 1, rows, cols), lambda z, s: (0, z, 0, 0)),
        ),
        out_shape=jax.ShapeDtypeStruct((FIELDS, levels, rows, cols), F32),
        cost_estimate=pl.CostEstimate(flops=10**7, bytes_accessed=2 * perturbations.size * 4, transcendentals=0),
        name="member_sums",
    )(assignment, perturbations)


def shift_rows(x, by):
    blank = jnp.zeros_like(x[:, :1])
    if by > 0:
        return jnp.concatenate([blank, x[:, :-1]], axis=1)
    return jnp.concatenate([x[:, 1:], blank], axis=1)


def shift_cols(x, by):
    lane = lax.broadcasted_iota(jnp.int32, x.shape, 2)
    if by > 0:
        return jnp.where(lane == 0, 0.0, pltpu.roll(x, 1, 2))
    return jnp.where(lane == x.shape[2] - 1, 0.0, pltpu.roll(x, x.shape[2] - 1, 2))


def transport_kernel(
    inc_top, inc_own, inc_bot, con_top, con_own, con_bot, obs_own, inn_own, dep_ref, adj_ref
):
    halo = inc_top.shape[1]
    rows = inc_own.shape[1]
    join = lambda a, b, c: jnp.concatenate([a, b, c], axis=1)
    state = join(inc_top[...], inc_own[...], inc_bot[...])

    def coeffs(step):
        c = [
            join(con_top[4 * step + k], con_own[4 * step + k], con_bot[4 * step + k]) for k in range(4)
        ]
        return c, 1.0 - (c[0] + c[1] + c[2] + c[3])

    for step in range(STEPS):
        c, center = coeffs(step)
        state = (
            center * state
            + c[0] * shift_rows(state, 1)
            + c[1] * shift_rows(state, -1)
            + c[2] * shift_cols(state, 1)
            + c[3] * shift_cols(state, -1)
        )
    weight = join(con_top[4 * STEPS], obs_own[...], con_bot[4 * STEPS])
    target = join(con_top[4 * STEPS + 1], inn_own[...], con_bot[4 * STEPS + 1])
    state = weight * (state - target)
    dep_ref[...] = state[:, halo : halo + rows]
    for step in range(STEPS - 1, -1, -1):
        c, center = coeffs(step)
        state = (
            center * state
            + shift_rows(c[0] * state, -1)
            + shift_rows(c[1] * state, 1)
            + shift_cols(c[2] * state, -1)
            + shift_cols(c[3] * state, 1)
        )
    adj_ref[...] = state[:, halo : halo + rows]


def transport(inc, con, obs_weight, innovation):
    shape = jax.ShapeDtypeStruct(obs_weight.shape, F32)
    return pl.pallas_call(
        transport_kernel,
        out_shape=(shape, shape),
        cost_estimate=pl.CostEstimate(flops=10**8, bytes_accessed=3 * 2**20, transcendentals=0),
        name="transport",
    )(*inc, *con, obs_weight, innovation)


def beside(block, dim, depth, axis="region"):
    count = lax.axis_size(axis)
    forward = [(i, i + 1) for i in range(count - 1)]
    backward = [(b, a) for a, b in forward]
    extent = block.shape[dim]
    low = lax.ppermute(lax.slice_in_dim(block, extent - depth, extent, axis=dim), axis, forward)
    high = lax.ppermute(lax.slice_in_dim(block, 0, depth, axis=dim), axis, backward)
    return low, high


def shards(controls, perturbations, assignment, courant, innovation, obs_weight):
    fields, levels, rows, cols = controls.shape
    planes = lax.axis_size("member")
    plane = lax.axis_index("member")
    region = lax.axis_index("region")
    regions = lax.axis_size("region")
    own_levels = levels // planes
    halo = 2 * STEPS

    col_basis, forward, backward, scale = diffusion_tables(rows, cols)
    place = jnp.where(region == 0, 0, jnp.where(region == regions - 1, 2, 1))
    tables = (
        jnp.asarray(col_basis),
        lax.dynamic_index_in_dim(jnp.asarray(forward), place, 0, keepdims=False),
        jnp.asarray(backward),
        jnp.asarray(scale),
    )

    local_members = perturbations.shape[0]
    own_assignment = lax.dynamic_slice_in_dim(assignment, plane * local_members, local_members, 0)
    partial_sums = member_sums(own_assignment, perturbations)
    sums = lax.psum_scatter(partial_sums, "member", scatter_dimension=0, tiled=True)

    top, bot = beside(controls, 2, PASSES)
    flat = courant.reshape((4 * STEPS,) + courant.shape[2:])
    ends = lambda a: jnp.concatenate([a[:, :halo], a[:, rows - halo :]], axis=1)
    edge = jnp.concatenate(
        [
            jnp.concatenate([flat[:, :, :halo], flat[:, :, rows - halo :]], axis=2),
            ends(obs_weight)[None],
            ends(innovation)[None],
        ],
        axis=0,
    )
    con_top, con_bot = beside(edge, 2, halo)
    smoothed = smooth(top, controls, bot, tables)

    partial = jnp.sum(smoothed * sums, 0).reshape(planes, own_levels, rows, cols)
    pick = lambda k: lax.dynamic_index_in_dim(partial, lax.rem(plane + k, planes), 0, keepdims=False)
    turn = lambda k: [(i, (i + k) % planes) for i in range(planes)]
    increment = pick(0)
    for k in range(1, planes):
        increment = increment + lax.ppermute(pick(k), "member", turn(k))
    inc_top, inc_bot = beside(increment, 1, halo)
    sums_top, sums_bot = beside(sums, 2, PASSES)
    departure, adjoint = transport(
        (inc_top, increment, inc_bot), (con_top, flat, con_bot), obs_weight, innovation
    )
    full = jnp.concatenate(
        [adjoint] + [lax.ppermute(adjoint, "member", turn(k)) for k in range(1, planes)], axis=0
    )
    adj_top, adj_bot = beside(full, 1, PASSES)
    level = lax.iota(jnp.int32, levels)
    slots = lax.rem(plane - level // own_levels + planes, planes) * own_levels + lax.rem(level, own_levels)
    gradient = gradient_of(
        slots, controls, (sums_top, sums, sums_bot), (adj_top, full, adj_bot), tables
    )
    return (gradient, departure)


def solution(mesh):
    return jax.shard_map(
        shards,
        mesh=mesh,
        in_specs=(
            P("member", None, "region", None),
            P("member", None, "region", None),
            P(),
            P(None, None, "member", "region", None),
            P("member", "region", None),
            P("member", "region", None),
        ),
        out_specs=(P("member", None, "region", None), P("member", "region", None)),
        check_vma=False,
    )
```

time: 446 us -> 175 us (0.39)
  waiting for transfers between devices: 237 us -> 80.8 us
  starting transfers between devices: 88.4 us -> 35.8 us
  other arithmetic: 41.8 us -> 2.52 us
  Pallas kernels: 0 us -> 32.4 us
  local copies, waits for them, and re-layouts: 29.7 us -> 6.03 us
  matrix products: 15.3 us -> 0 us
  blocking collectives: 12.3 us -> 0 us
    all_gather x1 -> x0, waiting for transfers between devices: 78.4 us -> none  [shards(): all_fields = lax.all_gather(smoothed, 'member', axis=0, tiled=True)]
    reduce_scatter x2 -> x1, waiting for transfers between devices: 96.1 us -> 35.9 us  [shards(): lax.psum_scatter(partial_sums, 'member', scatter_dimension=0, tiled=True)]
    ppermute x32 -> x16, starting transfers between devices: 88.1 us -> 35.7 us  [the longest x5 21.7 us: beside(): lax.ppermute(lax.slice_in_dim(block, extent - depth, extent, axis=dim), a...]
    mul x36 -> x0, other arithmetic: 35 us -> none  [the longest x31 33.7 us: spread(): extended = relax_once(extended) * inside]
    pallas_call x0 -> x4, Pallas kernels: none -> 32.4 us  [the longest x1 11.3 us: gradient_of(): pl.pallas_call(gradient_kernel, grid_spec=pltpu.PrefetchScalarGridSpec(nu...]
    slice x55 -> x2, local copies, waits for them, and re-layouts: 25.1 us -> 0.93 us  [beside(): lax.slice_in_dim(block, 0, depth, axis=dim)]
    ppermute x32 -> x16, waiting for transfers between devices: 62.5 us -> 44.9 us  [the longest x5 22.5 us: beside(): lax.ppermute(lax.slice_in_dim(block, extent - depth, extent, axis=dim), a...]
    dot_general x2 -> x0, matrix products: 15.3 us -> none  [the longest x1 10.9 us: shards(): jnp.einsum('kl,kzxy->lzxy', own_hot, perturbations, precision=highest)]
  transfers between devices with their start and end apart: 35 -> 17, of which waited for: 27 -> 10; matrix products, arithmetic and copies ran while one was open for 1% -> 3% of each run, Pallas kernels for 0% -> 8%
where the time goes in v1:
time: 175 us; the launch traced here: 172 us
  waiting for transfers between devices  80.8 us (46%)
  starting transfers between devices  35.8 us (20%)
  Pallas kernels  32.4 us (19%)
  between operations  14.3 us (8%)
  local copies, waits for them, and re-layouts  6.03 us (3%)
  other arithmetic  2.52 us (1%)
    reduce_scatter x1, waiting for transfers between devices, shards(): lax.psum_scatter(partial_sums, 'member', scatter_dimension=0, tiled=True)  35.9 us
    ppermute x5, waiting for transfers between devices, beside(): lax.ppermute(lax.slice_in_dim(block, extent - depth, extent, axis=dim), a...  22.5 us
    ppermute x5, starting transfers between devices, beside(): lax.ppermute(lax.slice_in_dim(block, extent - depth, extent, axis=dim), a...  21.7 us
    ppermute x5, waiting for transfers between devices, beside(): lax.ppermute(lax.slice_in_dim(block, 0, depth, axis=dim), axis, backward)  17.8 us
    pallas_call x1, Pallas kernels, gradient_of(): pl.pallas_call(gradient_kernel, grid_spec=pltpu.PrefetchScalarGridSpec(nu...  11.3 us
    ppermute x5, starting transfers between devices, beside(): lax.ppermute(lax.slice_in_dim(block, 0, depth, axis=dim), axis, backward)  10.4 us
    pallas_call x1, Pallas kernels, smooth(): pl.pallas_call(smooth_kernel, grid=(fields,), in_specs=[block(top), block...  10.2 us
    pallas_call x1, Pallas kernels, member_sums(): pl.pallas_call(member_sums_kernel, grid_spec=pltpu.PrefetchScalarGridSpec...  7.56 us
  transfers between devices with their start and end apart: 17, of which 10 were waited for; matrix products, arithmetic and copies ran while one was open for 3% of the time, Pallas kernels for 8%

profile of v1, /device:TPU:19, one launch (start us, length us, event | category | flops | bytes accessed | tf_op | source)
XLA Modules:
  0.0 171.9 jit_solution(14365746457229516495)
XLA Ops:
  7.2 1.2 dynamic_slice.20.assign_ref
  8.5 7.6 %member_sums.1 = f32[16,8,16,512]{3,2,1,0:T(8,128)} custom-call(s32[16]{0:T(128)} %dynamic_slice.20.assign_ref, f32[16,8,16,512]{3,2,1,0:T(8,128)} %members_ref.1), custom_call_target="tpu_custom_call" | custom-call | flops 10000000 | bytes 8388608 | tf_op jit(solution)/shard_map/member_sums/pallas_call | solution.py:155
  16.0 3.8 %collective-permute-start.2 = (f32[4,8,16,512]{3,2,1,0:T(8,128)}, f32[4,8,16,512]{3,2,1,0:T(8,128)}, u32[]{:S(2)}, u32[]{:S(2)}) collective-permute-start(f32[4,8,16,512]{3,2,1,0:T(8,128)} %ctl_ref.1), channel_id=1, source_target_pairs={{0,4},{4,8},{8,12},{12,16},{16,20},{20,24},{24,28},{1,5},{5,9},{9,... | collective-permute-start | bytes 3145736 | tf_op jit(solution)/shard_map/ppermute | solution.py:237
  19.9 1.9 %collective-permute-start.3 = (f32[4,8,16,512]{3,2,1,0:T(8,128)}, f32[4,8,16,512]{3,2,1,0:T(8,128)}, u32[]{:S(2)}, u32[]{:S(2)}) collective-permute-start(f32[4,8,16,512]{3,2,1,0:T(8,128)} %ctl_ref.1), channel_id=1, source_target_pairs={{4,0},{8,4},{12,8},{16,12},{20,16},{24,20},{28,24},{5,1},{9,5},{13... | collective-permute-start | bytes 3145736 | tf_op jit(solution)/shard_map/ppermute | solution.py:238
  21.9 0.9 fusion.7
  22.9 2.5 %collective-permute-start.10 = (f32[18,2,8,512]{3,2,1,0:T(8,128)}, f32[18,2,8,512]{3,2,1,0:T(8,128)S(1)}, u32[]{:S(2)}, u32[]{:S(2)}) collective-permute-start(f32[18,2,8,512]{3,2,1,0:T(8,128)} %get-tuple-element.6), channel_id=1, source_target_pairs={{4,0},{8,4},{12,8},{16,12},{20,16},{24,20},{28,24},{5,1},{9,5},{13... | collective-permute-start | bytes 1769480 | tf_op jit(solution)/shard_map/ppermute | solution.py:238
  25.4 3.9 %collective-permute-start.9 = (f32[18,2,8,512]{3,2,1,0:T(8,128)S(1)}, f32[18,2,8,512]{3,2,1,0:T(8,128)S(1)}, u32[]{:S(2)}, u32[]{:S(2)}) collective-permute-start(f32[18,2,8,512]{3,2,1,0:T(8,128)S(1)} %get-tuple-element.7), channel_id=1, source_target_pairs={{0,4},{4,8},{8,12},{12,16},{16,20},{20,24},{24,28},{1,5},{5,9},{9,... | collective-permute-start | bytes 1769480 | tf_op jit(solution)/shard_map/ppermute | solution.py:237
  29.3 1.6 dynamic-slice_bitcast_fusion.fwd_ref
  31.0 9.4 %collective-permute-done.2.top_ref = f32[4,8,16,512]{3,2,1,0:T(8,128)} collective-permute-done((f32[4,8,16,512]{3,2,1,0:T(8,128)}, f32[4,8,16,512]{3,2,1,0:T(8,128)}, u32[]{:S(2)}, u32[]{:S(2)}) %collective-permute-start.2) | collective-permute-done | bytes 1048608 | tf_op jit(solution)/shard_map/ppermute | solution.py:237
  40.4 8.0 %collective-permute-done.3.bot_ref = f32[4,8,16,512]{3,2,1,0:T(8,128)} collective-permute-done((f32[4,8,16,512]{3,2,1,0:T(8,128)}, f32[4,8,16,512]{3,2,1,0:T(8,128)}, u32[]{:S(2)}, u32[]{:S(2)}) %collective-permute-start.3) | collective-permute-done | bytes 1048608 | tf_op jit(solution)/shard_map/ppermute | solution.py:238
  48.4 10.2 %smooth.1 = f32[4,8,16,512]{3,2,1,0:T(8,128)} custom-call(f32[4,8,16,512]{3,2,1,0:T(8,128)} %collective-permute-done.2.top_ref, f32[4,8,16,512]{3,2,1,0:T(8,128)} %ctl_ref.1, f32[4,8,16,512]{3,2,1,0:T(8,128)} %collective-permute-done.3.bot_ref, bf16[2,512,512]{2,1,0:T(8,128)(2,1)} %constant.75.clone.col_ref, ...), custom_call_target="tpu_custom_call" | custom-call | flops 5000000000 | bytes 4194304 | tf_op jit(solution)/shard_map/smooth/pallas_call | solution.py:114
  58.6 35.9 %reduce-scatter.2.cloned.1.call-done.own_ref = f32[4,8,16,512]{3,2,1,0:T(8,128)} async-done(((f32[16,8,16,512]{3,2,1,0:T(8,128)}), f32[4,8,16,512]{3,2,1,0:T(8,128)}) %reduce-scatter.2.cloned.1.call-update) | async-done | bytes 1048592 | tf_op jit(solution)/shard_map/reduce_scatter | solution.py:263
  94.5 1.9 %multiply_reduce_fusion = f32[8,16,512]{2,1,0:T(8,128)S(1)} fusion(f32[4,8,16,512]{3,2,1,0:T(8,128)} %smooth.1, f32[4,8,16,512]{3,2,1,0:T(8,128)} %reduce-scatter.2.cloned.1.call-done.own_ref), kind=kLoop, calls=%fused_computation.1 | loop fusion | flops 458752 | bytes 2359296 | tf_op jit(solution)/shard_map/reduce_sum | solution.py:279
  96.6 0.8 collective-permute-start.5
  97.4 0.9 collective-permute-start.6
  98.3 1.3 collective-permute-done.4
  99.6 7.2 %collective-permute-start = (f32[4,8,16,512]{3,2,1,0:T(8,128)S(1)}, f32[4,8,16,512]{3,2,1,0:T(8,128)}, u32[]{:S(2)}, u32[]{:S(2)}) collective-permute-start(f32[4,8,16,512]{3,2,1,0:T(8,128)S(1)} %copy-done.1), channel_id=1, source_target_pairs={{0,4},{4,8},{8,12},{12,16},{16,20},{20,24},{24,28},{1,5},{5,9},{9,... | collective-permute-start | bytes 3145736 | tf_op jit(solution)/shard_map/ppermute | solution.py:237
  106.8 1.9 %collective-permute-start.1 = (f32[4,8,16,512]{3,2,1,0:T(8,128)S(1)}, f32[4,8,16,512]{3,2,1,0:T(8,128)}, u32[]{:S(2)}, u32[]{:S(2)}) collective-permute-start(f32[4,8,16,512]{3,2,1,0:T(8,128)S(1)} %copy-done.1), channel_id=1, source_target_pairs={{4,0},{8,4},{12,8},{16,12},{20,16},{24,20},{28,24},{5,1},{9,5},{13... | collective-permute-start | bytes 3145736 | tf_op jit(solution)/shard_map/ppermute | solution.py:238
  108.8 4.5 %collective-permute-start.7 = (f32[2,8,512]{2,1,0:T(8,128)S(1)}, f32[2,8,512]{2,1,0:T(8,128)S(1)}, u32[]{:S(2)}, u32[]{:S(2)}) collective-permute-start(f32[2,8,512]{2,1,0:T(8,128)S(1)} %get-tuple-element.12), channel_id=1, source_target_pairs={{0,4},{4,8},{8,12},{12,16},{16,20},{20,24},{24,28},{1,5},{5,9},{9,... | collective-permute-start | bytes 98312 | tf_op jit(solution)/shard_map/ppermute | solution.py:237
  113.3 1.9 %collective-permute-start.8 = (f32[2,8,512]{2,1,0:T(8,128)S(1)}, f32[2,8,512]{2,1,0:T(8,128)S(1)}, u32[]{:S(2)}, u32[]{:S(2)}) collective-permute-start(f32[2,8,512]{2,1,0:T(8,128)S(1)} %get-tuple-element.11), channel_id=1, source_target_pairs={{4,0},{8,4},{12,8},{16,12},{20,16},{24,20},{28,24},{5,1},{9,5},{13... | collective-permute-start | bytes 98312 | tf_op jit(solution)/shard_map/ppermute | solution.py:238
  115.3 12.3 %collective-permute-done.7.inc_top = f32[2,8,512]{2,1,0:T(8,128)S(1)} collective-permute-done((f32[2,8,512]{2,1,0:T(8,128)S(1)}, f32[2,8,512]{2,1,0:T(8,128)S(1)}, u32[]{:S(2)}, u32[]{:S(2)}) %collective-permute-start.7) | collective-permute-done | bytes 32800 | tf_op jit(solution)/shard_map/ppermute | solution.py:237
  127.6 4.4 %collective-permute-done.8.inc_bot = f32[2,8,512]{2,1,0:T(8,128)S(1)} collective-permute-done((f32[2,8,512]{2,1,0:T(8,128)S(1)}, f32[2,8,512]{2,1,0:T(8,128)S(1)}, u32[]{:S(2)}, u32[]{:S(2)}) %collective-permute-start.8) | collective-permute-done | bytes 32800 | tf_op jit(solution)/shard_map/ppermute | solution.py:238
  132.7 3.3 %transport.1 = (f32[2,16,512]{2,1,0:T(8,128)}, f32[2,16,512]{2,1,0:T(8,128)}) custom-call(f32[2,8,512]{2,1,0:T(8,128)} %copy-done.7, f32[2,16,512]{2,1,0:T(8,128)} %copy-done.4, f32[2,8,512]{2,1,0:T(8,128)} %copy-done.8, f32[18,2,8,512]{3,2,1,0:T(8,128)} %copy-done.3, f32[16,2,16,512]{3,2,1,0:T(8,128)} %bitcast.18, f32[18,2,8,512]{3,2,1,0:T(8,128)} %copy-done.2, ...), custom_call_target="tpu_custom_call" | custom-call | flops 100000000 | bytes 3145728 | tf_op jit(solution)/shard_map/transport/pallas_call | solution.py:224
  136.5 1.3 collective-permute-start.13
  137.8 0.9 constant_dynamic-update-slice_fusion.3
  138.7 3.0 %collective-permute-done.11 = f32[2,16,512]{2,1,0:T(8,128)S(1)} collective-permute-done((f32[2,16,512]{2,1,0:T(8,128)}, f32[2,16,512]{2,1,0:T(8,128)S(1)}, u32[]{:S(2)}, u32[]{:S(2)}) %collective-permute-start.11) | collective-permute-done | bytes 65568 | tf_op jit(solution)/shard_map/ppermute | solution.py:291
  142.1 2.3 %collective-permute-start.14 = (f32[8,16,512]{2,1,0:T(8,128)S(1)}, f32[8,16,512]{2,1,0:T(8,128)S(1)}, u32[]{:S(2)}, u32[]{:S(2)}) collective-permute-start(f32[8,16,512]{2,1,0:T(8,128)S(1)} %constant_dynamic-update-slice_fusion.aown_ref), channel_id=1, source_target_pairs={{0,4},{4,8},{8,12},{12,16},{16,20},{20,24},{24,28},{1,5},{5,9},{9,... | collective-permute-start | bytes 786440 | tf_op jit(solution)/shard_map/ppermute | solution.py:237
  144.4 2.1 %collective-permute-start.15 = (f32[8,16,512]{2,1,0:T(8,128)S(1)}, f32[8,16,512]{2,1,0:T(8,128)S(1)}, u32[]{:S(2)}, u32[]{:S(2)}) collective-permute-start(f32[8,16,512]{2,1,0:T(8,128)S(1)} %constant_dynamic-update-slice_fusion.aown_ref), channel_id=1, source_target_pairs={{4,0},{8,4},{12,8},{16,12},{20,16},{24,20},{28,24},{5,1},{9,5},{13... | collective-permute-start | bytes 786440 | tf_op jit(solution)/shard_map/ppermute | solution.py:238
  147.0 0.7 collective-permute-done.14.atop_ref
  147.7 5.3 %collective-permute-done.15.abot_ref = f32[8,16,512]{2,1,0:T(8,128)S(1)} collective-permute-done((f32[8,16,512]{2,1,0:T(8,128)S(1)}, f32[8,16,512]{2,1,0:T(8,128)S(1)}, u32[]{:S(2)}, u32[]{:S(2)}) %collective-permute-start.15) | collective-permute-done | bytes 262176 | tf_op jit(solution)/shard_map/ppermute | solution.py:238
  153.0 0.7 copy-done.11
  153.7 11.3 %gradient.1 = f32[4,8,16,512]{3,2,1,0:T(8,128)} custom-call(s32[8]{0:T(128)} %fusion.2.slot_ref, f32[4,8,16,512]{3,2,1,0:T(8,128)} %ctl_ref.1, f32[4,8,16,512]{3,2,1,0:T(8,128)} %collective-permute-done.top_ref, f32[4,8,16,512]{3,2,1,0:T(8,128)} %reduce-scatter.2.cloned.1.call-done.own_ref, f32[4,8,16,512]{3,2,1,0:T(8,128)} %collective-permute-done.1.bot_ref, ...), custom_call_target="tpu_custom_call" | custom-call | flops 5000000000 | bytes 5242880 | tf_op jit(solution)/shard_map/gradient/pallas_call | solution.py:129
  (44 shorter events, 2.5 us)
Async XLA Ops:
  7.2 87.3 %reduce-scatter.2.cloned.1.call-start = ((), (), s32[]{:S(2)}) async-start(), calls=%async_computation.1 | async-start | bytes 5242880 | tf_op jit(solution)/shard_map/reduce_scatter | solution.py:263
  16.0 5.8 %copy-start = (f32[4,4,2,16,512]{4,3,2,1,0:T(8,128)S(1)}, f32[4,4,2,16,512]{4,3,2,1,0:T(8,128)}, u32[]{:S(2)}) copy-start(f32[4,4,2,16,512]{4,3,2,1,0:T(8,128)} %param.13) | copy-start | bytes 3145732
  16.0 5.8 %copy-start.5 = (f32[2,16,512]{2,1,0:T(8,128)S(1)}, f32[2,16,512]{2,1,0:T(8,128)}, u32[]{:S(2)}) copy-start(f32[2,16,512]{2,1,0:T(8,128)} %inn_own.1) | copy-start | bytes 196612
  16.0 5.8 %copy-start.6 = (f32[2,16,512]{2,1,0:T(8,128)S(1)}, f32[2,16,512]{2,1,0:T(8,128)}, u32[]{:S(2)}) copy-start(f32[2,16,512]{2,1,0:T(8,128)} %obs_own.1) | copy-start | bytes 196612
  16.0 24.3 %collective-permute-start.2 = (f32[4,8,16,512]{3,2,1,0:T(8,128)}, f32[4,8,16,512]{3,2,1,0:T(8,128)}, u32[]{:S(2)}, u32[]{:S(2)}) collective-permute-start(f32[4,8,16,512]{3,2,1,0:T(8,128)} %ctl_ref.1), channel_id=1, source_target_pairs={{0,4},{4,8},{8,12},{12,16},{16,20},{20,24},{24,28},{1,5},{5,9},{9,... | collective-permute-start | bytes 3145736 | tf_op jit(solution)/shard_map/ppermute | solution.py:237
  19.9 28.6 %collective-permute-start.3 = (f32[4,8,16,512]{3,2,1,0:T(8,128)}, f32[4,8,16,512]{3,2,1,0:T(8,128)}, u32[]{:S(2)}, u32[]{:S(2)}) collective-permute-start(f32[4,8,16,512]{3,2,1,0:T(8,128)} %ctl_ref.1), channel_id=1, source_target_pairs={{4,0},{8,4},{12,8},{16,12},{20,16},{24,20},{28,24},{5,1},{9,5},{13... | collective-permute-start | bytes 3145736 | tf_op jit(solution)/shard_map/ppermute | solution.py:238
  22.9 90.5 %collective-permute-start.10 = (f32[18,2,8,512]{3,2,1,0:T(8,128)}, f32[18,2,8,512]{3,2,1,0:T(8,128)S(1)}, u32[]{:S(2)}, u32[]{:S(2)}) collective-permute-start(f32[18,2,8,512]{3,2,1,0:T(8,128)} %get-tuple-element.6), channel_id=1, source_target_pairs={{4,0},{8,4},{12,8},{16,12},{20,16},{24,20},{28,24},{5,1},{9,5},{13... | collective-permute-start | bytes 1769480 | tf_op jit(solution)/shard_map/ppermute | solution.py:238
  25.4 89.9 %collective-permute-start.9 = (f32[18,2,8,512]{3,2,1,0:T(8,128)S(1)}, f32[18,2,8,512]{3,2,1,0:T(8,128)S(1)}, u32[]{:S(2)}, u32[]{:S(2)}) collective-permute-start(f32[18,2,8,512]{3,2,1,0:T(8,128)S(1)} %get-tuple-element.7), channel_id=1, source_target_pairs={{0,4},{4,8},{8,12},{12,16},{16,20},{20,24},{24,28},{1,5},{5,9},{9,... | collective-permute-start | bytes 1769480 | tf_op jit(solution)/shard_map/ppermute | solution.py:237
  94.5 5.1 %copy-start.1 = (f32[4,8,16,512]{3,2,1,0:T(8,128)S(1)}, f32[4,8,16,512]{3,2,1,0:T(8,128)}, u32[]{:S(2)}) copy-start(f32[4,8,16,512]{3,2,1,0:T(8,128)} %reduce-scatter.2.cloned.1.call-done.own_ref) | copy-start | bytes 3145732
  96.4 3.2 %collective-permute-start.4 = (f32[2,16,512]{2,1,0:T(8,128)S(1)}, f32[2,16,512]{2,1,0:T(8,128)S(1)}, u32[]{:S(2)}, u32[]{:S(2)}) collective-permute-start(f32[2,16,512]{2,1,0:T(8,128)S(1)} %get-tuple-element.8), channel_id=1, source_target_pairs={{0,1},{1,2},{2,3},{3,0},{4,5},{5,6},{6,7},{7,4},{8,9},{9,10},{10,1... | collective-permute-start | bytes 196616 | tf_op jit(solution)/shard_map/ppermute | solution.py:284
  96.6 10.1 %collective-permute-start.5 = (f32[2,16,512]{2,1,0:T(8,128)S(1)}, f32[2,16,512]{2,1,0:T(8,128)S(1)}, u32[]{:S(2)}, u32[]{:S(2)}) collective-permute-start(f32[2,16,512]{2,1,0:T(8,128)S(1)} %get-tuple-element.10), channel_id=1, source_target_pairs={{0,2},{1,3},{2,0},{3,1},{4,6},{5,7},{6,4},{7,5},{8,10},{9,11},{10,... | collective-permute-start | bytes 196616 | tf_op jit(solution)/shard_map/ppermute | solution.py:284
  97.4 11.3 %collective-permute-start.6 = (f32[2,16,512]{2,1,0:T(8,128)S(1)}, f32[2,16,512]{2,1,0:T(8,128)S(1)}, u32[]{:S(2)}, u32[]{:S(2)}) collective-permute-start(f32[2,16,512]{2,1,0:T(8,128)S(1)} %get-tuple-element.9), channel_id=1, source_target_pairs={{0,3},{1,0},{2,1},{3,2},{4,7},{5,4},{6,5},{7,6},{8,11},{9,8},{10,9... | collective-permute-start | bytes 196616 | tf_op jit(solution)/shard_map/ppermute | solution.py:284
  99.6 53.4 %collective-permute-start = (f32[4,8,16,512]{3,2,1,0:T(8,128)S(1)}, f32[4,8,16,512]{3,2,1,0:T(8,128)}, u32[]{:S(2)}, u32[]{:S(2)}) collective-permute-start(f32[4,8,16,512]{3,2,1,0:T(8,128)S(1)} %copy-done.1), channel_id=1, source_target_pairs={{0,4},{4,8},{8,12},{12,16},{16,20},{20,24},{24,28},{1,5},{5,9},{9,... | collective-permute-start | bytes 3145736 | tf_op jit(solution)/shard_map/ppermute | solution.py:237
  106.8 46.2 %collective-permute-start.1 = (f32[4,8,16,512]{3,2,1,0:T(8,128)S(1)}, f32[4,8,16,512]{3,2,1,0:T(8,128)}, u32[]{:S(2)}, u32[]{:S(2)}) collective-permute-start(f32[4,8,16,512]{3,2,1,0:T(8,128)S(1)} %copy-done.1), channel_id=1, source_target_pairs={{4,0},{8,4},{12,8},{16,12},{20,16},{24,20},{28,24},{5,1},{9,5},{13... | collective-permute-start | bytes 3145736 | tf_op jit(solution)/shard_map/ppermute | solution.py:238
  108.7 23.3 %copy-start.4 = (f32[2,16,512]{2,1,0:T(8,128)}, f32[2,16,512]{2,1,0:T(8,128)S(1)}, u32[]{:S(2)}) copy-start(f32[2,16,512]{2,1,0:T(8,128)S(1)} %fusion.1.inc_own) | copy-start | bytes 196612
  108.8 18.9 %collective-permute-start.7 = (f32[2,8,512]{2,1,0:T(8,128)S(1)}, f32[2,8,512]{2,1,0:T(8,128)S(1)}, u32[]{:S(2)}, u32[]{:S(2)}) collective-permute-start(f32[2,8,512]{2,1,0:T(8,128)S(1)} %get-tuple-element.12), channel_id=1, source_target_pairs={{0,4},{4,8},{8,12},{12,16},{16,20},{20,24},{24,28},{1,5},{5,9},{9,... | collective-permute-start | bytes 98312 | tf_op jit(solution)/shard_map/ppermute | solution.py:237
  113.3 18.7 %copy-start.2 = (f32[18,2,8,512]{3,2,1,0:T(8,128)}, f32[18,2,8,512]{3,2,1,0:T(8,128)S(1)}, u32[]{:S(2)}) copy-start(f32[18,2,8,512]{3,2,1,0:T(8,128)S(1)} %collective-permute-done.10.con_bot) | copy-start | bytes 1769476
  113.3 18.7 %collective-permute-start.8 = (f32[2,8,512]{2,1,0:T(8,128)S(1)}, f32[2,8,512]{2,1,0:T(8,128)S(1)}, u32[]{:S(2)}, u32[]{:S(2)}) collective-permute-start(f32[2,8,512]{2,1,0:T(8,128)S(1)} %get-tuple-element.11), channel_id=1, source_target_pairs={{4,0},{8,4},{12,8},{16,12},{20,16},{24,20},{28,24},{5,1},{9,5},{13... | collective-permute-start | bytes 98312 | tf_op jit(solution)/shard_map/ppermute | solution.py:238
  115.3 16.8 %copy-start.3 = (f32[18,2,8,512]{3,2,1,0:T(8,128)}, f32[18,2,8,512]{3,2,1,0:T(8,128)S(1)}, u32[]{:S(2)}) copy-start(f32[18,2,8,512]{3,2,1,0:T(8,128)S(1)} %collective-permute-done.9.con_top) | copy-start | bytes 1769476
  127.6 4.4 %copy-start.7 = (f32[2,8,512]{2,1,0:T(8,128)}, f32[2,8,512]{2,1,0:T(8,128)S(1)}, u32[]{:S(2)}) copy-start(f32[2,8,512]{2,1,0:T(8,128)S(1)} %collective-permute-done.7.inc_top) | copy-start | bytes 98308
  132.1 0.6 copy-start.8
  136.0 5.7 %collective-permute-start.11 = (f32[2,16,512]{2,1,0:T(8,128)}, f32[2,16,512]{2,1,0:T(8,128)S(1)}, u32[]{:S(2)}, u32[]{:S(2)}) collective-permute-start(f32[2,16,512]{2,1,0:T(8,128)} %get-tuple-element.4), channel_id=1, source_target_pairs={{0,1},{1,2},{2,3},{3,0},{4,5},{5,6},{6,7},{7,4},{8,9},{9,10},{10,1... | collective-permute-start | bytes 196616 | tf_op jit(solution)/shard_map/ppermute | solution.py:291
  136.0 5.7 %collective-permute-start.12 = (f32[2,16,512]{2,1,0:T(8,128)}, f32[2,16,512]{2,1,0:T(8,128)S(1)}, u32[]{:S(2)}, u32[]{:S(2)}) collective-permute-start(f32[2,16,512]{2,1,0:T(8,128)} %get-tuple-element.4), channel_id=1, source_target_pairs={{0,2},{1,3},{2,0},{3,1},{4,6},{5,7},{6,4},{7,5},{8,10},{9,11},{10,... | collective-permute-start | bytes 196616 | tf_op jit(solution)/shard_map/ppermute | solution.py:291
  136.5 5.6 %collective-permute-start.13 = (f32[2,16,512]{2,1,0:T(8,128)}, f32[2,16,512]{2,1,0:T(8,128)S(1)}, u32[]{:S(2)}, u32[]{:S(2)}) collective-permute-start(f32[2,16,512]{2,1,0:T(8,128)} %get-tuple-element.4), channel_id=1, source_target_pairs={{0,3},{1,0},{2,1},{3,2},{4,7},{5,4},{6,5},{7,6},{8,11},{9,8},{10,9... | collective-permute-start | bytes 196616 | tf_op jit(solution)/shard_map/ppermute | solution.py:291
  142.1 10.9 %copy-start.9 = (f32[8,16,512]{2,1,0:T(8,128)}, f32[8,16,512]{2,1,0:T(8,128)S(1)}, u32[]{:S(2)}) copy-start(f32[8,16,512]{2,1,0:T(8,128)S(1)} %constant_dynamic-update-slice_fusion.aown_ref) | copy-start | bytes 786436
  142.1 5.6 %collective-permute-start.14 = (f32[8,16,512]{2,1,0:T(8,128)S(1)}, f32[8,16,512]{2,1,0:T(8,128)S(1)}, u32[]{:S(2)}, u32[]{:S(2)}) collective-permute-start(f32[8,16,512]{2,1,0:T(8,128)S(1)} %constant_dynamic-update-slice_fusion.aown_ref), channel_id=1, source_target_pairs={{0,4},{4,8},{8,12},{12,16},{16,20},{20,24},{24,28},{1,5},{5,9},{9,... | collective-permute-start | bytes 786440 | tf_op jit(solution)/shard_map/ppermute | solution.py:237
  144.4 8.6 %collective-permute-start.15 = (f32[8,16,512]{2,1,0:T(8,128)S(1)}, f32[8,16,512]{2,1,0:T(8,128)S(1)}, u32[]{:S(2)}, u32[]{:S(2)}) collective-permute-start(f32[8,16,512]{2,1,0:T(8,128)S(1)} %constant_dynamic-update-slice_fusion.aown_ref), channel_id=1, source_target_pairs={{4,0},{8,4},{12,8},{16,12},{20,16},{24,20},{28,24},{5,1},{9,5},{13... | collective-permute-start | bytes 786440 | tf_op jit(solution)/shard_map/ppermute | solution.py:238
  147.7 5.3 %copy-start.10 = (f32[8,16,512]{2,1,0:T(8,128)}, f32[8,16,512]{2,1,0:T(8,128)S(1)}, u32[]{:S(2)}) copy-start(f32[8,16,512]{2,1,0:T(8,128)S(1)} %collective-permute-done.14.atop_ref) | copy-start | bytes 786436
  153.0 0.7 copy-start.11
Sparse Core Ops, SparseCore 0:
  16.2 78.2 reduce-scatter.1

commit v2 on v1

--- a/solution.py
+++ b/solution.py
@@ -8,11 +8,14 @@
 from jax.experimental.pallas import tpu as pltpu
 from jax.sharding import PartitionSpec as P
 
+
 FIELDS = 16
 PASSES = 16
 STEPS = 4
 RATE = 0.2
 STACK = 4
+TILE = 8
+PARTS = 2
 F32 = jnp.float32
 BF16 = jnp.bfloat16
 
@@ -79,42 +82,55 @@
 
 
 def smooth_kernel(top_ref, own_ref, bot_ref, col_ref, fwd_ref, bwd_ref, scale_ref, out_ref):
-    ext = jnp.concatenate([top_ref[0], own_ref[0], bot_ref[0]], axis=1)
-    out_ref[0] = diffuse_block(ext, col_ref, fwd_ref, bwd_ref, scale_ref, own_ref.shape[2])
-
-
-def gradient_kernel(
-    slot_ref, ctl_ref, top_ref, own_ref, bot_ref, atop_ref, aown_ref, abot_ref,
-    col_ref, fwd_ref, bwd_ref, scale_ref, out_ref,
-):
-    levels = own_ref.shape[1]
+    flat = lambda ref, rows: ref[...].reshape(-1, rows, ref.shape[-1])
+    ext = jnp.concatenate(
+        [flat(top_ref, PASSES), flat(own_ref, own_ref.shape[2]), flat(bot_ref, PASSES)], axis=1
+    )
+    out = diffuse_block(ext, col_ref, fwd_ref, bwd_ref, scale_ref, own_ref.shape[2])
+    out_ref[...] = out.reshape(out_ref.shape)
+
+
+def gradient_kernel(planes, ctl_ref, *refs):
+    sums, adjoints, tables, out_ref = refs[:-8], refs[-8:-5], refs[-5:-1], refs[-1]
+    step, levels, rows, _ = ctl_ref.shape
+    span = sums[0].shape[1]
+    own = levels // planes
+    plane = lax.axis_index("member")
+    slots = [lax.rem(plane + planes - z // own, planes) * own + z % own for z in range(levels)]
     parts = []
-    for z in range(levels):
-        s = slot_ref[z]
-        parts.append(
-            jnp.concatenate(
-                [top_ref[0, z] * atop_ref[s], own_ref[0, z] * aown_ref[s], bot_ref[0, z] * abot_ref[s]],
-                axis=0,
+    for f in range(step):
+        for z in range(levels):
+            blocks = sums[3 * (z // span) : 3 * (z // span) + 3]
+            parts.append(
+                jnp.concatenate([b[f, z % span] * a[slots[z]] for b, a in zip(blocks, adjoints)], axis=0)
             )
-        )
-    ext = jnp.stack(parts)
-    out_ref[0] = ctl_ref[0] + diffuse_block(ext, col_ref, fwd_ref, bwd_ref, scale_ref, own_ref.shape[2])
+    out = diffuse_block(jnp.stack(parts), *tables, rows)
+    out_ref[...] = ctl_ref[...] + out.reshape(out_ref.shape)
+
+
+def grid_place():
+    region, regions = lax.axis_index("region"), lax.axis_size("region")
+    return (region > 0).astype(jnp.int32) + (region == regions - 1).astype(jnp.int32)
 
 
 def table_specs(tables):
     def spec(t):
+        if t.ndim == 4:
+            return pl.BlockSpec((None,) + t.shape[1:], lambda *_: (grid_place(), 0, 0, 0))
         return pl.BlockSpec(t.shape, functools.partial(lambda n, *_: (0,) * n, t.ndim))
 
     return [spec(t) for t in tables]
 
 
 def smooth(top, own, bot, tables):
-    fields, levels, rows, cols = own.shape
-    block = lambda a: pl.BlockSpec((1,) + a.shape[1:], lambda f: (f, 0, 0, 0))
+    fields, levels, _, cols = own.shape
+    step = 2 if fields % 2 == 0 else 1
+    block = lambda a: pl.BlockSpec((step,) + a.shape[1:], lambda f: (f, 0, 0, 0))
+    halo = pl.BlockSpec((step * levels * PASSES // TILE, TILE, cols), lambda f: (f, 0, 0))
     return pl.pallas_call(
         smooth_kernel,
-        grid=(fields,),
-        in_specs=[block(top), block(own), block(bot)] + table_specs(tables),
+        grid=(fields // step,),
+        in_specs=[halo, block(own), halo] + table_specs(tables),
         out_specs=block(own),
         out_shape=jax.ShapeDtypeStruct(own.shape, F32),
         cost_estimate=pl.CostEstimate(flops=5 * 10**9, bytes_accessed=4 * own.size * 4, transcendentals=0),
@@ -122,48 +138,126 @@
     )(top, own, bot, *tables)
 
 
-def gradient_of(slots, controls, sums, adjoints, tables):
-    fields, levels, rows, cols = controls.shape
-    block = lambda a: pl.BlockSpec((1,) + a.shape[1:], lambda f, s: (f, 0, 0, 0))
-    whole = lambda a: pl.BlockSpec(a.shape, lambda f, s: (0, 0, 0))
-    return pl.pallas_call(
-        gradient_kernel,
-        grid_spec=pltpu.PrefetchScalarGridSpec(
-            num_scalar_prefetch=1,
-            grid=(fields,),
-            in_specs=[block(controls)]
-            + [block(a) for a in sums]
-            + [whole(a) for a in adjoints]
-            + table_specs(tables),
-            out_specs=block(controls),
-        ),
+def gradient_of(planes, controls, sums, adjoints, tables):
+    fields, _, _, _ = controls.shape
+    step = 2 if fields % 2 == 0 else 1
+    block = lambda a: pl.BlockSpec((step,) + a.shape[1:], lambda f: (f, 0, 0, 0))
+    return pl.pallas_call(
+        functools.partial(gradient_kernel, planes),
+        grid=(fields // step,),
+        in_specs=[block(controls)]
+        + [block(a) for a in sums]
+        + table_specs(adjoints)
+        + table_specs(tables),
+        out_specs=block(controls),
         out_shape=jax.ShapeDtypeStruct(controls.shape, F32),
         cost_estimate=pl.CostEstimate(flops=5 * 10**9, bytes_accessed=5 * controls.size * 4, transcendentals=0),
         name="gradient",
-    )(slots, controls, *sums, *adjoints, *tables)
-
-
-def member_sums_kernel(assign_ref, members_ref, out_ref):
+    )(controls, *sums, *adjoints, *tables)
+
+
+def member_sums_kernel(assign_ref, members_ref, out_ref, last_ref, first_ref):
+    members = members_ref.shape[0]
+    offset = lax.axis_index("member") * members
     out_ref[...] = jnp.zeros_like(out_ref)
-    for k in range(members_ref.shape[0]):
-        field = assign_ref[k]
+    for k in range(members):
+        field = assign_ref[offset + k]
         out_ref[field] = out_ref[field] + members_ref[k]
-
-
-def member_sums(assignment, perturbations):
-    members, levels, rows, cols = perturbations.shape
+    fields = first_ref.shape[0]
+    last_ref[...] = out_ref[out_ref.shape[0] - fields :]
+    first_ref[...] = out_ref[:fields]
+
+
+def member_sums(assignment, perturbations, part, levels, fields):
+    members, _, rows, cols = perturbations.shape
+    step = 2 if levels % 2 == 0 else 1
+    start = part * levels // step
+    spec = lambda n: pl.BlockSpec((n, step, rows, cols), lambda z, s: (0, z, 0, 0))
+    shape = lambda n: jax.ShapeDtypeStruct((n, levels, rows, cols), F32)
     return pl.pallas_call(
         member_sums_kernel,
         grid_spec=pltpu.PrefetchScalarGridSpec(
             num_scalar_prefetch=1,
-            grid=(levels,),
-            in_specs=[pl.BlockSpec((members, 1, rows, cols), lambda z, s: (0, z, 0, 0))],
-            out_specs=pl.BlockSpec((FIELDS, 1, rows, cols), lambda z, s: (0, z, 0, 0)),
+            grid=(levels // step,),
+            in_specs=[pl.BlockSpec((members, step, rows, cols), lambda z, s: (0, z + start, 0, 0))],
+            out_specs=(spec(FIELDS), spec(fields), spec(fields)),
         ),
-        out_shape=jax.ShapeDtypeStruct((FIELDS, levels, rows, cols), F32),
-        cost_estimate=pl.CostEstimate(flops=10**7, bytes_accessed=2 * perturbations.size * 4, transcendentals=0),
+        out_shape=(shape(FIELDS), shape(fields), shape(fields)),
+        cost_estimate=pl.CostEstimate(flops=10**7, bytes_accessed=perturbations.size * 4, transcendentals=0),
         name="member_sums",
     )(assignment, perturbations)
+
+
+def forward_kernel(index_ref, rise_ref, fall_ref, up_ref, down_ref, rise_out, fall_out):
+    rise_out[...] = rise_ref[...] + up_ref[...]
+    fall_out[...] = fall_ref[...] + down_ref[...]
+
+
+def block_spec(shape, which):
+    return pl.BlockSpec(shape, lambda i, s: (s[which],) + (0,) * (len(shape) - 1))
+
+
+def whole_spec(shape):
+    return pl.BlockSpec(shape, lambda i, s: (0,) * len(shape))
+
+
+def forward_sums(index, partial_sums, up, down):
+    spec = whole_spec(up.shape)
+    return pl.pallas_call(
+        forward_kernel,
+        grid_spec=pltpu.PrefetchScalarGridSpec(
+            num_scalar_prefetch=1,
+            grid=(1,),
+            in_specs=[block_spec(up.shape, 0), block_spec(up.shape, 1), spec, spec],
+            out_specs=(spec, spec),
+        ),
+        out_shape=(jax.ShapeDtypeStruct(up.shape, F32),) * 2,
+        cost_estimate=pl.CostEstimate(flops=10**6, bytes_accessed=6 * up.size * 4, transcendentals=0),
+        name="forward_sums",
+    )(index, partial_sums, partial_sums, up, down)
+
+
+def finish_kernel(planes, index_ref, field_ref, *refs):
+    parts, sums, outs, joined = refs[: 3 * PARTS], refs[3 * PARTS : 4 * PARTS], refs[4 * PARTS : -1], refs[-1]
+    span = parts[0].shape[1]
+    for p in range(PARTS):
+        own, up, down = parts[3 * p : 3 * p + 3]
+        levels = slice(p * span, (p + 1) * span)
+        term = None
+        for f in range(own.shape[0]):
+            total = own[f] + up[f] + down[f]
+            sums[p][f] = total
+            term = field_ref[f, levels] * total if term is None else term + field_ref[f, levels] * total
+        joined[levels] = term
+    own_levels = outs[0].shape[0]
+    plane = lax.axis_index("member")
+    for k, out in enumerate(outs):
+        start = lax.rem(plane + k, planes) * own_levels
+        for z in range(own_levels):
+            out[z] = joined[start + z]
+
+
+def finish_sums(index, partial_sums, up, down, smoothed, planes):
+    _, levels, rows, cols = smoothed.shape
+    spec = whole_spec(up[0].shape)
+    out_shapes = [u.shape for u in up] + [(levels // planes, rows, cols)] * planes
+    operands, specs = [smoothed], [whole_spec(smoothed.shape)]
+    for p in range(PARTS):
+        operands += [partial_sums[p], up[p], down[p]]
+        specs += [block_spec(up[p].shape, 0), spec, spec]
+    return pl.pallas_call(
+        functools.partial(finish_kernel, planes),
+        grid_spec=pltpu.PrefetchScalarGridSpec(
+            num_scalar_prefetch=1,
+            grid=(1,),
+            in_specs=specs,
+            out_specs=[whole_spec(o) for o in out_shapes],
+            scratch_shapes=[pltpu.VMEM((levels, rows, cols), F32)],
+        ),
+        out_shape=[jax.ShapeDtypeStruct(o, F32) for o in out_shapes],
+        cost_estimate=pl.CostEstimate(flops=10**6, bytes_accessed=5 * smoothed.size * 4, transcendentals=0),
+        name="finish_sums",
+    )(index, *operands)
 
 
 def shift_rows(x, by):
@@ -181,9 +275,10 @@
 
 
 def transport_kernel(
-    inc_top, inc_own, inc_bot, con_top, con_own, con_bot, obs_own, inn_own, dep_ref, adj_ref
+    inc_top, inc_own, inc_bot, top_ref, con_own, bot_ref, obs_own, inn_own, dep_ref, adj_ref
 ):
     halo = inc_top.shape[1]
+    con_top, con_bot = [r[...].reshape((-1,) + inc_top.shape) for r in (top_ref, bot_ref)]
     rows = inc_own.shape[1]
     join = lambda a, b, c: jnp.concatenate([a, b, c], axis=1)
     state = join(inc_top[...], inc_own[...], inc_bot[...])
@@ -219,10 +314,18 @@
     adj_ref[...] = state[:, halo : halo + rows]
 
 
-def transport(inc, con, obs_weight, innovation):
+def transport(inc, con, obs_weight, innovation, used):
     shape = jax.ShapeDtypeStruct(obs_weight.shape, F32)
+    whole = lambda a: pl.BlockSpec(a.shape, lambda i: (0,) * a.ndim)
+    tail = con[0].shape[0] - used
+    part = pl.BlockSpec(
+        (pl.Element(tail), pl.Element(con[0].shape[1]), pl.Element(con[0].shape[2])), lambda i: (used, 0, 0)
+    )
     return pl.pallas_call(
         transport_kernel,
+        grid=(1,),
+        in_specs=[whole(a) for a in inc] + [part, whole(con[1]), part, whole(obs_weight), whole(innovation)],
+        out_specs=(whole(obs_weight), whole(obs_weight)),
         out_shape=(shape, shape),
         cost_estimate=pl.CostEstimate(flops=10**8, bytes_accessed=3 * 2**20, transcendentals=0),
         name="transport",
@@ -243,59 +346,72 @@
     fields, levels, rows, cols = controls.shape
     planes = lax.axis_size("member")
     plane = lax.axis_index("member")
-    region = lax.axis_index("region")
     regions = lax.axis_size("region")
-    own_levels = levels // planes
     halo = 2 * STEPS
 
     col_basis, forward, backward, scale = diffusion_tables(rows, cols)
-    place = jnp.where(region == 0, 0, jnp.where(region == regions - 1, 2, 1))
     tables = (
         jnp.asarray(col_basis),
-        lax.dynamic_index_in_dim(jnp.asarray(forward), place, 0, keepdims=False),
+        jnp.asarray(forward),
         jnp.asarray(backward),
         jnp.asarray(scale),
     )
 
-    local_members = perturbations.shape[0]
-    own_assignment = lax.dynamic_slice_in_dim(assignment, plane * local_members, local_members, 0)
-    partial_sums = member_sums(own_assignment, perturbations)
-    sums = lax.psum_scatter(partial_sums, "member", scatter_dimension=0, tiled=True)
-
-    top, bot = beside(controls, 2, PASSES)
+    span = levels // PARTS
+    partial_sums = [member_sums(assignment, perturbations, p, span, fields) for p in range(PARTS)]
+
     flat = courant.reshape((4 * STEPS,) + courant.shape[2:])
-    ends = lambda a: jnp.concatenate([a[:, :halo], a[:, rows - halo :]], axis=1)
-    edge = jnp.concatenate(
-        [
-            jnp.concatenate([flat[:, :, :halo], flat[:, :, rows - halo :]], axis=2),
-            ends(obs_weight)[None],
-            ends(innovation)[None],
-        ],
-        axis=0,
-    )
-    con_top, con_bot = beside(edge, 2, halo)
+
+    def message(low):
+        cut = lambda a, dim, depth: lax.slice_in_dim(
+            a, *((0, depth) if low else (rows - depth, rows)), axis=dim
+        )
+        edge = [cut(flat, 2, halo), cut(obs_weight, 1, halo)[None], cut(innovation, 1, halo)[None]]
+        return jnp.concatenate(
+            [cut(controls, 2, PASSES).reshape(-1, TILE, cols)] + [e.reshape(-1, TILE, cols) for e in edge]
+        )
+
+    ahead = [(i, i + 1) for i in range(regions - 1)]
+    top = lax.ppermute(message(False), "region", ahead)
+    bot = lax.ppermute(message(True), "region", [(j, i) for i, j in ahead])
+    used = fields * levels * PASSES // TILE
     smoothed = smooth(top, controls, bot, tables)
 
-    partial = jnp.sum(smoothed * sums, 0).reshape(planes, own_levels, rows, cols)
-    pick = lambda k: lax.dynamic_index_in_dim(partial, lax.rem(plane + k, planes), 0, keepdims=False)
+    up = [None] * PARTS
+    down = [None] * PARTS
+    for t in range(planes - 1):
+        targets = jnp.clip(
+            jnp.stack([plane + (planes - 1) - t, plane - (planes - 1) + t]), 0, planes - 1
+        )
+        for p in range(PARTS):
+            whole, rise, fall = partial_sums[p]
+            if t > 0:
+                rise, fall = forward_sums(targets, whole, up[p], down[p])
+            up[p] = lax.ppermute(rise, "member", [(i, i + 1) for i in range(t + 1)])
+            down[p] = lax.ppermute(
+                fall, "member", [(planes - 1 - i, planes - 2 - i) for i in range(t + 1)]
+            )
+    finished = finish_sums(
+        plane[None], [whole for whole, _, _ in partial_sums], up, down, smoothed, planes
+    )
+    sums, partial = finished[:PARTS], finished[PARTS:]
     turn = lambda k: [(i, (i + k) % planes) for i in range(planes)]
-    increment = pick(0)
+    increment = partial[0]
     for k in range(1, planes):
-        increment = increment + lax.ppermute(pick(k), "member", turn(k))
+        increment = increment + lax.ppermute(partial[k], "member", turn(k))
     inc_top, inc_bot = beside(increment, 1, halo)
-    sums_top, sums_bot = beside(sums, 2, PASSES)
+    sums_ext = []
+    for p in range(PARTS):
+        sums_top, sums_bot = beside(sums[p], 2, PASSES)
+        sums_ext += [sums_top, sums[p], sums_bot]
     departure, adjoint = transport(
-        (inc_top, increment, inc_bot), (con_top, flat, con_bot), obs_weight, innovation
+        (inc_top, increment, inc_bot), (top, flat, bot), obs_weight, innovation, used
     )
     full = jnp.concatenate(
         [adjoint] + [lax.ppermute(adjoint, "member", turn(k)) for k in range(1, planes)], axis=0
     )
     adj_top, adj_bot = beside(full, 1, PASSES)
-    level = lax.iota(jnp.int32, levels)
-    slots = lax.rem(plane - level // own_levels + planes, planes) * own_levels + lax.rem(level, own_levels)
-    gradient = gradient_of(
-        slots, controls, (sums_top, sums, sums_bot), (adj_top, full, adj_bot), tables
-    )
+    gradient = gradient_of(planes, controls, sums_ext, (adj_top, full, adj_bot), tables)
     return (gradient, departure)
 
 

time: 175 us -> 172 us (0.983)
  the two profiles are of different devices: /device:TPU:19 before, /device:TPU:6 now
where the time goes in v2:
time: 172 us; the launch traced here: 171 us
  starting transfers between devices  70.6 us (41%)
  Pallas kernels  47.1 us (27%)
  waiting for transfers between devices  41.6 us (24%)
  local copies, waits for them, and re-layouts  6.59 us (4%)
  other arithmetic  4.2 us (2%)
    ppermute x6, starting transfers between devices, shards(): up[p] = lax.ppermute(rise, 'member', [(i, i + 1) for i in range(t + 1)])  27.5 us
    ppermute x4, waiting for transfers between devices, beside(): lax.ppermute(lax.slice_in_dim(block, extent - depth, extent, axis=dim), a...  23.2 us
    ppermute x4, starting transfers between devices, beside(): lax.ppermute(lax.slice_in_dim(block, 0, depth, axis=dim), axis, backward)  14.8 us
    pallas_call x4, Pallas kernels, forward_sums(): pl.pallas_call(forward_kernel, grid_spec=pltpu.PrefetchScalarGridSpec(num...  13.1 us
    pallas_call x1, Pallas kernels, gradient_of(): pl.pallas_call(functools.partial(gradient_kernel, planes), grid=(fields /...  10.4 us
    pallas_call x1, Pallas kernels, smooth(): pl.pallas_call(smooth_kernel, grid=(fields // step,), in_specs=[halo, blo...  9.34 us
    ppermute x6, starting transfers between devices, shards(): lax.ppermute(fall, 'member', [(planes - 1 - i, planes - 2 - i) for i in r...  8.43 us
    ppermute x4, starting transfers between devices, beside(): lax.ppermute(lax.slice_in_dim(block, extent - depth, extent, axis=dim), a...  7.81 us
  transfers between devices with their start and end apart: 28, of which 10 were waited for; matrix products, arithmetic and copies ran while one was open for 1% of the time, Pallas kernels for 18%

profile of v2, /device:TPU:6, one launch (start us, length us, event | category | flops | bytes accessed | tf_op | source)
XLA Modules:
  0.0 171.0 jit_solution(18087244490867062702)
XLA Ops:
  2.2 2.1 %fusion.3 = (f32[100,8,512]{2,1,0:T(8,128)}, f32[100,8,512]{2,1,0:T(8,128)}) fusion(f32[64,8,512]{2,1,0:T(8,128)S(1)} %bitcast.13, f32[2,8,512]{2,1,0:T(8,128)S(1)} %get-tuple-element.57, f32[2,8,512]{2,1,0:T(8,128)S(1)} %get-tuple-element.52, f32[32,8,512]{2,1,0:T(8,128)S(1)} %bitcast.11, f32[2,8,512]{2,1,0:T(8,128)S(1)} %get-tuple-element.56, ...), kind=kLoop, calls=%fused_computation.5 | loop fusion | flops 2457600 | bytes 5505024 | tf_op jit(solution)/shard_map/concatenate | solution.py:370
  6.3 2.5 %collective-permute-start = (f32[100,8,512]{2,1,0:T(8,128)}, f32[100,8,512]{2,1,0:T(8,128)S(1)}, u32[]{:S(2)}, u32[]{:S(2)}) collective-permute-start(f32[100,8,512]{2,1,0:T(8,128)} %get-tuple-element.47), channel_id=1, source_target_pairs={{0,4},{4,8},{8,12},{12,16},{16,20},{20,24},{24,28},{1,5},{5,9},{9,... | collective-permute-start | bytes 4915208 | tf_op jit(solution)/shard_map/ppermute | solution.py:375
  8.8 3.8 %member_sums.3 = (f32[16,4,16,512]{3,2,1,0:T(8,128)}, f32[4,4,16,512]{3,2,1,0:T(8,128)}, f32[4,4,16,512]{3,2,1,0:T(8,128)}) custom-call(s32[64]{0:T(128)} %assign_ref.3, f32[16,8,16,512]{3,2,1,0:T(8,128)} %members_ref.3), custom_call_target="tpu_custom_call" | custom-call | flops 10000000 | bytes 4194304 | tf_op jit(solution)/shard_map/member_sums/pallas_call | solution.py:177
  12.6 4.3 %collective-permute-start.8 = (f32[4,4,16,512]{3,2,1,0:T(8,128)}, f32[4,4,16,512]{3,2,1,0:T(8,128)}, u32[]{:S(2)}, u32[]{:S(2)}) collective-permute-start(f32[4,4,16,512]{3,2,1,0:T(8,128)} %get-tuple-element.32), channel_id=1, source_target_pairs={{0,1},{4,5},{8,9},{12,13},{16,17},{20,21},{24,25},{28,29}} | collective-permute-start | bytes 1572872 | tf_op jit(solution)/shard_map/ppermute | solution.py:390
  18.3 3.8 %member_sums.2 = (f32[16,4,16,512]{3,2,1,0:T(8,128)}, f32[4,4,16,512]{3,2,1,0:T(8,128)}, f32[4,4,16,512]{3,2,1,0:T(8,128)}) custom-call(s32[64]{0:T(128)} %assign_ref.3, f32[16,8,16,512]{3,2,1,0:T(8,128)} %members_ref.3), custom_call_target="tpu_custom_call" | custom-call | flops 10000000 | bytes 4194304 | tf_op jit(solution)/shard_map/member_sums/pallas_call | solution.py:177
  22.1 2.2 %collective-permute-start.2 = (f32[4,4,16,512]{3,2,1,0:T(8,128)}, f32[4,4,16,512]{3,2,1,0:T(8,128)}, u32[]{:S(2)}, u32[]{:S(2)}) collective-permute-start(f32[4,4,16,512]{3,2,1,0:T(8,128)} %get-tuple-element.25), channel_id=1, source_target_pairs={{0,1},{4,5},{8,9},{12,13},{16,17},{20,21},{24,25},{28,29}} | collective-permute-start | bytes 1572872 | tf_op jit(solution)/shard_map/ppermute | solution.py:390
  24.9 3.7 %collective-permute-done.8.up_ref = f32[4,4,16,512]{3,2,1,0:T(8,128)} collective-permute-done((f32[4,4,16,512]{3,2,1,0:T(8,128)}, f32[4,4,16,512]{3,2,1,0:T(8,128)}, u32[]{:S(2)}, u32[]{:S(2)}) %collective-permute-start.8) | collective-permute-done | bytes 524320 | tf_op jit(solution)/shard_map/ppermute | solution.py:390
  30.1 3.2 %forward_sums.6 = (f32[4,4,16,512]{3,2,1,0:T(8,128)}, f32[4,4,16,512]{3,2,1,0:T(8,128)}) custom-call(s32[2]{0:T(128)} %add_clamp_fusion.1.index_ref, f32[16,4,16,512]{3,2,1,0:T(8,128)} %get-tuple-element.31.rise_ref.fall_ref.refs_3_, f32[16,4,16,512]{3,2,1,0:T(8,128)} %get-tuple-element.31.rise_ref.fall_ref.refs_3_, ...), custom_call_target="tpu_custom_call" | custom-call | flops 1000000 | bytes 3145728 | tf_op jit(solution)/shard_map/forward_sums/pallas_call | solution.py:206
  33.4 5.2 %collective-permute-start.10 = (f32[4,4,16,512]{3,2,1,0:T(8,128)}, f32[4,4,16,512]{3,2,1,0:T(8,128)}, u32[]{:S(2)}, u32[]{:S(2)}) collective-permute-start(f32[4,4,16,512]{3,2,1,0:T(8,128)} %get-tuple-element.34), channel_id=1, source_target_pairs={{0,1},{1,2},{4,5},{5,6},{8,9},{9,10},{12,13},{13,14},{16,17},{17,1... | collective-permute-start | bytes 1572872 | tf_op jit(solution)/shard_map/ppermute | solution.py:390
  41.3 3.2 %forward_sums.4 = (f32[4,4,16,512]{3,2,1,0:T(8,128)}, f32[4,4,16,512]{3,2,1,0:T(8,128)}) custom-call(s32[2]{0:T(128)} %add_clamp_fusion.1.index_ref, f32[16,4,16,512]{3,2,1,0:T(8,128)} %get-tuple-element.24.rise_ref.fall_ref.refs_0_, f32[16,4,16,512]{3,2,1,0:T(8,128)} %get-tuple-element.24.rise_ref.fall_ref.refs_0_, ...), custom_call_target="tpu_custom_call" | custom-call | flops 1000000 | bytes 3145728 | tf_op jit(solution)/shard_map/forward_sums/pallas_call | solution.py:206
  44.6 5.0 %collective-permute-start.4 = (f32[4,4,16,512]{3,2,1,0:T(8,128)}, f32[4,4,16,512]{3,2,1,0:T(8,128)}, u32[]{:S(2)}, u32[]{:S(2)}) collective-permute-start(f32[4,4,16,512]{3,2,1,0:T(8,128)} %get-tuple-element.27), channel_id=1, source_target_pairs={{0,1},{1,2},{4,5},{5,6},{8,9},{9,10},{12,13},{13,14},{16,17},{17,1... | collective-permute-start | bytes 1572872 | tf_op jit(solution)/shard_map/ppermute | solution.py:390
  53.2 3.3 %forward_sums.7 = (f32[4,4,16,512]{3,2,1,0:T(8,128)}, f32[4,4,16,512]{3,2,1,0:T(8,128)}) custom-call(s32[2]{0:T(128)} %add_clamp_fusion.index_ref, f32[16,4,16,512]{3,2,1,0:T(8,128)} %get-tuple-element.31.rise_ref.fall_ref.refs_3_, f32[16,4,16,512]{3,2,1,0:T(8,128)} %get-tuple-element.31.rise_ref.fall_ref.refs_3_, ...), custom_call_target="tpu_custom_call" | custom-call | flops 1000000 | bytes 3145728 | tf_op jit(solution)/shard_map/forward_sums/pallas_call | solution.py:206
  56.5 5.0 %collective-permute-start.12 = (f32[4,4,16,512]{3,2,1,0:T(8,128)}, f32[4,4,16,512]{3,2,1,0:T(8,128)}, u32[]{:S(2)}, u32[]{:S(2)}) collective-permute-start(f32[4,4,16,512]{3,2,1,0:T(8,128)} %get-tuple-element.36), channel_id=1, source_target_pairs={{0,1},{1,2},{2,3},{4,5},{5,6},{6,7},{8,9},{9,10},{10,11},{12,13},{... | collective-permute-start | bytes 1572872 | tf_op jit(solution)/shard_map/ppermute | solution.py:390
  63.7 3.3 %forward_sums.5 = (f32[4,4,16,512]{3,2,1,0:T(8,128)}, f32[4,4,16,512]{3,2,1,0:T(8,128)}) custom-call(s32[2]{0:T(128)} %add_clamp_fusion.index_ref, f32[16,4,16,512]{3,2,1,0:T(8,128)} %get-tuple-element.24.rise_ref.fall_ref.refs_0_, f32[16,4,16,512]{3,2,1,0:T(8,128)} %get-tuple-element.24.rise_ref.fall_ref.refs_0_, ...), custom_call_target="tpu_custom_call" | custom-call | flops 1000000 | bytes 3145728 | tf_op jit(solution)/shard_map/forward_sums/pallas_call | solution.py:206
  66.9 5.8 %collective-permute-start.6 = (f32[4,4,16,512]{3,2,1,0:T(8,128)}, f32[4,4,16,512]{3,2,1,0:T(8,128)}, u32[]{:S(2)}, u32[]{:S(2)}) collective-permute-start(f32[4,4,16,512]{3,2,1,0:T(8,128)} %get-tuple-element.29), channel_id=1, source_target_pairs={{0,1},{1,2},{2,3},{4,5},{5,6},{6,7},{8,9},{9,10},{10,11},{12,13},{... | collective-permute-start | bytes 1572872 | tf_op jit(solution)/shard_map/ppermute | solution.py:390
  75.3 9.3 %smooth.1.field_ref = f32[4,8,16,512]{3,2,1,0:T(8,128)} custom-call(f32[100,8,512]{2,1,0:T(8,128)} %copy-done.1, f32[4,8,16,512]{3,2,1,0:T(8,128)} %ctl_ref.1, f32[100,8,512]{2,1,0:T(8,128)} %copy-done, bf16[2,512,512]{2,1,0:T(8,128)(2,1)} %constant.29.clone.col_ref.refs_9_, bf16[3,2,192,192]{3,2,1,0:T(8,128)(2,1)} %constant.30.clone.fwd_ref.refs_10_, ...), custom_call_target="tpu_custom_call" | custom-call | flops 5000000000 | bytes 4194304 | tf_op jit(solution)/shard_map/smooth/pallas_call | solution.py:130
  84.7 2.6 %collective-permute-done.7.refs_2_ = f32[4,4,16,512]{3,2,1,0:T(8,128)} collective-permute-done((f32[4,4,16,512]{3,2,1,0:T(8,128)}, f32[4,4,16,512]{3,2,1,0:T(8,128)}, u32[]{:S(2)}, u32[]{:S(2)}) %collective-permute-start.7) | collective-permute-done | bytes 524320 | tf_op jit(solution)/shard_map/ppermute | solution.py:391
  87.3 3.3 %finish_sums.1 = (f32[4,4,16,512]{3,2,1,0:T(8,128)}, f32[4,4,16,512]{3,2,1,0:T(8,128)}, f32[2,16,512]{2,1,0:T(8,128)}, f32[2,16,512]{2,1,0:T(8,128)}, f32[2,16,512]{2,1,0:T(8,128)}, /*index=5*/f32[2,16,512]{2,1,0:T(8,128)}) custom-call(s32[1]{0:T(128)} %bitcast.index_ref, f32[4,8,16,512]{3,2,1,0:T(8,128)} %smooth.1.field_ref, ...), custom_call_target="tpu_custom_call" | custom-call | flops 1000000 | bytes 5242880 | tf_op jit(solution)/shard_map/finish_sums/pallas_call | solution.py:248
  92.4 2.4 %collective-permute-start.20 = (f32[2,16,512]{2,1,0:T(8,128)}, f32[2,16,512]{2,1,0:T(8,128)S(1)}, u32[]{:S(2)}, u32[]{:S(2)}) collective-permute-start(f32[2,16,512]{2,1,0:T(8,128)} %get-tuple-element.43), channel_id=1, source_target_pairs={{0,3},{1,0},{2,1},{3,2},{4,7},{5,4},{6,5},{7,6},{8,11},{9,8},{10,9... | collective-permute-start | bytes 196616 | tf_op jit(solution)/shard_map/ppermute | solution.py:401
  94.8 2.1 %collective-permute-done.18 = f32[2,16,512]{2,1,0:T(8,128)S(1)} collective-permute-done((f32[2,16,512]{2,1,0:T(8,128)}, f32[2,16,512]{2,1,0:T(8,128)S(1)}, u32[]{:S(2)}, u32[]{:S(2)}) %collective-permute-start.18) | collective-permute-done | bytes 65568 | tf_op jit(solution)/shard_map/ppermute | solution.py:401
  99.2 2.5 %collective-permute-start.22 = (f32[2,8,512]{2,1,0:T(8,128)S(1)}, f32[2,8,512]{2,1,0:T(8,128)S(1)}, u32[]{:S(2)}, u32[]{:S(2)}) collective-permute-start(f32[2,8,512]{2,1,0:T(8,128)S(1)} %get-tuple-element.50), channel_id=1, source_target_pairs={{4,0},{8,4},{12,8},{16,12},{20,16},{24,20},{28,24},{5,1},{9,5},{13... | collective-permute-start | bytes 98312 | tf_op jit(solution)/shard_map/ppermute | solution.py:341
  101.8 2.1 %collective-permute-start.21 = (f32[2,8,512]{2,1,0:T(8,128)S(1)}, f32[2,8,512]{2,1,0:T(8,128)S(1)}, u32[]{:S(2)}, u32[]{:S(2)}) collective-permute-start(f32[2,8,512]{2,1,0:T(8,128)S(1)} %get-tuple-element.51), channel_id=1, source_target_pairs={{0,4},{4,8},{8,12},{12,16},{16,20},{20,24},{24,28},{1,5},{5,9},{9,... | collective-permute-start | bytes 98312 | tf_op jit(solution)/shard_map/ppermute | solution.py:340
  103.8 5.0 %collective-permute-done.21.inc_top = f32[2,8,512]{2,1,0:T(8,128)S(1)} collective-permute-done((f32[2,8,512]{2,1,0:T(8,128)S(1)}, f32[2,8,512]{2,1,0:T(8,128)S(1)}, u32[]{:S(2)}, u32[]{:S(2)}) %collective-permute-start.21) | collective-permute-done | bytes 32800 | tf_op jit(solution)/shard_map/ppermute | solution.py:340
  109.5 3.3 %transport.1 = (f32[2,16,512]{2,1,0:T(8,128)}, f32[2,16,512]{2,1,0:T(8,128)}) custom-call(f32[2,8,512]{2,1,0:T(8,128)} %copy-done.7, f32[2,16,512]{2,1,0:T(8,128)} %copy-done.3, f32[2,8,512]{2,1,0:T(8,128)} %copy-done.6, f32[100,8,512]{2,1,0:T(8,128)} %copy-done.1, f32[16,2,16,512]{3,2,1,0:T(8,128)} %bitcast.10, f32[100,8,512]{2,1,0:T(8,128)} %copy-done, ...), custom_call_target="tpu_custom_call" | custom-call | flops 100000000 | bytes 3145728 | tf_op jit(solution)/shard_map/transport/pallas_call | solution.py:324
  112.8 2.9 %collective-permute-start.25 = (f32[2,16,512]{2,1,0:T(8,128)}, f32[2,16,512]{2,1,0:T(8,128)S(1)}, u32[]{:S(2)}, u32[]{:S(2)}) collective-permute-start(f32[2,16,512]{2,1,0:T(8,128)} %get-tuple-element.44), channel_id=1, source_target_pairs={{0,3},{1,0},{2,1},{3,2},{4,7},{5,4},{6,5},{7,6},{8,11},{9,8},{10,9... | collective-permute-start | bytes 196616 | tf_op jit(solution)/shard_map/ppermute | solution.py:411
  117.2 4.8 %collective-permute-done.23 = f32[2,16,512]{2,1,0:T(8,128)S(1)} collective-permute-done((f32[2,16,512]{2,1,0:T(8,128)}, f32[2,16,512]{2,1,0:T(8,128)S(1)}, u32[]{:S(2)}, u32[]{:S(2)}) %collective-permute-start.23) | collective-permute-done | bytes 65568 | tf_op jit(solution)/shard_map/ppermute | solution.py:411
  122.1 1.9 %collective-permute-start.27 = (f32[8,16,512]{2,1,0:T(8,128)S(1)}, f32[8,16,512]{2,1,0:T(8,128)S(1)}, u32[]{:S(2)}, u32[]{:S(2)}) collective-permute-start(f32[8,16,512]{2,1,0:T(8,128)S(1)} %constant_dynamic-update-slice_fusion.refs_7_), channel_id=1, source_target_pairs={{4,0},{8,4},{12,8},{16,12},{20,16},{24,20},{28,24},{5,1},{9,5},{13... | collective-permute-start | bytes 786440 | tf_op jit(solution)/shard_map/ppermute | solution.py:341
  124.1 6.7 %collective-permute-start.15 = (f32[4,4,16,512]{3,2,1,0:T(8,128)S(1)}, f32[4,4,16,512]{3,2,1,0:T(8,128)S(1)}, u32[]{:S(2)}, u32[]{:S(2)}) collective-permute-start(f32[4,4,16,512]{3,2,1,0:T(8,128)S(1)} %copy-done.9), channel_id=1, source_target_pairs={{4,0},{8,4},{12,8},{16,12},{20,16},{24,20},{28,24},{5,1},{9,5},{13... | collective-permute-start | bytes 1572872 | tf_op jit(solution)/shard_map/ppermute | solution.py:341
  132.7 3.6 %collective-permute-start.17 = (f32[4,4,16,512]{3,2,1,0:T(8,128)S(1)}, f32[4,4,16,512]{3,2,1,0:T(8,128)S(1)}, u32[]{:S(2)}, u32[]{:S(2)}) collective-permute-start(f32[4,4,16,512]{3,2,1,0:T(8,128)S(1)} %copy-done.10), channel_id=1, source_target_pairs={{4,0},{8,4},{12,8},{16,12},{20,16},{24,20},{28,24},{5,1},{9,5},{13... | collective-permute-start | bytes 1572872 | tf_op jit(solution)/shard_map/ppermute | solution.py:341
  138.3 1.9 %collective-permute-start.26 = (f32[8,16,512]{2,1,0:T(8,128)S(1)}, f32[8,16,512]{2,1,0:T(8,128)S(1)}, u32[]{:S(2)}, u32[]{:S(2)}) collective-permute-start(f32[8,16,512]{2,1,0:T(8,128)S(1)} %constant_dynamic-update-slice_fusion.refs_7_), channel_id=1, source_target_pairs={{0,4},{4,8},{8,12},{12,16},{16,20},{20,24},{24,28},{1,5},{5,9},{9,... | collective-permute-start | bytes 786440 | tf_op jit(solution)/shard_map/ppermute | solution.py:340
  140.2 18.1 %collective-permute-done.26.refs_6_ = f32[8,16,512]{2,1,0:T(8,128)S(1)} collective-permute-done((f32[8,16,512]{2,1,0:T(8,128)S(1)}, f32[8,16,512]{2,1,0:T(8,128)S(1)}, u32[]{:S(2)}, u32[]{:S(2)}) %collective-permute-start.26) | collective-permute-done | bytes 262176 | tf_op jit(solution)/shard_map/ppermute | solution.py:340
  160.6 10.4 %gradient.1 = f32[4,8,16,512]{3,2,1,0:T(8,128)} custom-call(f32[4,8,16,512]{3,2,1,0:T(8,128)} %ctl_ref.1, f32[4,4,16,512]{3,2,1,0:T(8,128)} %copy-done.12, f32[4,4,16,512]{3,2,1,0:T(8,128)} %get-tuple-element.38.refs_1_, f32[4,4,16,512]{3,2,1,0:T(8,128)} %copy-done.11, f32[4,4,16,512]{3,2,1,0:T(8,128)} %copy-done.14, ...), custom_call_target="tpu_custom_call" | custom-call | flops 5000000000 | bytes 5242880 | tf_op jit(solution)/shard_map/gradient/pallas_call | solution.py:145
  (79 shorter events, 30.3 us)
Async XLA Ops:
  4.3 68.4 %collective-permute-start.1 = (f32[100,8,512]{2,1,0:T(8,128)}, f32[100,8,512]{2,1,0:T(8,128)S(1)}, u32[]{:S(2)}, u32[]{:S(2)}) collective-permute-start(f32[100,8,512]{2,1,0:T(8,128)} %get-tuple-element.46), channel_id=1, source_target_pairs={{4,0},{8,4},{12,8},{16,12},{20,16},{24,20},{28,24},{5,1},{9,5},{13... | collective-permute-start | bytes 4915208 | tf_op jit(solution)/shard_map/ppermute | solution.py:376
  6.3 67.8 %collective-permute-start = (f32[100,8,512]{2,1,0:T(8,128)}, f32[100,8,512]{2,1,0:T(8,128)S(1)}, u32[]{:S(2)}, u32[]{:S(2)}) collective-permute-start(f32[100,8,512]{2,1,0:T(8,128)} %get-tuple-element.47), channel_id=1, source_target_pairs={{0,4},{4,8},{8,12},{12,16},{16,20},{20,24},{24,28},{1,5},{5,9},{9,... | collective-permute-start | bytes 4915208 | tf_op jit(solution)/shard_map/ppermute | solution.py:375
  12.6 16.1 %collective-permute-start.8 = (f32[4,4,16,512]{3,2,1,0:T(8,128)}, f32[4,4,16,512]{3,2,1,0:T(8,128)}, u32[]{:S(2)}, u32[]{:S(2)}) collective-permute-start(f32[4,4,16,512]{3,2,1,0:T(8,128)} %get-tuple-element.32), channel_id=1, source_target_pairs={{0,1},{4,5},{8,9},{12,13},{16,17},{20,21},{24,25},{28,29}} | collective-permute-start | bytes 1572872 | tf_op jit(solution)/shard_map/ppermute | solution.py:390
  16.8 13.3 %collective-permute-start.9 = (f32[4,4,16,512]{3,2,1,0:T(8,128)}, f32[4,4,16,512]{3,2,1,0:T(8,128)}, u32[]{:S(2)}, u32[]{:S(2)}) collective-permute-start(f32[4,4,16,512]{3,2,1,0:T(8,128)} %get-tuple-element.33), channel_id=1, source_target_pairs={{3,2},{7,6},{11,10},{15,14},{19,18},{23,22},{27,26},{31,30}} | collective-permute-start | bytes 1572872 | tf_op jit(solution)/shard_map/ppermute | solution.py:391
  22.1 17.8 %collective-permute-start.2 = (f32[4,4,16,512]{3,2,1,0:T(8,128)}, f32[4,4,16,512]{3,2,1,0:T(8,128)}, u32[]{:S(2)}, u32[]{:S(2)}) collective-permute-start(f32[4,4,16,512]{3,2,1,0:T(8,128)} %get-tuple-element.25), channel_id=1, source_target_pairs={{0,1},{4,5},{8,9},{12,13},{16,17},{20,21},{24,25},{28,29}} | collective-permute-start | bytes 1572872 | tf_op jit(solution)/shard_map/ppermute | solution.py:390
  28.7 12.7 %collective-permute-start.3 = (f32[4,4,16,512]{3,2,1,0:T(8,128)}, f32[4,4,16,512]{3,2,1,0:T(8,128)}, u32[]{:S(2)}, u32[]{:S(2)}) collective-permute-start(f32[4,4,16,512]{3,2,1,0:T(8,128)} %get-tuple-element.26), channel_id=1, source_target_pairs={{3,2},{7,6},{11,10},{15,14},{19,18},{23,22},{27,26},{31,30}} | collective-permute-start | bytes 1572872 | tf_op jit(solution)/shard_map/ppermute | solution.py:391
  33.4 17.8 %collective-permute-start.10 = (f32[4,4,16,512]{3,2,1,0:T(8,128)}, f32[4,4,16,512]{3,2,1,0:T(8,128)}, u32[]{:S(2)}, u32[]{:S(2)}) collective-permute-start(f32[4,4,16,512]{3,2,1,0:T(8,128)} %get-tuple-element.34), channel_id=1, source_target_pairs={{0,1},{1,2},{4,5},{5,6},{8,9},{9,10},{12,13},{13,14},{16,17},{17,1... | collective-permute-start | bytes 1572872 | tf_op jit(solution)/shard_map/ppermute | solution.py:390
  39.9 13.3 %collective-permute-start.11 = (f32[4,4,16,512]{3,2,1,0:T(8,128)}, f32[4,4,16,512]{3,2,1,0:T(8,128)}, u32[]{:S(2)}, u32[]{:S(2)}) collective-permute-start(f32[4,4,16,512]{3,2,1,0:T(8,128)} %get-tuple-element.35), channel_id=1, source_target_pairs={{3,2},{2,1},{7,6},{6,5},{11,10},{10,9},{15,14},{14,13},{19,18},{18... | collective-permute-start | bytes 1572872 | tf_op jit(solution)/shard_map/ppermute | solution.py:391
  44.6 17.8 %collective-permute-start.4 = (f32[4,4,16,512]{3,2,1,0:T(8,128)}, f32[4,4,16,512]{3,2,1,0:T(8,128)}, u32[]{:S(2)}, u32[]{:S(2)}) collective-permute-start(f32[4,4,16,512]{3,2,1,0:T(8,128)} %get-tuple-element.27), channel_id=1, source_target_pairs={{0,1},{1,2},{4,5},{5,6},{8,9},{9,10},{12,13},{13,14},{16,17},{17,1... | collective-permute-start | bytes 1572872 | tf_op jit(solution)/shard_map/ppermute | solution.py:390
  51.1 12.5 %collective-permute-start.5 = (f32[4,4,16,512]{3,2,1,0:T(8,128)}, f32[4,4,16,512]{3,2,1,0:T(8,128)}, u32[]{:S(2)}, u32[]{:S(2)}) collective-permute-start(f32[4,4,16,512]{3,2,1,0:T(8,128)} %get-tuple-element.28), channel_id=1, source_target_pairs={{3,2},{2,1},{7,6},{6,5},{11,10},{10,9},{15,14},{14,13},{19,18},{18... | collective-permute-start | bytes 1572872 | tf_op jit(solution)/shard_map/ppermute | solution.py:391
  56.5 28.1 %collective-permute-start.12 = (f32[4,4,16,512]{3,2,1,0:T(8,128)}, f32[4,4,16,512]{3,2,1,0:T(8,128)}, u32[]{:S(2)}, u32[]{:S(2)}) collective-permute-start(f32[4,4,16,512]{3,2,1,0:T(8,128)} %get-tuple-element.36), channel_id=1, source_target_pairs={{0,1},{1,2},{2,3},{4,5},{5,6},{6,7},{8,9},{9,10},{10,11},{12,13},{... | collective-permute-start | bytes 1572872 | tf_op jit(solution)/shard_map/ppermute | solution.py:390
  62.4 22.3 %collective-permute-start.13 = (f32[4,4,16,512]{3,2,1,0:T(8,128)}, f32[4,4,16,512]{3,2,1,0:T(8,128)}, u32[]{:S(2)}, u32[]{:S(2)}) collective-permute-start(f32[4,4,16,512]{3,2,1,0:T(8,128)} %get-tuple-element.37), channel_id=1, source_target_pairs={{3,2},{2,1},{1,0},{7,6},{6,5},{5,4},{11,10},{10,9},{9,8},{15,14},{... | collective-permute-start | bytes 1572872 | tf_op jit(solution)/shard_map/ppermute | solution.py:391
  66.9 17.7 %collective-permute-start.6 = (f32[4,4,16,512]{3,2,1,0:T(8,128)}, f32[4,4,16,512]{3,2,1,0:T(8,128)}, u32[]{:S(2)}, u32[]{:S(2)}) collective-permute-start(f32[4,4,16,512]{3,2,1,0:T(8,128)} %get-tuple-element.29), channel_id=1, source_target_pairs={{0,1},{1,2},{2,3},{4,5},{5,6},{6,7},{8,9},{9,10},{10,11},{12,13},{... | collective-permute-start | bytes 1572872 | tf_op jit(solution)/shard_map/ppermute | solution.py:390
  72.8 14.5 %collective-permute-start.7 = (f32[4,4,16,512]{3,2,1,0:T(8,128)}, f32[4,4,16,512]{3,2,1,0:T(8,128)}, u32[]{:S(2)}, u32[]{:S(2)}) collective-permute-start(f32[4,4,16,512]{3,2,1,0:T(8,128)} %get-tuple-element.30), channel_id=1, source_target_pairs={{3,2},{2,1},{1,0},{7,6},{6,5},{5,4},{11,10},{10,9},{9,8},{15,14},{... | collective-permute-start | bytes 1572872 | tf_op jit(solution)/shard_map/ppermute | solution.py:391
  90.6 6.3 %collective-permute-start.18 = (f32[2,16,512]{2,1,0:T(8,128)}, f32[2,16,512]{2,1,0:T(8,128)S(1)}, u32[]{:S(2)}, u32[]{:S(2)}) collective-permute-start(f32[2,16,512]{2,1,0:T(8,128)} %get-tuple-element.41), channel_id=1, source_target_pairs={{0,1},{1,2},{2,3},{3,0},{4,5},{5,6},{6,7},{7,4},{8,9},{9,10},{10,1... | collective-permute-start | bytes 196616 | tf_op jit(solution)/shard_map/ppermute | solution.py:401
  92.4 5.9 %collective-permute-start.19 = (f32[2,16,512]{2,1,0:T(8,128)}, f32[2,16,512]{2,1,0:T(8,128)S(1)}, u32[]{:S(2)}, u32[]{:S(2)}) collective-permute-start(f32[2,16,512]{2,1,0:T(8,128)} %get-tuple-element.42), channel_id=1, source_target_pairs={{0,2},{1,3},{2,0},{3,1},{4,6},{5,7},{6,4},{7,5},{8,10},{9,11},{10,... | collective-permute-start | bytes 196616 | tf_op jit(solution)/shard_map/ppermute | solution.py:401
  92.4 5.9 %collective-permute-start.20 = (f32[2,16,512]{2,1,0:T(8,128)}, f32[2,16,512]{2,1,0:T(8,128)S(1)}, u32[]{:S(2)}, u32[]{:S(2)}) collective-permute-start(f32[2,16,512]{2,1,0:T(8,128)} %get-tuple-element.43), channel_id=1, source_target_pairs={{0,3},{1,0},{2,1},{3,2},{4,7},{5,4},{6,5},{7,6},{8,11},{9,8},{10,9... | collective-permute-start | bytes 196616 | tf_op jit(solution)/shard_map/ppermute | solution.py:401
  99.2 4.6 %collective-permute-start.22 = (f32[2,8,512]{2,1,0:T(8,128)S(1)}, f32[2,8,512]{2,1,0:T(8,128)S(1)}, u32[]{:S(2)}, u32[]{:S(2)}) collective-permute-start(f32[2,8,512]{2,1,0:T(8,128)S(1)} %get-tuple-element.50), channel_id=1, source_target_pairs={{4,0},{8,4},{12,8},{16,12},{20,16},{24,20},{28,24},{5,1},{9,5},{13... | collective-permute-start | bytes 98312 | tf_op jit(solution)/shard_map/ppermute | solution.py:341
  101.7 22.3 %copy-start.9 = (f32[4,4,16,512]{3,2,1,0:T(8,128)S(1)}, f32[4,4,16,512]{3,2,1,0:T(8,128)}, u32[]{:S(2)}) copy-start(f32[4,4,16,512]{3,2,1,0:T(8,128)} %get-tuple-element.38.refs_1_) | copy-start | bytes 1572868
  101.8 30.9 %copy-start.10 = (f32[4,4,16,512]{3,2,1,0:T(8,128)S(1)}, f32[4,4,16,512]{3,2,1,0:T(8,128)}, u32[]{:S(2)}) copy-start(f32[4,4,16,512]{3,2,1,0:T(8,128)} %get-tuple-element.39.refs_4_) | copy-start | bytes 1572868
  101.8 7.1 %collective-permute-start.21 = (f32[2,8,512]{2,1,0:T(8,128)S(1)}, f32[2,8,512]{2,1,0:T(8,128)S(1)}, u32[]{:S(2)}, u32[]{:S(2)}) collective-permute-start(f32[2,8,512]{2,1,0:T(8,128)S(1)} %get-tuple-element.51), channel_id=1, source_target_pairs={{0,4},{4,8},{8,12},{12,16},{16,20},{20,24},{24,28},{1,5},{5,9},{9,... | collective-permute-start | bytes 98312 | tf_op jit(solution)/shard_map/ppermute | solution.py:340
  112.8 9.2 %collective-permute-start.25 = (f32[2,16,512]{2,1,0:T(8,128)}, f32[2,16,512]{2,1,0:T(8,128)S(1)}, u32[]{:S(2)}, u32[]{:S(2)}) collective-permute-start(f32[2,16,512]{2,1,0:T(8,128)} %get-tuple-element.44), channel_id=1, source_target_pairs={{0,3},{1,0},{2,1},{3,2},{4,7},{5,4},{6,5},{7,6},{8,11},{9,8},{10,9... | collective-permute-start | bytes 196616 | tf_op jit(solution)/shard_map/ppermute | solution.py:411
  115.8 6.3 %collective-permute-start.24 = (f32[2,16,512]{2,1,0:T(8,128)}, f32[2,16,512]{2,1,0:T(8,128)S(1)}, u32[]{:S(2)}, u32[]{:S(2)}) collective-permute-start(f32[2,16,512]{2,1,0:T(8,128)} %get-tuple-element.44), channel_id=1, source_target_pairs={{0,2},{1,3},{2,0},{3,1},{4,6},{5,7},{6,4},{7,5},{8,10},{9,11},{10,... | collective-permute-start | bytes 196616 | tf_op jit(solution)/shard_map/ppermute | solution.py:411
  115.8 6.3 %collective-permute-start.23 = (f32[2,16,512]{2,1,0:T(8,128)}, f32[2,16,512]{2,1,0:T(8,128)S(1)}, u32[]{:S(2)}, u32[]{:S(2)}) collective-permute-start(f32[2,16,512]{2,1,0:T(8,128)} %get-tuple-element.44), channel_id=1, source_target_pairs={{0,1},{1,2},{2,3},{3,0},{4,5},{5,6},{6,7},{7,4},{8,9},{9,10},{10,1... | collective-permute-start | bytes 196616 | tf_op jit(solution)/shard_map/ppermute | solution.py:411
  122.1 36.9 %copy-start.8 = (f32[8,16,512]{2,1,0:T(8,128)}, f32[8,16,512]{2,1,0:T(8,128)S(1)}, u32[]{:S(2)}) copy-start(f32[8,16,512]{2,1,0:T(8,128)S(1)} %constant_dynamic-update-slice_fusion.refs_7_) | copy-start | bytes 786436
  122.1 16.1 %collective-permute-start.27 = (f32[8,16,512]{2,1,0:T(8,128)S(1)}, f32[8,16,512]{2,1,0:T(8,128)S(1)}, u32[]{:S(2)}, u32[]{:S(2)}) collective-permute-start(f32[8,16,512]{2,1,0:T(8,128)S(1)} %constant_dynamic-update-slice_fusion.refs_7_), channel_id=1, source_target_pairs={{4,0},{8,4},{12,8},{16,12},{20,16},{24,20},{28,24},{5,1},{9,5},{13... | collective-permute-start | bytes 786440 | tf_op jit(solution)/shard_map/ppermute | solution.py:341
  124.1 34.3 %collective-permute-start.15 = (f32[4,4,16,512]{3,2,1,0:T(8,128)S(1)}, f32[4,4,16,512]{3,2,1,0:T(8,128)S(1)}, u32[]{:S(2)}, u32[]{:S(2)}) collective-permute-start(f32[4,4,16,512]{3,2,1,0:T(8,128)S(1)} %copy-done.9), channel_id=1, source_target_pairs={{4,0},{8,4},{12,8},{16,12},{20,16},{24,20},{28,24},{5,1},{9,5},{13... | collective-permute-start | bytes 1572872 | tf_op jit(solution)/shard_map/ppermute | solution.py:341
  130.7 27.6 %collective-permute-start.14 = (f32[4,4,16,512]{3,2,1,0:T(8,128)S(1)}, f32[4,4,16,512]{3,2,1,0:T(8,128)S(1)}, u32[]{:S(2)}, u32[]{:S(2)}) collective-permute-start(f32[4,4,16,512]{3,2,1,0:T(8,128)S(1)} %copy-done.9), channel_id=1, source_target_pairs={{0,4},{4,8},{8,12},{12,16},{16,20},{20,24},{24,28},{1,5},{5,9},{9,... | collective-permute-start | bytes 1572872 | tf_op jit(solution)/shard_map/ppermute | solution.py:340
  132.7 25.7 %collective-permute-start.17 = (f32[4,4,16,512]{3,2,1,0:T(8,128)S(1)}, f32[4,4,16,512]{3,2,1,0:T(8,128)S(1)}, u32[]{:S(2)}, u32[]{:S(2)}) collective-permute-start(f32[4,4,16,512]{3,2,1,0:T(8,128)S(1)} %copy-done.10), channel_id=1, source_target_pairs={{4,0},{8,4},{12,8},{16,12},{20,16},{24,20},{28,24},{5,1},{9,5},{13... | collective-permute-start | bytes 1572872 | tf_op jit(solution)/shard_map/ppermute | solution.py:341
  136.3 22.7 %collective-permute-start.16 = (f32[4,4,16,512]{3,2,1,0:T(8,128)S(1)}, f32[4,4,16,512]{3,2,1,0:T(8,128)S(1)}, u32[]{:S(2)}, u32[]{:S(2)}) collective-permute-start(f32[4,4,16,512]{3,2,1,0:T(8,128)S(1)} %copy-done.10), channel_id=1, source_target_pairs={{0,4},{4,8},{8,12},{12,16},{16,20},{20,24},{24,28},{1,5},{5,9},{9,... | collective-permute-start | bytes 1572872 | tf_op jit(solution)/shard_map/ppermute | solution.py:340
  138.3 20.1 %copy-start.15 = (f32[8,16,512]{2,1,0:T(8,128)}, f32[8,16,512]{2,1,0:T(8,128)S(1)}, u32[]{:S(2)}) copy-start(f32[8,16,512]{2,1,0:T(8,128)S(1)} %collective-permute-done.27.refs_8_) | copy-start | bytes 786436
  138.3 20.0 %collective-permute-start.26 = (f32[8,16,512]{2,1,0:T(8,128)S(1)}, f32[8,16,512]{2,1,0:T(8,128)S(1)}, u32[]{:S(2)}, u32[]{:S(2)}) collective-permute-start(f32[8,16,512]{2,1,0:T(8,128)S(1)} %constant_dynamic-update-slice_fusion.refs_7_), channel_id=1, source_target_pairs={{0,4},{4,8},{8,12},{12,16},{16,20},{20,24},{24,28},{1,5},{5,9},{9,... | collective-permute-start | bytes 786440 | tf_op jit(solution)/shard_map/ppermute | solution.py:340
  (13 other events, 26.6 us)

commit v3 on v2

--- a/solution.py
+++ b/solution.py
@@ -15,6 +15,7 @@
 RATE = 0.2
 STACK = 4
 TILE = 8
+MIB = 2**20
 PARTS = 2
 F32 = jnp.float32
 BF16 = jnp.bfloat16
@@ -135,6 +136,7 @@
         out_shape=jax.ShapeDtypeStruct(own.shape, F32),
         cost_estimate=pl.CostEstimate(flops=5 * 10**9, bytes_accessed=4 * own.size * 4, transcendentals=0),
         name="smooth",
+        compiler_params=pltpu.CompilerParams(vmem_limit_bytes=20 * MIB),
     )(top, own, bot, *tables)
 
 
@@ -153,6 +155,7 @@
         out_shape=jax.ShapeDtypeStruct(controls.shape, F32),
         cost_estimate=pl.CostEstimate(flops=5 * 10**9, bytes_accessed=5 * controls.size * 4, transcendentals=0),
         name="gradient",
+        compiler_params=pltpu.CompilerParams(vmem_limit_bytes=24 * MIB),
     )(controls, *sums, *adjoints, *tables)
 
 
@@ -214,6 +217,7 @@
         out_shape=(jax.ShapeDtypeStruct(up.shape, F32),) * 2,
         cost_estimate=pl.CostEstimate(flops=10**6, bytes_accessed=6 * up.size * 4, transcendentals=0),
         name="forward_sums",
+        compiler_params=pltpu.CompilerParams(vmem_limit_bytes=14 * MIB),
     )(index, partial_sums, partial_sums, up, down)
 
 
@@ -257,6 +261,7 @@
         out_shape=[jax.ShapeDtypeStruct(o, F32) for o in out_shapes],
         cost_estimate=pl.CostEstimate(flops=10**6, bytes_accessed=5 * smoothed.size * 4, transcendentals=0),
         name="finish_sums",
+        compiler_params=pltpu.CompilerParams(vmem_limit_bytes=16 * MIB),
     )(index, *operands)
 
 
@@ -329,6 +334,7 @@
         out_shape=(shape, shape),
         cost_estimate=pl.CostEstimate(flops=10**8, bytes_accessed=3 * 2**20, transcendentals=0),
         name="transport",
+        compiler_params=pltpu.CompilerParams(vmem_limit_bytes=16 * MIB),
     )(*inc, *con, obs_weight, innovation)
 
 

time: 172 us -> 161 us (0.936)
  Pallas kernels: 47.1 us -> 35.1 us
  waiting for transfers between devices: 41.6 us -> 47.7 us
  local copies, waits for them, and re-layouts: 6.59 us -> 3.6 us
  other arithmetic: 4.2 us -> 2.31 us
    ppermute x6, waiting for transfers between devices: 7.44 us -> 13.2 us  [shards(): up[p] = lax.ppermute(rise, 'member', [(i, i + 1) for i in range(t + 1)])]
    pallas_call x4, Pallas kernels: 13.1 us -> 8.9 us  [forward_sums(): pl.pallas_call(forward_kernel, grid_spec=pltpu.PrefetchScalarGridSpec(num...]
    pallas_call x1, Pallas kernels: 3.32 us -> 0.25 us  [finish_sums(): pl.pallas_call(functools.partial(finish_kernel, planes), grid_spec=pltpu....]
    unnamed x37 -> x29, local copies, waits for them, and re-layouts: 5.2 us -> 2.21 us
    pallas_call x1, Pallas kernels: 10.4 us -> 7.6 us  [gradient_of(): pl.pallas_call(functools.partial(gradient_kernel, planes), grid=(fields /...]
    ppermute x4, waiting for transfers between devices: 23.2 us -> 21.4 us  [beside(): lax.ppermute(lax.slice_in_dim(block, extent - depth, extent, axis=dim), a...]
  transfers between devices with their start and end apart: 28 -> 28, of which waited for: 10 -> 11; matrix products, arithmetic and copies ran while one was open for 1% -> 0% of each run, Pallas kernels for 18% -> 15%
where the time goes in v3:
time: 161 us; the launch traced here: 160 us
  starting transfers between devices  70.5 us (44%)
  waiting for transfers between devices  47.7 us (30%)
  Pallas kernels  35.1 us (22%)
  local copies, waits for them, and re-layouts  3.6 us (2%)
  other arithmetic  2.31 us (1%)
    ppermute x6, starting transfers between devices, shards(): up[p] = lax.ppermute(rise, 'member', [(i, i + 1) for i in range(t + 1)])  26.4 us
    ppermute x4, waiting for transfers between devices, beside(): lax.ppermute(lax.slice_in_dim(block, extent - depth, extent, axis=dim), a...  21.4 us
    ppermute x4, starting transfers between devices, beside(): lax.ppermute(lax.slice_in_dim(block, 0, depth, axis=dim), axis, backward)  13.8 us
    ppermute x6, waiting for transfers between devices, shards(): up[p] = lax.ppermute(rise, 'member', [(i, i + 1) for i in range(t + 1)])  13.2 us
    pallas_call x4, Pallas kernels, forward_sums(): pl.pallas_call(forward_kernel, grid_spec=pltpu.PrefetchScalarGridSpec(num...  8.9 us
    pallas_call x1, Pallas kernels, smooth(): pl.pallas_call(smooth_kernel, grid=(fields // step,), in_specs=[halo, blo...  7.99 us
    ppermute x6, starting transfers between devices, shards(): lax.ppermute(fall, 'member', [(planes - 1 - i, planes - 2 - i) for i in r...  7.92 us
    ppermute x4, starting transfers between devices, beside(): lax.ppermute(lax.slice_in_dim(block, extent - depth, extent, axis=dim), a...  7.68 us
  transfers between devices with their start and end apart: 28, of which 11 were waited for; matrix products, arithmetic and copies ran while one was open for 0% of the time, Pallas kernels for 15%

profile of v3, /device:TPU:6, one launch (start us, length us, event | category | flops | bytes accessed | tf_op | source)
XLA Modules:
  0.0 160.3 jit_solution(9001291361118017854)
XLA Ops:
  2.2 2.1 %fusion.3 = (f32[100,8,512]{2,1,0:T(8,128)}, f32[100,8,512]{2,1,0:T(8,128)}) fusion(f32[64,8,512]{2,1,0:T(8,128)S(1)} %bitcast.11, f32[2,8,512]{2,1,0:T(8,128)S(1)} %get-tuple-element.57, f32[2,8,512]{2,1,0:T(8,128)S(1)} %get-tuple-element.52, f32[32,8,512]{2,1,0:T(8,128)S(1)} %bitcast.12, f32[2,8,512]{2,1,0:T(8,128)S(1)} %get-tuple-element.56, ...), kind=kLoop, calls=%fused_computation.5 | loop fusion | flops 2457600 | bytes 5505024 | tf_op jit(solution)/shard_map/concatenate | solution.py:376
  6.3 3.6 %collective-permute-start = (f32[100,8,512]{2,1,0:T(8,128)}, f32[100,8,512]{2,1,0:T(8,128)}, u32[]{:S(2)}, u32[]{:S(2)}) collective-permute-start(f32[100,8,512]{2,1,0:T(8,128)} %get-tuple-element.47), channel_id=1, source_target_pairs={{0,4},{4,8},{8,12},{12,16},{16,20},{20,24},{24,28},{1,5},{5,9},{9,... | collective-permute-start | bytes 4915208 | tf_op jit(solution)/shard_map/ppermute | solution.py:381
  9.9 3.8 %member_sums.3 = (f32[16,4,16,512]{3,2,1,0:T(8,128)}, f32[4,4,16,512]{3,2,1,0:T(8,128)}, f32[4,4,16,512]{3,2,1,0:T(8,128)}) custom-call(s32[64]{0:T(128)} %assign_ref.3, f32[16,8,16,512]{3,2,1,0:T(8,128)} %members_ref.3), custom_call_target="tpu_custom_call" | custom-call | flops 10000000 | bytes 4194304 | tf_op jit(solution)/shard_map/member_sums/pallas_call | solution.py:180
  13.6 4.3 %collective-permute-start.8 = (f32[4,4,16,512]{3,2,1,0:T(8,128)}, f32[4,4,16,512]{3,2,1,0:T(8,128)}, u32[]{:S(2)}, u32[]{:S(2)}) collective-permute-start(f32[4,4,16,512]{3,2,1,0:T(8,128)} %get-tuple-element.32), channel_id=1, source_target_pairs={{0,1},{4,5},{8,9},{12,13},{16,17},{20,21},{24,25},{28,29}} | collective-permute-start | bytes 1572872 | tf_op jit(solution)/shard_map/ppermute | solution.py:396
  19.6 3.8 %member_sums.2 = (f32[16,4,16,512]{3,2,1,0:T(8,128)}, f32[4,4,16,512]{3,2,1,0:T(8,128)}, f32[4,4,16,512]{3,2,1,0:T(8,128)}) custom-call(s32[64]{0:T(128)} %assign_ref.3, f32[16,8,16,512]{3,2,1,0:T(8,128)} %members_ref.3), custom_call_target="tpu_custom_call" | custom-call | flops 10000000 | bytes 4194304 | tf_op jit(solution)/shard_map/member_sums/pallas_call | solution.py:180
  23.3 2.1 %collective-permute-start.2 = (f32[4,4,16,512]{3,2,1,0:T(8,128)}, f32[4,4,16,512]{3,2,1,0:T(8,128)}, u32[]{:S(2)}, u32[]{:S(2)}) collective-permute-start(f32[4,4,16,512]{3,2,1,0:T(8,128)} %get-tuple-element.25), channel_id=1, source_target_pairs={{0,1},{4,5},{8,9},{12,13},{16,17},{20,21},{24,25},{28,29}} | collective-permute-start | bytes 1572872 | tf_op jit(solution)/shard_map/ppermute | solution.py:396
  25.5 4.2 %collective-permute-done.8.up_ref = f32[4,4,16,512]{3,2,1,0:T(8,128)} collective-permute-done((f32[4,4,16,512]{3,2,1,0:T(8,128)}, f32[4,4,16,512]{3,2,1,0:T(8,128)}, u32[]{:S(2)}, u32[]{:S(2)}) %collective-permute-start.8) | collective-permute-done | bytes 524320 | tf_op jit(solution)/shard_map/ppermute | solution.py:396
  30.5 2.7 %forward_sums.6 = (f32[4,4,16,512]{3,2,1,0:T(8,128)S(1)}, f32[4,4,16,512]{3,2,1,0:T(8,128)}) custom-call(s32[2]{0:T(128)S(1)} %add_clamp_fusion.1.index_ref, f32[16,4,16,512]{3,2,1,0:T(8,128)S(1)} %copy-done, f32[16,4,16,512]{3,2,1,0:T(8,128)S(1)} %copy-done, f32[4,4,16,512]{3,2,1,0:T(8,128)} %collective-permute-done.8.up_ref, ...), custom_call_target="tpu_custom_call" | custom-call | flops 1000000 | bytes 3145728 | tf_op jit(solution)/shard_map/forward_sums/pallas_call | solution.py:209
  33.2 4.4 %collective-permute-start.10 = (f32[4,4,16,512]{3,2,1,0:T(8,128)S(1)}, f32[4,4,16,512]{3,2,1,0:T(8,128)S(1)}, u32[]{:S(2)}, u32[]{:S(2)}) collective-permute-start(f32[4,4,16,512]{3,2,1,0:T(8,128)S(1)} %get-tuple-element.34), channel_id=1, source_target_pairs={{0,1},{1,2},{4,5},{5,6},{8,9},{9,10},{12,13},{13,14},{16,17},{17,1... | collective-permute-start | bytes 1572872 | tf_op jit(solution)/shard_map/ppermute | solution.py:396
  37.6 3.4 %collective-permute-done.2.up_ref = f32[4,4,16,512]{3,2,1,0:T(8,128)} collective-permute-done((f32[4,4,16,512]{3,2,1,0:T(8,128)}, f32[4,4,16,512]{3,2,1,0:T(8,128)}, u32[]{:S(2)}, u32[]{:S(2)}) %collective-permute-start.2) | collective-permute-done | bytes 524320 | tf_op jit(solution)/shard_map/ppermute | solution.py:396
  42.4 2.6 %forward_sums.4 = (f32[4,4,16,512]{3,2,1,0:T(8,128)}, f32[4,4,16,512]{3,2,1,0:T(8,128)}) custom-call(s32[2]{0:T(128)S(1)} %add_clamp_fusion.1.index_ref, f32[16,4,16,512]{3,2,1,0:T(8,128)S(1)} %copy-done.1, f32[16,4,16,512]{3,2,1,0:T(8,128)S(1)} %copy-done.1, f32[4,4,16,512]{3,2,1,0:T(8,128)} %collective-permute-done.2.up_ref, ...), custom_call_target="tpu_custom_call" | custom-call | flops 1000000 | bytes 3145728 | tf_op jit(solution)/shard_map/forward_sums/pallas_call | solution.py:209
  45.1 5.0 %collective-permute-start.4 = (f32[4,4,16,512]{3,2,1,0:T(8,128)}, f32[4,4,16,512]{3,2,1,0:T(8,128)}, u32[]{:S(2)}, u32[]{:S(2)}) collective-permute-start(f32[4,4,16,512]{3,2,1,0:T(8,128)} %get-tuple-element.27), channel_id=1, source_target_pairs={{0,1},{1,2},{4,5},{5,6},{8,9},{9,10},{12,13},{13,14},{16,17},{17,1... | collective-permute-start | bytes 1572872 | tf_op jit(solution)/shard_map/ppermute | solution.py:396
  50.1 2.0 %collective-permute-done.10.up_ref = f32[4,4,16,512]{3,2,1,0:T(8,128)S(1)} collective-permute-done((f32[4,4,16,512]{3,2,1,0:T(8,128)S(1)}, f32[4,4,16,512]{3,2,1,0:T(8,128)S(1)}, u32[]{:S(2)}, u32[]{:S(2)}) %collective-permute-start.10) | collective-permute-done | bytes 524320 | tf_op jit(solution)/shard_map/ppermute | solution.py:396
  57.3 4.3 %collective-permute-start.12 = (f32[4,4,16,512]{3,2,1,0:T(8,128)S(1)}, f32[4,4,16,512]{3,2,1,0:T(8,128)S(1)}, u32[]{:S(2)}, u32[]{:S(2)}) collective-permute-start(f32[4,4,16,512]{3,2,1,0:T(8,128)S(1)} %get-tuple-element.36), channel_id=1, source_target_pairs={{0,1},{1,2},{2,3},{4,5},{5,6},{6,7},{8,9},{9,10},{10,11},{12,13},{... | collective-permute-start | bytes 1572872 | tf_op jit(solution)/shard_map/ppermute | solution.py:396
  66.7 6.3 %collective-permute-start.6 = (f32[4,4,16,512]{3,2,1,0:T(8,128)S(1)}, f32[4,4,16,512]{3,2,1,0:T(8,128)S(1)}, u32[]{:S(2)}, u32[]{:S(2)}) collective-permute-start(f32[4,4,16,512]{3,2,1,0:T(8,128)S(1)} %get-tuple-element.29), channel_id=1, source_target_pairs={{0,1},{1,2},{2,3},{4,5},{5,6},{6,7},{8,9},{9,10},{10,11},{12,13},{... | collective-permute-start | bytes 1572872 | tf_op jit(solution)/shard_map/ppermute | solution.py:396
  74.4 8.0 %smooth.1.field_ref = f32[4,8,16,512]{3,2,1,0:T(8,128)S(1)} custom-call(f32[100,8,512]{2,1,0:T(8,128)} %collective-permute-done.top_ref, f32[4,8,16,512]{3,2,1,0:T(8,128)S(1)} %copy-done.4, f32[100,8,512]{2,1,0:T(8,128)} %collective-permute-done.1.bot_ref, bf16[2,512,512]{2,1,0:T(8,128)(2,1)S(1)} %copy-done.9, bf16[3,2,192,192]{3,2,1,0:T(8,128)(2,1)S(1)} %copy-done.10, ...), custom_call_target="tpu_custom_call" | custom-call | flops 5000000000 | bytes 4194304 | tf_op jit(solution)/shard_map/smooth/pallas_call | solution.py:131
  84.2 4.0 %collective-permute-done.7.refs_2_ = f32[4,4,16,512]{3,2,1,0:T(8,128)S(1)} collective-permute-done((f32[4,4,16,512]{3,2,1,0:T(8,128)S(1)}, f32[4,4,16,512]{3,2,1,0:T(8,128)S(1)}, u32[]{:S(2)}, u32[]{:S(2)}) %collective-permute-start.7) | collective-permute-done | bytes 524320 | tf_op jit(solution)/shard_map/ppermute | solution.py:397
  88.5 3.3 %collective-permute-start.18 = (f32[2,16,512]{2,1,0:T(8,128)S(1)}, f32[2,16,512]{2,1,0:T(8,128)S(1)}, u32[]{:S(2)}, u32[]{:S(2)}) collective-permute-start(f32[2,16,512]{2,1,0:T(8,128)S(1)} %get-tuple-element.41), channel_id=1, source_target_pairs={{0,1},{1,2},{2,3},{3,0},{4,5},{5,6},{6,7},{7,4},{8,9},{9,10},{10,1... | collective-permute-start | bytes 196616 | tf_op jit(solution)/shard_map/ppermute | solution.py:407
  91.8 2.4 %collective-permute-start.20 = (f32[2,16,512]{2,1,0:T(8,128)S(1)}, f32[2,16,512]{2,1,0:T(8,128)S(1)}, u32[]{:S(2)}, u32[]{:S(2)}) collective-permute-start(f32[2,16,512]{2,1,0:T(8,128)S(1)} %get-tuple-element.43), channel_id=1, source_target_pairs={{0,3},{1,0},{2,1},{3,2},{4,7},{5,4},{6,5},{7,6},{8,11},{9,8},{10,9... | collective-permute-start | bytes 196616 | tf_op jit(solution)/shard_map/ppermute | solution.py:407
  94.6 2.6 %collective-permute-done.19 = f32[2,16,512]{2,1,0:T(8,128)S(1)} collective-permute-done((f32[2,16,512]{2,1,0:T(8,128)S(1)}, f32[2,16,512]{2,1,0:T(8,128)S(1)}, u32[]{:S(2)}, u32[]{:S(2)}) %collective-permute-start.19) | collective-permute-done | bytes 65568 | tf_op jit(solution)/shard_map/ppermute | solution.py:407
  97.2 3.2 %collective-permute-start.22 = (f32[2,8,512]{2,1,0:T(8,128)S(1)}, f32[2,8,512]{2,1,0:T(8,128)S(1)}, u32[]{:S(2)}, u32[]{:S(2)}) collective-permute-start(f32[2,8,512]{2,1,0:T(8,128)S(1)} %get-tuple-element.50), channel_id=1, source_target_pairs={{4,0},{8,4},{12,8},{16,12},{20,16},{24,20},{28,24},{5,1},{9,5},{13... | collective-permute-start | bytes 98312 | tf_op jit(solution)/shard_map/ppermute | solution.py:347
  100.5 1.9 %collective-permute-start.21 = (f32[2,8,512]{2,1,0:T(8,128)S(1)}, f32[2,8,512]{2,1,0:T(8,128)S(1)}, u32[]{:S(2)}, u32[]{:S(2)}) collective-permute-start(f32[2,8,512]{2,1,0:T(8,128)S(1)} %get-tuple-element.51), channel_id=1, source_target_pairs={{0,4},{4,8},{8,12},{12,16},{16,20},{20,24},{24,28},{1,5},{5,9},{9,... | collective-permute-start | bytes 98312 | tf_op jit(solution)/shard_map/ppermute | solution.py:346
  102.4 3.3 %collective-permute-done.21.inc_top = f32[2,8,512]{2,1,0:T(8,128)S(1)} collective-permute-done((f32[2,8,512]{2,1,0:T(8,128)S(1)}, f32[2,8,512]{2,1,0:T(8,128)S(1)}, u32[]{:S(2)}, u32[]{:S(2)}) %collective-permute-start.21) | collective-permute-done | bytes 32800 | tf_op jit(solution)/shard_map/ppermute | solution.py:346
  105.7 2.8 %transport.1 = (f32[2,16,512]{2,1,0:T(8,128)}, f32[2,16,512]{2,1,0:T(8,128)S(1)}) custom-call(f32[2,8,512]{2,1,0:T(8,128)S(1)} %collective-permute-done.21.inc_top, f32[2,16,512]{2,1,0:T(8,128)S(1)} %add_add_fusion.inc_own, f32[2,8,512]{2,1,0:T(8,128)S(1)} %collective-permute-done.22.inc_bot, f32[100,8,512]{2,1,0:T(8,128)} %collective-permute-done.top_ref, ...), custom_call_target="tpu_custom_call" | custom-call | flops 100000000 | bytes 3145728 | tf_op jit(solution)/shard_map/transport/pallas_call | solution.py:329
  108.6 1.9 %collective-permute-start.25 = (f32[2,16,512]{2,1,0:T(8,128)S(1)}, f32[2,16,512]{2,1,0:T(8,128)S(1)}, u32[]{:S(2)}, u32[]{:S(2)}) collective-permute-start(f32[2,16,512]{2,1,0:T(8,128)S(1)} %get-tuple-element.44), channel_id=1, source_target_pairs={{0,3},{1,0},{2,1},{3,2},{4,7},{5,4},{6,5},{7,6},{8,11},{9,8},{10,9... | collective-permute-start | bytes 196616 | tf_op jit(solution)/shard_map/ppermute | solution.py:417
  112.0 6.1 %collective-permute-done.23 = f32[2,16,512]{2,1,0:T(8,128)S(1)} collective-permute-done((f32[2,16,512]{2,1,0:T(8,128)S(1)}, f32[2,16,512]{2,1,0:T(8,128)S(1)}, u32[]{:S(2)}, u32[]{:S(2)}) %collective-permute-start.23) | collective-permute-done | bytes 65568 | tf_op jit(solution)/shard_map/ppermute | solution.py:417
  118.1 1.9 %collective-permute-start.27 = (f32[8,16,512]{2,1,0:T(8,128)S(1)}, f32[8,16,512]{2,1,0:T(8,128)S(1)}, u32[]{:S(2)}, u32[]{:S(2)}) collective-permute-start(f32[8,16,512]{2,1,0:T(8,128)S(1)} %constant_dynamic-update-slice_fusion.refs_7_), channel_id=1, source_target_pairs={{4,0},{8,4},{12,8},{16,12},{20,16},{24,20},{28,24},{5,1},{9,5},{13... | collective-permute-start | bytes 786440 | tf_op jit(solution)/shard_map/ppermute | solution.py:347
  120.0 5.0 %collective-permute-start.15 = (f32[4,4,16,512]{3,2,1,0:T(8,128)S(1)}, f32[4,4,16,512]{3,2,1,0:T(8,128)S(1)}, u32[]{:S(2)}, u32[]{:S(2)}) collective-permute-start(f32[4,4,16,512]{3,2,1,0:T(8,128)S(1)} %get-tuple-element.38.refs_1_), channel_id=1, source_target_pairs={{4,0},{8,4},{12,8},{16,12},{20,16},{24,20},{28,24},{5,1},{9,5},{13... | collective-permute-start | bytes 1572872 | tf_op jit(solution)/shard_map/ppermute | solution.py:347
  127.0 3.6 %collective-permute-start.17 = (f32[4,4,16,512]{3,2,1,0:T(8,128)S(1)}, f32[4,4,16,512]{3,2,1,0:T(8,128)S(1)}, u32[]{:S(2)}, u32[]{:S(2)}) collective-permute-start(f32[4,4,16,512]{3,2,1,0:T(8,128)S(1)} %get-tuple-element.39.refs_4_), channel_id=1, source_target_pairs={{4,0},{8,4},{12,8},{16,12},{20,16},{24,20},{28,24},{5,1},{9,5},{13... | collective-permute-start | bytes 1572872 | tf_op jit(solution)/shard_map/ppermute | solution.py:347
  132.6 1.9 %collective-permute-start.26 = (f32[8,16,512]{2,1,0:T(8,128)S(1)}, f32[8,16,512]{2,1,0:T(8,128)S(1)}, u32[]{:S(2)}, u32[]{:S(2)}) collective-permute-start(f32[8,16,512]{2,1,0:T(8,128)S(1)} %constant_dynamic-update-slice_fusion.refs_7_), channel_id=1, source_target_pairs={{0,4},{4,8},{8,12},{12,16},{16,20},{20,24},{24,28},{1,5},{5,9},{9,... | collective-permute-start | bytes 786440 | tf_op jit(solution)/shard_map/ppermute | solution.py:346
  134.5 18.1 %collective-permute-done.26.refs_6_ = f32[8,16,512]{2,1,0:T(8,128)S(1)} collective-permute-done((f32[8,16,512]{2,1,0:T(8,128)S(1)}, f32[8,16,512]{2,1,0:T(8,128)S(1)}, u32[]{:S(2)}, u32[]{:S(2)}) %collective-permute-start.26) | collective-permute-done | bytes 262176 | tf_op jit(solution)/shard_map/ppermute | solution.py:346
  152.7 7.6 %gradient.1 = f32[4,8,16,512]{3,2,1,0:T(8,128)} custom-call(f32[4,8,16,512]{3,2,1,0:T(8,128)S(1)} %copy-done.4, f32[4,4,16,512]{3,2,1,0:T(8,128)S(1)} %collective-permute-done.14.refs_0_, f32[4,4,16,512]{3,2,1,0:T(8,128)S(1)} %get-tuple-element.38.refs_1_, f32[4,4,16,512]{3,2,1,0:T(8,128)S(1)} %collective-permute-done.15.refs_2_, ...), custom_call_target="tpu_custom_call" | custom-call | flops 5000000000 | bytes 5242880 | tf_op jit(solution)/shard_map/gradient/pallas_call | solution.py:147
  (71 shorter events, 26.7 us)
Async XLA Ops:
  4.4 68.7 %collective-permute-start.1 = (f32[100,8,512]{2,1,0:T(8,128)}, f32[100,8,512]{2,1,0:T(8,128)}, u32[]{:S(2)}, u32[]{:S(2)}) collective-permute-start(f32[100,8,512]{2,1,0:T(8,128)} %get-tuple-element.46), channel_id=1, source_target_pairs={{4,0},{8,4},{12,8},{16,12},{20,16},{24,20},{28,24},{5,1},{9,5},{13... | collective-permute-start | bytes 4915208 | tf_op jit(solution)/shard_map/ppermute | solution.py:382
  6.3 68.1 %collective-permute-start = (f32[100,8,512]{2,1,0:T(8,128)}, f32[100,8,512]{2,1,0:T(8,128)}, u32[]{:S(2)}, u32[]{:S(2)}) collective-permute-start(f32[100,8,512]{2,1,0:T(8,128)} %get-tuple-element.47), channel_id=1, source_target_pairs={{0,4},{4,8},{8,12},{12,16},{16,20},{20,24},{24,28},{1,5},{5,9},{9,... | collective-permute-start | bytes 4915208 | tf_op jit(solution)/shard_map/ppermute | solution.py:381
  13.6 16.1 %collective-permute-start.8 = (f32[4,4,16,512]{3,2,1,0:T(8,128)}, f32[4,4,16,512]{3,2,1,0:T(8,128)}, u32[]{:S(2)}, u32[]{:S(2)}) collective-permute-start(f32[4,4,16,512]{3,2,1,0:T(8,128)} %get-tuple-element.32), channel_id=1, source_target_pairs={{0,1},{4,5},{8,9},{12,13},{16,17},{20,21},{24,25},{28,29}} | collective-permute-start | bytes 1572872 | tf_op jit(solution)/shard_map/ppermute | solution.py:396
  17.9 12.5 %copy-start = (f32[16,4,16,512]{3,2,1,0:T(8,128)S(1)}, f32[16,4,16,512]{3,2,1,0:T(8,128)}, u32[]{:S(2)}) copy-start(f32[16,4,16,512]{3,2,1,0:T(8,128)} %get-tuple-element.31.rise_ref.fall_ref.refs_3_) | copy-start | bytes 6291460
  17.9 12.5 %collective-permute-start.9 = (f32[4,4,16,512]{3,2,1,0:T(8,128)}, f32[4,4,16,512]{3,2,1,0:T(8,128)}, u32[]{:S(2)}, u32[]{:S(2)}) collective-permute-start(f32[4,4,16,512]{3,2,1,0:T(8,128)} %get-tuple-element.33), channel_id=1, source_target_pairs={{3,2},{7,6},{11,10},{15,14},{19,18},{23,22},{27,26},{31,30}} | collective-permute-start | bytes 1572872 | tf_op jit(solution)/shard_map/ppermute | solution.py:397
  23.3 17.6 %collective-permute-start.2 = (f32[4,4,16,512]{3,2,1,0:T(8,128)}, f32[4,4,16,512]{3,2,1,0:T(8,128)}, u32[]{:S(2)}, u32[]{:S(2)}) collective-permute-start(f32[4,4,16,512]{3,2,1,0:T(8,128)} %get-tuple-element.25), channel_id=1, source_target_pairs={{0,1},{4,5},{8,9},{12,13},{16,17},{20,21},{24,25},{28,29}} | collective-permute-start | bytes 1572872 | tf_op jit(solution)/shard_map/ppermute | solution.py:396
  29.7 12.7 %collective-permute-start.3 = (f32[4,4,16,512]{3,2,1,0:T(8,128)}, f32[4,4,16,512]{3,2,1,0:T(8,128)S(1)}, u32[]{:S(2)}, u32[]{:S(2)}) collective-permute-start(f32[4,4,16,512]{3,2,1,0:T(8,128)} %get-tuple-element.26), channel_id=1, source_target_pairs={{3,2},{7,6},{11,10},{15,14},{19,18},{23,22},{27,26},{31,30}} | collective-permute-start | bytes 1572872 | tf_op jit(solution)/shard_map/ppermute | solution.py:397
  30.4 12.0 %copy-start.1 = (f32[16,4,16,512]{3,2,1,0:T(8,128)S(1)}, f32[16,4,16,512]{3,2,1,0:T(8,128)}, u32[]{:S(2)}) copy-start(f32[16,4,16,512]{3,2,1,0:T(8,128)} %get-tuple-element.24.rise_ref.fall_ref.refs_0_) | copy-start | bytes 6291460
  33.2 18.9 %collective-permute-start.10 = (f32[4,4,16,512]{3,2,1,0:T(8,128)S(1)}, f32[4,4,16,512]{3,2,1,0:T(8,128)S(1)}, u32[]{:S(2)}, u32[]{:S(2)}) collective-permute-start(f32[4,4,16,512]{3,2,1,0:T(8,128)S(1)} %get-tuple-element.34), channel_id=1, source_target_pairs={{0,1},{1,2},{4,5},{5,6},{8,9},{9,10},{12,13},{13,14},{16,17},{17,1... | collective-permute-start | bytes 1572872 | tf_op jit(solution)/shard_map/ppermute | solution.py:396
  41.0 13.5 %collective-permute-start.11 = (f32[4,4,16,512]{3,2,1,0:T(8,128)}, f32[4,4,16,512]{3,2,1,0:T(8,128)}, u32[]{:S(2)}, u32[]{:S(2)}) collective-permute-start(f32[4,4,16,512]{3,2,1,0:T(8,128)} %get-tuple-element.35), channel_id=1, source_target_pairs={{3,2},{2,1},{7,6},{6,5},{11,10},{10,9},{15,14},{14,13},{19,18},{18... | collective-permute-start | bytes 1572872 | tf_op jit(solution)/shard_map/ppermute | solution.py:397
  45.1 18.4 %collective-permute-start.4 = (f32[4,4,16,512]{3,2,1,0:T(8,128)}, f32[4,4,16,512]{3,2,1,0:T(8,128)}, u32[]{:S(2)}, u32[]{:S(2)}) collective-permute-start(f32[4,4,16,512]{3,2,1,0:T(8,128)} %get-tuple-element.27), channel_id=1, source_target_pairs={{0,1},{1,2},{4,5},{5,6},{8,9},{9,10},{12,13},{13,14},{16,17},{17,1... | collective-permute-start | bytes 1572872 | tf_op jit(solution)/shard_map/ppermute | solution.py:396
  52.9 12.0 %collective-permute-start.5 = (f32[4,4,16,512]{3,2,1,0:T(8,128)}, f32[4,4,16,512]{3,2,1,0:T(8,128)}, u32[]{:S(2)}, u32[]{:S(2)}) collective-permute-start(f32[4,4,16,512]{3,2,1,0:T(8,128)} %get-tuple-element.28), channel_id=1, source_target_pairs={{3,2},{2,1},{7,6},{6,5},{11,10},{10,9},{15,14},{14,13},{19,18},{18... | collective-permute-start | bytes 1572872 | tf_op jit(solution)/shard_map/ppermute | solution.py:397
  57.3 25.1 %collective-permute-start.12 = (f32[4,4,16,512]{3,2,1,0:T(8,128)S(1)}, f32[4,4,16,512]{3,2,1,0:T(8,128)S(1)}, u32[]{:S(2)}, u32[]{:S(2)}) collective-permute-start(f32[4,4,16,512]{3,2,1,0:T(8,128)S(1)} %get-tuple-element.36), channel_id=1, source_target_pairs={{0,1},{1,2},{2,3},{4,5},{5,6},{6,7},{8,9},{9,10},{10,11},{12,13},{... | collective-permute-start | bytes 1572872 | tf_op jit(solution)/shard_map/ppermute | solution.py:396
  63.4 11.0 %copy-start.12 = (bf16[2,64,192]{2,1,0:T(8,128)(2,1)S(1)}, bf16[2,64,192]{2,1,0:T(8,128)(2,1)}, u32[]{:S(2)}) copy-start(bf16[2,64,192]{2,1,0:T(8,128)(2,1)} %constant.31.clone.bwd_ref.refs_11_) | copy-start | bytes 147460
  63.4 19.0 %collective-permute-start.13 = (f32[4,4,16,512]{3,2,1,0:T(8,128)S(1)}, f32[4,4,16,512]{3,2,1,0:T(8,128)S(1)}, u32[]{:S(2)}, u32[]{:S(2)}) collective-permute-start(f32[4,4,16,512]{3,2,1,0:T(8,128)S(1)} %get-tuple-element.37), channel_id=1, source_target_pairs={{3,2},{2,1},{1,0},{7,6},{6,5},{5,4},{11,10},{10,9},{9,8},{15,14},{... | collective-permute-start | bytes 1572872 | tf_op jit(solution)/shard_map/ppermute | solution.py:397
  66.7 17.5 %collective-permute-start.6 = (f32[4,4,16,512]{3,2,1,0:T(8,128)S(1)}, f32[4,4,16,512]{3,2,1,0:T(8,128)S(1)}, u32[]{:S(2)}, u32[]{:S(2)}) collective-permute-start(f32[4,4,16,512]{3,2,1,0:T(8,128)S(1)} %get-tuple-element.29), channel_id=1, source_target_pairs={{0,1},{1,2},{2,3},{4,5},{5,6},{6,7},{8,9},{9,10},{10,11},{12,13},{... | collective-permute-start | bytes 1572872 | tf_op jit(solution)/shard_map/ppermute | solution.py:396
  73.1 15.1 %collective-permute-start.7 = (f32[4,4,16,512]{3,2,1,0:T(8,128)S(1)}, f32[4,4,16,512]{3,2,1,0:T(8,128)S(1)}, u32[]{:S(2)}, u32[]{:S(2)}) collective-permute-start(f32[4,4,16,512]{3,2,1,0:T(8,128)S(1)} %get-tuple-element.30), channel_id=1, source_target_pairs={{3,2},{2,1},{1,0},{7,6},{6,5},{5,4},{11,10},{10,9},{9,8},{15,14},{... | collective-permute-start | bytes 1572872 | tf_op jit(solution)/shard_map/ppermute | solution.py:397
  88.2 17.5 %copy-start.3 = (f32[4,4,2,16,512]{4,3,2,1,0:T(8,128)S(1)}, f32[4,4,2,16,512]{4,3,2,1,0:T(8,128)}, u32[]{:S(2)}) copy-start(f32[4,4,2,16,512]{4,3,2,1,0:T(8,128)} %param.13) | copy-start | bytes 3145732
  88.5 6.1 %collective-permute-start.18 = (f32[2,16,512]{2,1,0:T(8,128)S(1)}, f32[2,16,512]{2,1,0:T(8,128)S(1)}, u32[]{:S(2)}, u32[]{:S(2)}) collective-permute-start(f32[2,16,512]{2,1,0:T(8,128)S(1)} %get-tuple-element.41), channel_id=1, source_target_pairs={{0,1},{1,2},{2,3},{3,0},{4,5},{5,6},{6,7},{7,4},{8,9},{9,10},{10,1... | collective-permute-start | bytes 196616 | tf_op jit(solution)/shard_map/ppermute | solution.py:407
  91.8 5.4 %collective-permute-start.19 = (f32[2,16,512]{2,1,0:T(8,128)S(1)}, f32[2,16,512]{2,1,0:T(8,128)S(1)}, u32[]{:S(2)}, u32[]{:S(2)}) collective-permute-start(f32[2,16,512]{2,1,0:T(8,128)S(1)} %get-tuple-element.42), channel_id=1, source_target_pairs={{0,2},{1,3},{2,0},{3,1},{4,6},{5,7},{6,4},{7,5},{8,10},{9,11},{10,... | collective-permute-start | bytes 196616 | tf_op jit(solution)/shard_map/ppermute | solution.py:407
  91.8 5.4 %collective-permute-start.20 = (f32[2,16,512]{2,1,0:T(8,128)S(1)}, f32[2,16,512]{2,1,0:T(8,128)S(1)}, u32[]{:S(2)}, u32[]{:S(2)}) collective-permute-start(f32[2,16,512]{2,1,0:T(8,128)S(1)} %get-tuple-element.43), channel_id=1, source_target_pairs={{0,3},{1,0},{2,1},{3,2},{4,7},{5,4},{6,5},{7,6},{8,11},{9,8},{10,9... | collective-permute-start | bytes 196616 | tf_op jit(solution)/shard_map/ppermute | solution.py:407
  97.2 5.2 %collective-permute-start.22 = (f32[2,8,512]{2,1,0:T(8,128)S(1)}, f32[2,8,512]{2,1,0:T(8,128)S(1)}, u32[]{:S(2)}, u32[]{:S(2)}) collective-permute-start(f32[2,8,512]{2,1,0:T(8,128)S(1)} %get-tuple-element.50), channel_id=1, source_target_pairs={{4,0},{8,4},{12,8},{16,12},{20,16},{24,20},{28,24},{5,1},{9,5},{13... | collective-permute-start | bytes 98312 | tf_op jit(solution)/shard_map/ppermute | solution.py:347
  100.5 5.2 %collective-permute-start.21 = (f32[2,8,512]{2,1,0:T(8,128)S(1)}, f32[2,8,512]{2,1,0:T(8,128)S(1)}, u32[]{:S(2)}, u32[]{:S(2)}) collective-permute-start(f32[2,8,512]{2,1,0:T(8,128)S(1)} %get-tuple-element.51), channel_id=1, source_target_pairs={{0,4},{4,8},{8,12},{12,16},{16,20},{20,24},{24,28},{1,5},{5,9},{9,... | collective-permute-start | bytes 98312 | tf_op jit(solution)/shard_map/ppermute | solution.py:346
  108.6 9.5 %collective-permute-start.25 = (f32[2,16,512]{2,1,0:T(8,128)S(1)}, f32[2,16,512]{2,1,0:T(8,128)S(1)}, u32[]{:S(2)}, u32[]{:S(2)}) collective-permute-start(f32[2,16,512]{2,1,0:T(8,128)S(1)} %get-tuple-element.44), channel_id=1, source_target_pairs={{0,3},{1,0},{2,1},{3,2},{4,7},{5,4},{6,5},{7,6},{8,11},{9,8},{10,9... | collective-permute-start | bytes 196616 | tf_op jit(solution)/shard_map/ppermute | solution.py:417
  110.5 7.6 %collective-permute-start.24 = (f32[2,16,512]{2,1,0:T(8,128)S(1)}, f32[2,16,512]{2,1,0:T(8,128)S(1)}, u32[]{:S(2)}, u32[]{:S(2)}) collective-permute-start(f32[2,16,512]{2,1,0:T(8,128)S(1)} %get-tuple-element.44), channel_id=1, source_target_pairs={{0,2},{1,3},{2,0},{3,1},{4,6},{5,7},{6,4},{7,5},{8,10},{9,11},{10,... | collective-permute-start | bytes 196616 | tf_op jit(solution)/shard_map/ppermute | solution.py:417
  112.0 6.1 %collective-permute-start.23 = (f32[2,16,512]{2,1,0:T(8,128)S(1)}, f32[2,16,512]{2,1,0:T(8,128)S(1)}, u32[]{:S(2)}, u32[]{:S(2)}) collective-permute-start(f32[2,16,512]{2,1,0:T(8,128)S(1)} %get-tuple-element.44), channel_id=1, source_target_pairs={{0,1},{1,2},{2,3},{3,0},{4,5},{5,6},{6,7},{7,4},{8,9},{9,10},{10,1... | collective-permute-start | bytes 196616 | tf_op jit(solution)/shard_map/ppermute | solution.py:417
  118.1 14.5 %collective-permute-start.27 = (f32[8,16,512]{2,1,0:T(8,128)S(1)}, f32[8,16,512]{2,1,0:T(8,128)S(1)}, u32[]{:S(2)}, u32[]{:S(2)}) collective-permute-start(f32[8,16,512]{2,1,0:T(8,128)S(1)} %constant_dynamic-update-slice_fusion.refs_7_), channel_id=1, source_target_pairs={{4,0},{8,4},{12,8},{16,12},{20,16},{24,20},{28,24},{5,1},{9,5},{13... | collective-permute-start | bytes 786440 | tf_op jit(solution)/shard_map/ppermute | solution.py:347
  120.0 32.6 %collective-permute-start.15 = (f32[4,4,16,512]{3,2,1,0:T(8,128)S(1)}, f32[4,4,16,512]{3,2,1,0:T(8,128)S(1)}, u32[]{:S(2)}, u32[]{:S(2)}) collective-permute-start(f32[4,4,16,512]{3,2,1,0:T(8,128)S(1)} %get-tuple-element.38.refs_1_), channel_id=1, source_target_pairs={{4,0},{8,4},{12,8},{16,12},{20,16},{24,20},{28,24},{5,1},{9,5},{13... | collective-permute-start | bytes 1572872 | tf_op jit(solution)/shard_map/ppermute | solution.py:347
  125.1 27.6 %collective-permute-start.14 = (f32[4,4,16,512]{3,2,1,0:T(8,128)S(1)}, f32[4,4,16,512]{3,2,1,0:T(8,128)S(1)}, u32[]{:S(2)}, u32[]{:S(2)}) collective-permute-start(f32[4,4,16,512]{3,2,1,0:T(8,128)S(1)} %get-tuple-element.38.refs_1_), channel_id=1, source_target_pairs={{0,4},{4,8},{8,12},{12,16},{16,20},{20,24},{24,28},{1,5},{5,9},{9,... | collective-permute-start | bytes 1572872 | tf_op jit(solution)/shard_map/ppermute | solution.py:346
  127.0 25.7 %collective-permute-start.17 = (f32[4,4,16,512]{3,2,1,0:T(8,128)S(1)}, f32[4,4,16,512]{3,2,1,0:T(8,128)S(1)}, u32[]{:S(2)}, u32[]{:S(2)}) collective-permute-start(f32[4,4,16,512]{3,2,1,0:T(8,128)S(1)} %get-tuple-element.39.refs_4_), channel_id=1, source_target_pairs={{4,0},{8,4},{12,8},{16,12},{20,16},{24,20},{28,24},{5,1},{9,5},{13... | collective-permute-start | bytes 1572872 | tf_op jit(solution)/shard_map/ppermute | solution.py:347
  130.6 22.0 %collective-permute-start.16 = (f32[4,4,16,512]{3,2,1,0:T(8,128)S(1)}, f32[4,4,16,512]{3,2,1,0:T(8,128)S(1)}, u32[]{:S(2)}, u32[]{:S(2)}) collective-permute-start(f32[4,4,16,512]{3,2,1,0:T(8,128)S(1)} %get-tuple-element.39.refs_4_), channel_id=1, source_target_pairs={{0,4},{4,8},{8,12},{12,16},{16,20},{20,24},{24,28},{1,5},{5,9},{9,... | collective-permute-start | bytes 1572872 | tf_op jit(solution)/shard_map/ppermute | solution.py:346
  132.6 20.1 %collective-permute-start.26 = (f32[8,16,512]{2,1,0:T(8,128)S(1)}, f32[8,16,512]{2,1,0:T(8,128)S(1)}, u32[]{:S(2)}, u32[]{:S(2)}) collective-permute-start(f32[8,16,512]{2,1,0:T(8,128)S(1)} %constant_dynamic-update-slice_fusion.refs_7_), channel_id=1, source_target_pairs={{0,4},{4,8},{8,12},{12,16},{16,20},{20,24},{24,28},{1,5},{5,9},{9,... | collective-permute-start | bytes 786440 | tf_op jit(solution)/shard_map/ppermute | solution.py:346
  (9 other events, 49.8 us)

commit v4 on v3

--- a/solution.py
+++ b/solution.py
@@ -142,7 +142,7 @@
 
 def gradient_of(planes, controls, sums, adjoints, tables):
     fields, _, _, _ = controls.shape
-    step = 2 if fields % 2 == 0 else 1
+    step = fields
     block = lambda a: pl.BlockSpec((step,) + a.shape[1:], lambda f: (f, 0, 0, 0))
     return pl.pallas_call(
         functools.partial(gradient_kernel, planes),
@@ -413,9 +413,10 @@
     departure, adjoint = transport(
         (inc_top, increment, inc_bot), (top, flat, bot), obs_weight, innovation, used
     )
-    full = jnp.concatenate(
-        [adjoint] + [lax.ppermute(adjoint, "member", turn(k)) for k in range(1, planes)], axis=0
-    )
+    gathered = [adjoint]
+    for k in range(1, planes):
+        gathered.append(lax.ppermute(adjoint, "member", turn(k)))
+    full = jnp.concatenate(gathered, axis=0)
     adj_top, adj_bot = beside(full, 1, PASSES)
     gradient = gradient_of(planes, controls, sums_ext, (adj_top, full, adj_bot), tables)
     return (gradient, departure)

time: 161 us -> 161 us (level)
  no operation moved by 1% of the time
where the time goes in v4:
time: 161 us; the launch traced here: 160 us
  starting transfers between devices  70.7 us (44%)
  waiting for transfers between devices  47.5 us (30%)
  Pallas kernels  35.1 us (22%)
  local copies, waits for them, and re-layouts  3.6 us (2%)
  other arithmetic  2.31 us (1%)
    ppermute x6, starting transfers between devices, shards(): up[p] = lax.ppermute(rise, 'member', [(i, i + 1) for i in range(t + 1)])  26.4 us
    ppermute x4, waiting for transfers between devices, beside(): lax.ppermute(lax.slice_in_dim(block, extent - depth, extent, axis=dim), a...  21.3 us
    ppermute x4, starting transfers between devices, beside(): lax.ppermute(lax.slice_in_dim(block, 0, depth, axis=dim), axis, backward)  13.8 us
    ppermute x6, waiting for transfers between devices, shards(): up[p] = lax.ppermute(rise, 'member', [(i, i + 1) for i in range(t + 1)])  13.3 us
    pallas_call x4, Pallas kernels, forward_sums(): pl.pallas_call(forward_kernel, grid_spec=pltpu.PrefetchScalarGridSpec(num...  8.9 us
    pallas_call x1, Pallas kernels, smooth(): pl.pallas_call(smooth_kernel, grid=(fields // step,), in_specs=[halo, blo...  7.98 us
    ppermute x6, starting transfers between devices, shards(): lax.ppermute(fall, 'member', [(planes - 1 - i, planes - 2 - i) for i in r...  7.92 us
    ppermute x4, starting transfers between devices, beside(): lax.ppermute(lax.slice_in_dim(block, extent - depth, extent, axis=dim), a...  7.86 us
  transfers between devices with their start and end apart: 28, of which 11 were waited for; matrix products, arithmetic and copies ran while one was open for 0% of the time, Pallas kernels for 15%

profile of v4, /device:TPU:6, one launch (start us, length us, event | category | flops | bytes accessed | tf_op | source)
XLA Modules:
  0.0 160.3 jit_solution(11200268378133460715)
XLA Ops:
  2.2 2.1 %fusion.3 = (f32[100,8,512]{2,1,0:T(8,128)}, f32[100,8,512]{2,1,0:T(8,128)}) fusion(f32[64,8,512]{2,1,0:T(8,128)S(1)} %bitcast.11, f32[2,8,512]{2,1,0:T(8,128)S(1)} %get-tuple-element.57, f32[2,8,512]{2,1,0:T(8,128)S(1)} %get-tuple-element.52, f32[32,8,512]{2,1,0:T(8,128)S(1)} %bitcast.12, f32[2,8,512]{2,1,0:T(8,128)S(1)} %get-tuple-element.56, ...), kind=kLoop, calls=%fused_computation.5 | loop fusion | flops 2457600 | bytes 5505024 | tf_op jit(solution)/shard_map/concatenate | solution.py:376
  6.3 3.6 %collective-permute-start = (f32[100,8,512]{2,1,0:T(8,128)}, f32[100,8,512]{2,1,0:T(8,128)}, u32[]{:S(2)}, u32[]{:S(2)}) collective-permute-start(f32[100,8,512]{2,1,0:T(8,128)} %get-tuple-element.47), channel_id=1, source_target_pairs={{0,4},{4,8},{8,12},{12,16},{16,20},{20,24},{24,28},{1,5},{5,9},{9,... | collective-permute-start | bytes 4915208 | tf_op jit(solution)/shard_map/ppermute | solution.py:381
  9.9 3.8 %member_sums.3 = (f32[16,4,16,512]{3,2,1,0:T(8,128)}, f32[4,4,16,512]{3,2,1,0:T(8,128)}, f32[4,4,16,512]{3,2,1,0:T(8,128)}) custom-call(s32[64]{0:T(128)} %assign_ref.3, f32[16,8,16,512]{3,2,1,0:T(8,128)} %members_ref.3), custom_call_target="tpu_custom_call" | custom-call | flops 10000000 | bytes 4194304 | tf_op jit(solution)/shard_map/member_sums/pallas_call | solution.py:180
  13.6 4.3 %collective-permute-start.8 = (f32[4,4,16,512]{3,2,1,0:T(8,128)}, f32[4,4,16,512]{3,2,1,0:T(8,128)}, u32[]{:S(2)}, u32[]{:S(2)}) collective-permute-start(f32[4,4,16,512]{3,2,1,0:T(8,128)} %get-tuple-element.32), channel_id=1, source_target_pairs={{0,1},{4,5},{8,9},{12,13},{16,17},{20,21},{24,25},{28,29}} | collective-permute-start | bytes 1572872 | tf_op jit(solution)/shard_map/ppermute | solution.py:396
  19.6 3.8 %member_sums.2 = (f32[16,4,16,512]{3,2,1,0:T(8,128)}, f32[4,4,16,512]{3,2,1,0:T(8,128)}, f32[4,4,16,512]{3,2,1,0:T(8,128)}) custom-call(s32[64]{0:T(128)} %assign_ref.3, f32[16,8,16,512]{3,2,1,0:T(8,128)} %members_ref.3), custom_call_target="tpu_custom_call" | custom-call | flops 10000000 | bytes 4194304 | tf_op jit(solution)/shard_map/member_sums/pallas_call | solution.py:180
  23.3 2.1 %collective-permute-start.2 = (f32[4,4,16,512]{3,2,1,0:T(8,128)}, f32[4,4,16,512]{3,2,1,0:T(8,128)}, u32[]{:S(2)}, u32[]{:S(2)}) collective-permute-start(f32[4,4,16,512]{3,2,1,0:T(8,128)} %get-tuple-element.25), channel_id=1, source_target_pairs={{0,1},{4,5},{8,9},{12,13},{16,17},{20,21},{24,25},{28,29}} | collective-permute-start | bytes 1572872 | tf_op jit(solution)/shard_map/ppermute | solution.py:396
  25.5 4.2 %collective-permute-done.8.up_ref = f32[4,4,16,512]{3,2,1,0:T(8,128)} collective-permute-done((f32[4,4,16,512]{3,2,1,0:T(8,128)}, f32[4,4,16,512]{3,2,1,0:T(8,128)}, u32[]{:S(2)}, u32[]{:S(2)}) %collective-permute-start.8) | collective-permute-done | bytes 524320 | tf_op jit(solution)/shard_map/ppermute | solution.py:396
  30.5 2.7 %forward_sums.6 = (f32[4,4,16,512]{3,2,1,0:T(8,128)S(1)}, f32[4,4,16,512]{3,2,1,0:T(8,128)}) custom-call(s32[2]{0:T(128)S(1)} %add_clamp_fusion.1.index_ref, f32[16,4,16,512]{3,2,1,0:T(8,128)S(1)} %copy-done, f32[16,4,16,512]{3,2,1,0:T(8,128)S(1)} %copy-done, f32[4,4,16,512]{3,2,1,0:T(8,128)} %collective-permute-done.8.up_ref, ...), custom_call_target="tpu_custom_call" | custom-call | flops 1000000 | bytes 3145728 | tf_op jit(solution)/shard_map/forward_sums/pallas_call | solution.py:209
  33.2 4.4 %collective-permute-start.10 = (f32[4,4,16,512]{3,2,1,0:T(8,128)S(1)}, f32[4,4,16,512]{3,2,1,0:T(8,128)S(1)}, u32[]{:S(2)}, u32[]{:S(2)}) collective-permute-start(f32[4,4,16,512]{3,2,1,0:T(8,128)S(1)} %get-tuple-element.34), channel_id=1, source_target_pairs={{0,1},{1,2},{4,5},{5,6},{8,9},{9,10},{12,13},{13,14},{16,17},{17,1... | collective-permute-start | bytes 1572872 | tf_op jit(solution)/shard_map/ppermute | solution.py:396
  37.6 3.4 %collective-permute-done.2.up_ref = f32[4,4,16,512]{3,2,1,0:T(8,128)} collective-permute-done((f32[4,4,16,512]{3,2,1,0:T(8,128)}, f32[4,4,16,512]{3,2,1,0:T(8,128)}, u32[]{:S(2)}, u32[]{:S(2)}) %collective-permute-start.2) | collective-permute-done | bytes 524320 | tf_op jit(solution)/shard_map/ppermute | solution.py:396
  42.4 2.6 %forward_sums.4 = (f32[4,4,16,512]{3,2,1,0:T(8,128)}, f32[4,4,16,512]{3,2,1,0:T(8,128)}) custom-call(s32[2]{0:T(128)S(1)} %add_clamp_fusion.1.index_ref, f32[16,4,16,512]{3,2,1,0:T(8,128)S(1)} %copy-done.1, f32[16,4,16,512]{3,2,1,0:T(8,128)S(1)} %copy-done.1, f32[4,4,16,512]{3,2,1,0:T(8,128)} %collective-permute-done.2.up_ref, ...), custom_call_target="tpu_custom_call" | custom-call | flops 1000000 | bytes 3145728 | tf_op jit(solution)/shard_map/forward_sums/pallas_call | solution.py:209
  45.1 5.0 %collective-permute-start.4 = (f32[4,4,16,512]{3,2,1,0:T(8,128)}, f32[4,4,16,512]{3,2,1,0:T(8,128)}, u32[]{:S(2)}, u32[]{:S(2)}) collective-permute-start(f32[4,4,16,512]{3,2,1,0:T(8,128)} %get-tuple-element.27), channel_id=1, source_target_pairs={{0,1},{1,2},{4,5},{5,6},{8,9},{9,10},{12,13},{13,14},{16,17},{17,1... | collective-permute-start | bytes 1572872 | tf_op jit(solution)/shard_map/ppermute | solution.py:396
  50.1 2.0 %collective-permute-done.10.up_ref = f32[4,4,16,512]{3,2,1,0:T(8,128)S(1)} collective-permute-done((f32[4,4,16,512]{3,2,1,0:T(8,128)S(1)}, f32[4,4,16,512]{3,2,1,0:T(8,128)S(1)}, u32[]{:S(2)}, u32[]{:S(2)}) %collective-permute-start.10) | collective-permute-done | bytes 524320 | tf_op jit(solution)/shard_map/ppermute | solution.py:396
  57.3 4.3 %collective-permute-start.12 = (f32[4,4,16,512]{3,2,1,0:T(8,128)S(1)}, f32[4,4,16,512]{3,2,1,0:T(8,128)S(1)}, u32[]{:S(2)}, u32[]{:S(2)}) collective-permute-start(f32[4,4,16,512]{3,2,1,0:T(8,128)S(1)} %get-tuple-element.36), channel_id=1, source_target_pairs={{0,1},{1,2},{2,3},{4,5},{5,6},{6,7},{8,9},{9,10},{10,11},{12,13},{... | collective-permute-start | bytes 1572872 | tf_op jit(solution)/shard_map/ppermute | solution.py:396
  66.7 6.3 %collective-permute-start.6 = (f32[4,4,16,512]{3,2,1,0:T(8,128)S(1)}, f32[4,4,16,512]{3,2,1,0:T(8,128)S(1)}, u32[]{:S(2)}, u32[]{:S(2)}) collective-permute-start(f32[4,4,16,512]{3,2,1,0:T(8,128)S(1)} %get-tuple-element.29), channel_id=1, source_target_pairs={{0,1},{1,2},{2,3},{4,5},{5,6},{6,7},{8,9},{9,10},{10,11},{12,13},{... | collective-permute-start | bytes 1572872 | tf_op jit(solution)/shard_map/ppermute | solution.py:396
  74.4 8.0 %smooth.1.field_ref = f32[4,8,16,512]{3,2,1,0:T(8,128)S(1)} custom-call(f32[100,8,512]{2,1,0:T(8,128)} %collective-permute-done.top_ref, f32[4,8,16,512]{3,2,1,0:T(8,128)S(1)} %copy-done.4, f32[100,8,512]{2,1,0:T(8,128)} %collective-permute-done.1.bot_ref, bf16[2,512,512]{2,1,0:T(8,128)(2,1)S(1)} %copy-done.9, bf16[3,2,192,192]{3,2,1,0:T(8,128)(2,1)S(1)} %copy-done.10, ...), custom_call_target="tpu_custom_call" | custom-call | flops 5000000000 | bytes 4194304 | tf_op jit(solution)/shard_map/smooth/pallas_call | solution.py:131
  84.2 4.0 %collective-permute-done.7.refs_2_ = f32[4,4,16,512]{3,2,1,0:T(8,128)S(1)} collective-permute-done((f32[4,4,16,512]{3,2,1,0:T(8,128)S(1)}, f32[4,4,16,512]{3,2,1,0:T(8,128)S(1)}, u32[]{:S(2)}, u32[]{:S(2)}) %collective-permute-start.7) | collective-permute-done | bytes 524320 | tf_op jit(solution)/shard_map/ppermute | solution.py:397
  88.5 3.3 %collective-permute-start.18 = (f32[2,16,512]{2,1,0:T(8,128)S(1)}, f32[2,16,512]{2,1,0:T(8,128)S(1)}, u32[]{:S(2)}, u32[]{:S(2)}) collective-permute-start(f32[2,16,512]{2,1,0:T(8,128)S(1)} %get-tuple-element.41), channel_id=1, source_target_pairs={{0,1},{1,2},{2,3},{3,0},{4,5},{5,6},{6,7},{7,4},{8,9},{9,10},{10,1... | collective-permute-start | bytes 196616 | tf_op jit(solution)/shard_map/ppermute | solution.py:407
  91.8 2.4 %collective-permute-start.20 = (f32[2,16,512]{2,1,0:T(8,128)S(1)}, f32[2,16,512]{2,1,0:T(8,128)S(1)}, u32[]{:S(2)}, u32[]{:S(2)}) collective-permute-start(f32[2,16,512]{2,1,0:T(8,128)S(1)} %get-tuple-element.43), channel_id=1, source_target_pairs={{0,3},{1,0},{2,1},{3,2},{4,7},{5,4},{6,5},{7,6},{8,11},{9,8},{10,9... | collective-permute-start | bytes 196616 | tf_op jit(solution)/shard_map/ppermute | solution.py:407
  94.6 2.6 %collective-permute-done.19 = f32[2,16,512]{2,1,0:T(8,128)S(1)} collective-permute-done((f32[2,16,512]{2,1,0:T(8,128)S(1)}, f32[2,16,512]{2,1,0:T(8,128)S(1)}, u32[]{:S(2)}, u32[]{:S(2)}) %collective-permute-start.19) | collective-permute-done | bytes 65568 | tf_op jit(solution)/shard_map/ppermute | solution.py:407
  97.2 3.2 %collective-permute-start.22 = (f32[2,8,512]{2,1,0:T(8,128)S(1)}, f32[2,8,512]{2,1,0:T(8,128)S(1)}, u32[]{:S(2)}, u32[]{:S(2)}) collective-permute-start(f32[2,8,512]{2,1,0:T(8,128)S(1)} %get-tuple-element.50), channel_id=1, source_target_pairs={{4,0},{8,4},{12,8},{16,12},{20,16},{24,20},{28,24},{5,1},{9,5},{13... | collective-permute-start | bytes 98312 | tf_op jit(solution)/shard_map/ppermute | solution.py:347
  100.5 1.9 %collective-permute-start.21 = (f32[2,8,512]{2,1,0:T(8,128)S(1)}, f32[2,8,512]{2,1,0:T(8,128)S(1)}, u32[]{:S(2)}, u32[]{:S(2)}) collective-permute-start(f32[2,8,512]{2,1,0:T(8,128)S(1)} %get-tuple-element.51), channel_id=1, source_target_pairs={{0,4},{4,8},{8,12},{12,16},{16,20},{20,24},{24,28},{1,5},{5,9},{9,... | collective-permute-start | bytes 98312 | tf_op jit(solution)/shard_map/ppermute | solution.py:346
  102.4 3.3 %collective-permute-done.21.inc_top = f32[2,8,512]{2,1,0:T(8,128)S(1)} collective-permute-done((f32[2,8,512]{2,1,0:T(8,128)S(1)}, f32[2,8,512]{2,1,0:T(8,128)S(1)}, u32[]{:S(2)}, u32[]{:S(2)}) %collective-permute-start.21) | collective-permute-done | bytes 32800 | tf_op jit(solution)/shard_map/ppermute | solution.py:346
  105.7 2.8 %transport.1 = (f32[2,16,512]{2,1,0:T(8,128)}, f32[2,16,512]{2,1,0:T(8,128)S(1)}) custom-call(f32[2,8,512]{2,1,0:T(8,128)S(1)} %collective-permute-done.21.inc_top, f32[2,16,512]{2,1,0:T(8,128)S(1)} %add_add_fusion.inc_own, f32[2,8,512]{2,1,0:T(8,128)S(1)} %collective-permute-done.22.inc_bot, f32[100,8,512]{2,1,0:T(8,128)} %collective-permute-done.top_ref, ...), custom_call_target="tpu_custom_call" | custom-call | flops 100000000 | bytes 3145728 | tf_op jit(solution)/shard_map/transport/pallas_call | solution.py:329
  108.6 1.9 %collective-permute-start.25 = (f32[2,16,512]{2,1,0:T(8,128)S(1)}, f32[2,16,512]{2,1,0:T(8,128)S(1)}, u32[]{:S(2)}, u32[]{:S(2)}) collective-permute-start(f32[2,16,512]{2,1,0:T(8,128)S(1)} %get-tuple-element.44), channel_id=1, source_target_pairs={{0,3},{1,0},{2,1},{3,2},{4,7},{5,4},{6,5},{7,6},{8,11},{9,8},{10,9... | collective-permute-start | bytes 196616 | tf_op jit(solution)/shard_map/ppermute | solution.py:418
  112.0 6.1 %collective-permute-done.23 = f32[2,16,512]{2,1,0:T(8,128)S(1)} collective-permute-done((f32[2,16,512]{2,1,0:T(8,128)S(1)}, f32[2,16,512]{2,1,0:T(8,128)S(1)}, u32[]{:S(2)}, u32[]{:S(2)}) %collective-permute-start.23) | collective-permute-done | bytes 65568 | tf_op jit(solution)/shard_map/ppermute | solution.py:418
  118.1 1.9 %collective-permute-start.27 = (f32[8,16,512]{2,1,0:T(8,128)S(1)}, f32[8,16,512]{2,1,0:T(8,128)S(1)}, u32[]{:S(2)}, u32[]{:S(2)}) collective-permute-start(f32[8,16,512]{2,1,0:T(8,128)S(1)} %constant_dynamic-update-slice_fusion.refs_7_), channel_id=1, source_target_pairs={{4,0},{8,4},{12,8},{16,12},{20,16},{24,20},{28,24},{5,1},{9,5},{13... | collective-permute-start | bytes 786440 | tf_op jit(solution)/shard_map/ppermute | solution.py:347
  120.0 5.0 %collective-permute-start.15 = (f32[4,4,16,512]{3,2,1,0:T(8,128)S(1)}, f32[4,4,16,512]{3,2,1,0:T(8,128)S(1)}, u32[]{:S(2)}, u32[]{:S(2)}) collective-permute-start(f32[4,4,16,512]{3,2,1,0:T(8,128)S(1)} %get-tuple-element.38.refs_1_), channel_id=1, source_target_pairs={{4,0},{8,4},{12,8},{16,12},{20,16},{24,20},{28,24},{5,1},{9,5},{13... | collective-permute-start | bytes 1572872 | tf_op jit(solution)/shard_map/ppermute | solution.py:347
  127.0 3.6 %collective-permute-start.17 = (f32[4,4,16,512]{3,2,1,0:T(8,128)S(1)}, f32[4,4,16,512]{3,2,1,0:T(8,128)S(1)}, u32[]{:S(2)}, u32[]{:S(2)}) collective-permute-start(f32[4,4,16,512]{3,2,1,0:T(8,128)S(1)} %get-tuple-element.39.refs_4_), channel_id=1, source_target_pairs={{4,0},{8,4},{12,8},{16,12},{20,16},{24,20},{28,24},{5,1},{9,5},{13... | collective-permute-start | bytes 1572872 | tf_op jit(solution)/shard_map/ppermute | solution.py:347
  132.6 2.1 %collective-permute-start.26 = (f32[8,16,512]{2,1,0:T(8,128)S(1)}, f32[8,16,512]{2,1,0:T(8,128)S(1)}, u32[]{:S(2)}, u32[]{:S(2)}) collective-permute-start(f32[8,16,512]{2,1,0:T(8,128)S(1)} %constant_dynamic-update-slice_fusion.refs_7_), channel_id=1, source_target_pairs={{0,4},{4,8},{8,12},{12,16},{16,20},{20,24},{24,28},{1,5},{5,9},{9,... | collective-permute-start | bytes 786440 | tf_op jit(solution)/shard_map/ppermute | solution.py:346
  134.7 18.0 %collective-permute-done.26.refs_6_ = f32[8,16,512]{2,1,0:T(8,128)S(1)} collective-permute-done((f32[8,16,512]{2,1,0:T(8,128)S(1)}, f32[8,16,512]{2,1,0:T(8,128)S(1)}, u32[]{:S(2)}, u32[]{:S(2)}) %collective-permute-start.26) | collective-permute-done | bytes 262176 | tf_op jit(solution)/shard_map/ppermute | solution.py:346
  152.7 7.6 %gradient.1 = f32[4,8,16,512]{3,2,1,0:T(8,128)} custom-call(f32[4,8,16,512]{3,2,1,0:T(8,128)S(1)} %copy-done.4, f32[4,4,16,512]{3,2,1,0:T(8,128)S(1)} %collective-permute-done.14.refs_0_, f32[4,4,16,512]{3,2,1,0:T(8,128)S(1)} %get-tuple-element.38.refs_1_, f32[4,4,16,512]{3,2,1,0:T(8,128)S(1)} %collective-permute-done.15.refs_2_, ...), custom_call_target="tpu_custom_call" | custom-call | flops 5000000000 | bytes 5242880 | tf_op jit(solution)/shard_map/gradient/pallas_call | solution.py:147
  (71 shorter events, 26.7 us)
Async XLA Ops:
  4.4 68.7 %collective-permute-start.1 = (f32[100,8,512]{2,1,0:T(8,128)}, f32[100,8,512]{2,1,0:T(8,128)}, u32[]{:S(2)}, u32[]{:S(2)}) collective-permute-start(f32[100,8,512]{2,1,0:T(8,128)} %get-tuple-element.46), channel_id=1, source_target_pairs={{4,0},{8,4},{12,8},{16,12},{20,16},{24,20},{28,24},{5,1},{9,5},{13... | collective-permute-start | bytes 4915208 | tf_op jit(solution)/shard_map/ppermute | solution.py:382
  6.3 68.1 %collective-permute-start = (f32[100,8,512]{2,1,0:T(8,128)}, f32[100,8,512]{2,1,0:T(8,128)}, u32[]{:S(2)}, u32[]{:S(2)}) collective-permute-start(f32[100,8,512]{2,1,0:T(8,128)} %get-tuple-element.47), channel_id=1, source_target_pairs={{0,4},{4,8},{8,12},{12,16},{16,20},{20,24},{24,28},{1,5},{5,9},{9,... | collective-permute-start | bytes 4915208 | tf_op jit(solution)/shard_map/ppermute | solution.py:381
  13.6 16.1 %collective-permute-start.8 = (f32[4,4,16,512]{3,2,1,0:T(8,128)}, f32[4,4,16,512]{3,2,1,0:T(8,128)}, u32[]{:S(2)}, u32[]{:S(2)}) collective-permute-start(f32[4,4,16,512]{3,2,1,0:T(8,128)} %get-tuple-element.32), channel_id=1, source_target_pairs={{0,1},{4,5},{8,9},{12,13},{16,17},{20,21},{24,25},{28,29}} | collective-permute-start | bytes 1572872 | tf_op jit(solution)/shard_map/ppermute | solution.py:396
  17.9 12.5 %copy-start = (f32[16,4,16,512]{3,2,1,0:T(8,128)S(1)}, f32[16,4,16,512]{3,2,1,0:T(8,128)}, u32[]{:S(2)}) copy-start(f32[16,4,16,512]{3,2,1,0:T(8,128)} %get-tuple-element.31.rise_ref.fall_ref.refs_3_) | copy-start | bytes 6291460
  17.9 12.5 %collective-permute-start.9 = (f32[4,4,16,512]{3,2,1,0:T(8,128)}, f32[4,4,16,512]{3,2,1,0:T(8,128)}, u32[]{:S(2)}, u32[]{:S(2)}) collective-permute-start(f32[4,4,16,512]{3,2,1,0:T(8,128)} %get-tuple-element.33), channel_id=1, source_target_pairs={{3,2},{7,6},{11,10},{15,14},{19,18},{23,22},{27,26},{31,30}} | collective-permute-start | bytes 1572872 | tf_op jit(solution)/shard_map/ppermute | solution.py:397
  23.3 17.6 %collective-permute-start.2 = (f32[4,4,16,512]{3,2,1,0:T(8,128)}, f32[4,4,16,512]{3,2,1,0:T(8,128)}, u32[]{:S(2)}, u32[]{:S(2)}) collective-permute-start(f32[4,4,16,512]{3,2,1,0:T(8,128)} %get-tuple-element.25), channel_id=1, source_target_pairs={{0,1},{4,5},{8,9},{12,13},{16,17},{20,21},{24,25},{28,29}} | collective-permute-start | bytes 1572872 | tf_op jit(solution)/shard_map/ppermute | solution.py:396
  29.7 12.7 %collective-permute-start.3 = (f32[4,4,16,512]{3,2,1,0:T(8,128)}, f32[4,4,16,512]{3,2,1,0:T(8,128)S(1)}, u32[]{:S(2)}, u32[]{:S(2)}) collective-permute-start(f32[4,4,16,512]{3,2,1,0:T(8,128)} %get-tuple-element.26), channel_id=1, source_target_pairs={{3,2},{7,6},{11,10},{15,14},{19,18},{23,22},{27,26},{31,30}} | collective-permute-start | bytes 1572872 | tf_op jit(solution)/shard_map/ppermute | solution.py:397
  30.4 12.0 %copy-start.1 = (f32[16,4,16,512]{3,2,1,0:T(8,128)S(1)}, f32[16,4,16,512]{3,2,1,0:T(8,128)}, u32[]{:S(2)}) copy-start(f32[16,4,16,512]{3,2,1,0:T(8,128)} %get-tuple-element.24.rise_ref.fall_ref.refs_0_) | copy-start | bytes 6291460
  33.2 18.9 %collective-permute-start.10 = (f32[4,4,16,512]{3,2,1,0:T(8,128)S(1)}, f32[4,4,16,512]{3,2,1,0:T(8,128)S(1)}, u32[]{:S(2)}, u32[]{:S(2)}) collective-permute-start(f32[4,4,16,512]{3,2,1,0:T(8,128)S(1)} %get-tuple-element.34), channel_id=1, source_target_pairs={{0,1},{1,2},{4,5},{5,6},{8,9},{9,10},{12,13},{13,14},{16,17},{17,1... | collective-permute-start | bytes 1572872 | tf_op jit(solution)/shard_map/ppermute | solution.py:396
  41.0 13.5 %collective-permute-start.11 = (f32[4,4,16,512]{3,2,1,0:T(8,128)}, f32[4,4,16,512]{3,2,1,0:T(8,128)}, u32[]{:S(2)}, u32[]{:S(2)}) collective-permute-start(f32[4,4,16,512]{3,2,1,0:T(8,128)} %get-tuple-element.35), channel_id=1, source_target_pairs={{3,2},{2,1},{7,6},{6,5},{11,10},{10,9},{15,14},{14,13},{19,18},{18... | collective-permute-start | bytes 1572872 | tf_op jit(solution)/shard_map/ppermute | solution.py:397
  45.1 18.4 %collective-permute-start.4 = (f32[4,4,16,512]{3,2,1,0:T(8,128)}, f32[4,4,16,512]{3,2,1,0:T(8,128)}, u32[]{:S(2)}, u32[]{:S(2)}) collective-permute-start(f32[4,4,16,512]{3,2,1,0:T(8,128)} %get-tuple-element.27), channel_id=1, source_target_pairs={{0,1},{1,2},{4,5},{5,6},{8,9},{9,10},{12,13},{13,14},{16,17},{17,1... | collective-permute-start | bytes 1572872 | tf_op jit(solution)/shard_map/ppermute | solution.py:396
  52.9 12.0 %collective-permute-start.5 = (f32[4,4,16,512]{3,2,1,0:T(8,128)}, f32[4,4,16,512]{3,2,1,0:T(8,128)}, u32[]{:S(2)}, u32[]{:S(2)}) collective-permute-start(f32[4,4,16,512]{3,2,1,0:T(8,128)} %get-tuple-element.28), channel_id=1, source_target_pairs={{3,2},{2,1},{7,6},{6,5},{11,10},{10,9},{15,14},{14,13},{19,18},{18... | collective-permute-start | bytes 1572872 | tf_op jit(solution)/shard_map/ppermute | solution.py:397
  57.3 25.1 %collective-permute-start.12 = (f32[4,4,16,512]{3,2,1,0:T(8,128)S(1)}, f32[4,4,16,512]{3,2,1,0:T(8,128)S(1)}, u32[]{:S(2)}, u32[]{:S(2)}) collective-permute-start(f32[4,4,16,512]{3,2,1,0:T(8,128)S(1)} %get-tuple-element.36), channel_id=1, source_target_pairs={{0,1},{1,2},{2,3},{4,5},{5,6},{6,7},{8,9},{9,10},{10,11},{12,13},{... | collective-permute-start | bytes 1572872 | tf_op jit(solution)/shard_map/ppermute | solution.py:396
  63.4 11.0 %copy-start.12 = (bf16[2,64,192]{2,1,0:T(8,128)(2,1)S(1)}, bf16[2,64,192]{2,1,0:T(8,128)(2,1)}, u32[]{:S(2)}) copy-start(bf16[2,64,192]{2,1,0:T(8,128)(2,1)} %constant.31.clone.bwd_ref.refs_11_) | copy-start | bytes 147460
  63.4 19.0 %collective-permute-start.13 = (f32[4,4,16,512]{3,2,1,0:T(8,128)S(1)}, f32[4,4,16,512]{3,2,1,0:T(8,128)S(1)}, u32[]{:S(2)}, u32[]{:S(2)}) collective-permute-start(f32[4,4,16,512]{3,2,1,0:T(8,128)S(1)} %get-tuple-element.37), channel_id=1, source_target_pairs={{3,2},{2,1},{1,0},{7,6},{6,5},{5,4},{11,10},{10,9},{9,8},{15,14},{... | collective-permute-start | bytes 1572872 | tf_op jit(solution)/shard_map/ppermute | solution.py:397
  66.7 17.5 %collective-permute-start.6 = (f32[4,4,16,512]{3,2,1,0:T(8,128)S(1)}, f32[4,4,16,512]{3,2,1,0:T(8,128)S(1)}, u32[]{:S(2)}, u32[]{:S(2)}) collective-permute-start(f32[4,4,16,512]{3,2,1,0:T(8,128)S(1)} %get-tuple-element.29), channel_id=1, source_target_pairs={{0,1},{1,2},{2,3},{4,5},{5,6},{6,7},{8,9},{9,10},{10,11},{12,13},{... | collective-permute-start | bytes 1572872 | tf_op jit(solution)/shard_map/ppermute | solution.py:396
  73.1 15.1 %collective-permute-start.7 = (f32[4,4,16,512]{3,2,1,0:T(8,128)S(1)}, f32[4,4,16,512]{3,2,1,0:T(8,128)S(1)}, u32[]{:S(2)}, u32[]{:S(2)}) collective-permute-start(f32[4,4,16,512]{3,2,1,0:T(8,128)S(1)} %get-tuple-element.30), channel_id=1, source_target_pairs={{3,2},{2,1},{1,0},{7,6},{6,5},{5,4},{11,10},{10,9},{9,8},{15,14},{... | collective-permute-start | bytes 1572872 | tf_op jit(solution)/shard_map/ppermute | solution.py:397
  88.2 17.5 %copy-start.3 = (f32[4,4,2,16,512]{4,3,2,1,0:T(8,128)S(1)}, f32[4,4,2,16,512]{4,3,2,1,0:T(8,128)}, u32[]{:S(2)}) copy-start(f32[4,4,2,16,512]{4,3,2,1,0:T(8,128)} %param.13) | copy-start | bytes 3145732
  88.5 6.1 %collective-permute-start.18 = (f32[2,16,512]{2,1,0:T(8,128)S(1)}, f32[2,16,512]{2,1,0:T(8,128)S(1)}, u32[]{:S(2)}, u32[]{:S(2)}) collective-permute-start(f32[2,16,512]{2,1,0:T(8,128)S(1)} %get-tuple-element.41), channel_id=1, source_target_pairs={{0,1},{1,2},{2,3},{3,0},{4,5},{5,6},{6,7},{7,4},{8,9},{9,10},{10,1... | collective-permute-start | bytes 196616 | tf_op jit(solution)/shard_map/ppermute | solution.py:407
  91.8 5.4 %collective-permute-start.19 = (f32[2,16,512]{2,1,0:T(8,128)S(1)}, f32[2,16,512]{2,1,0:T(8,128)S(1)}, u32[]{:S(2)}, u32[]{:S(2)}) collective-permute-start(f32[2,16,512]{2,1,0:T(8,128)S(1)} %get-tuple-element.42), channel_id=1, source_target_pairs={{0,2},{1,3},{2,0},{3,1},{4,6},{5,7},{6,4},{7,5},{8,10},{9,11},{10,... | collective-permute-start | bytes 196616 | tf_op jit(solution)/shard_map/ppermute | solution.py:407
  91.8 5.4 %collective-permute-start.20 = (f32[2,16,512]{2,1,0:T(8,128)S(1)}, f32[2,16,512]{2,1,0:T(8,128)S(1)}, u32[]{:S(2)}, u32[]{:S(2)}) collective-permute-start(f32[2,16,512]{2,1,0:T(8,128)S(1)} %get-tuple-element.43), channel_id=1, source_target_pairs={{0,3},{1,0},{2,1},{3,2},{4,7},{5,4},{6,5},{7,6},{8,11},{9,8},{10,9... | collective-permute-start | bytes 196616 | tf_op jit(solution)/shard_map/ppermute | solution.py:407
  97.2 5.2 %collective-permute-start.22 = (f32[2,8,512]{2,1,0:T(8,128)S(1)}, f32[2,8,512]{2,1,0:T(8,128)S(1)}, u32[]{:S(2)}, u32[]{:S(2)}) collective-permute-start(f32[2,8,512]{2,1,0:T(8,128)S(1)} %get-tuple-element.50), channel_id=1, source_target_pairs={{4,0},{8,4},{12,8},{16,12},{20,16},{24,20},{28,24},{5,1},{9,5},{13... | collective-permute-start | bytes 98312 | tf_op jit(solution)/shard_map/ppermute | solution.py:347
  100.5 5.2 %collective-permute-start.21 = (f32[2,8,512]{2,1,0:T(8,128)S(1)}, f32[2,8,512]{2,1,0:T(8,128)S(1)}, u32[]{:S(2)}, u32[]{:S(2)}) collective-permute-start(f32[2,8,512]{2,1,0:T(8,128)S(1)} %get-tuple-element.51), channel_id=1, source_target_pairs={{0,4},{4,8},{8,12},{12,16},{16,20},{20,24},{24,28},{1,5},{5,9},{9,... | collective-permute-start | bytes 98312 | tf_op jit(solution)/shard_map/ppermute | solution.py:346
  108.6 9.5 %collective-permute-start.25 = (f32[2,16,512]{2,1,0:T(8,128)S(1)}, f32[2,16,512]{2,1,0:T(8,128)S(1)}, u32[]{:S(2)}, u32[]{:S(2)}) collective-permute-start(f32[2,16,512]{2,1,0:T(8,128)S(1)} %get-tuple-element.44), channel_id=1, source_target_pairs={{0,3},{1,0},{2,1},{3,2},{4,7},{5,4},{6,5},{7,6},{8,11},{9,8},{10,9... | collective-permute-start | bytes 196616 | tf_op jit(solution)/shard_map/ppermute | solution.py:418
  110.5 7.6 %collective-permute-start.24 = (f32[2,16,512]{2,1,0:T(8,128)S(1)}, f32[2,16,512]{2,1,0:T(8,128)S(1)}, u32[]{:S(2)}, u32[]{:S(2)}) collective-permute-start(f32[2,16,512]{2,1,0:T(8,128)S(1)} %get-tuple-element.44), channel_id=1, source_target_pairs={{0,2},{1,3},{2,0},{3,1},{4,6},{5,7},{6,4},{7,5},{8,10},{9,11},{10,... | collective-permute-start | bytes 196616 | tf_op jit(solution)/shard_map/ppermute | solution.py:418
  112.0 6.1 %collective-permute-start.23 = (f32[2,16,512]{2,1,0:T(8,128)S(1)}, f32[2,16,512]{2,1,0:T(8,128)S(1)}, u32[]{:S(2)}, u32[]{:S(2)}) collective-permute-start(f32[2,16,512]{2,1,0:T(8,128)S(1)} %get-tuple-element.44), channel_id=1, source_target_pairs={{0,1},{1,2},{2,3},{3,0},{4,5},{5,6},{6,7},{7,4},{8,9},{9,10},{10,1... | collective-permute-start | bytes 196616 | tf_op jit(solution)/shard_map/ppermute | solution.py:418
  118.1 14.5 %collective-permute-start.27 = (f32[8,16,512]{2,1,0:T(8,128)S(1)}, f32[8,16,512]{2,1,0:T(8,128)S(1)}, u32[]{:S(2)}, u32[]{:S(2)}) collective-permute-start(f32[8,16,512]{2,1,0:T(8,128)S(1)} %constant_dynamic-update-slice_fusion.refs_7_), channel_id=1, source_target_pairs={{4,0},{8,4},{12,8},{16,12},{20,16},{24,20},{28,24},{5,1},{9,5},{13... | collective-permute-start | bytes 786440 | tf_op jit(solution)/shard_map/ppermute | solution.py:347
  120.0 32.6 %collective-permute-start.15 = (f32[4,4,16,512]{3,2,1,0:T(8,128)S(1)}, f32[4,4,16,512]{3,2,1,0:T(8,128)S(1)}, u32[]{:S(2)}, u32[]{:S(2)}) collective-permute-start(f32[4,4,16,512]{3,2,1,0:T(8,128)S(1)} %get-tuple-element.38.refs_1_), channel_id=1, source_target_pairs={{4,0},{8,4},{12,8},{16,12},{20,16},{24,20},{28,24},{5,1},{9,5},{13... | collective-permute-start | bytes 1572872 | tf_op jit(solution)/shard_map/ppermute | solution.py:347
  125.1 27.6 %collective-permute-start.14 = (f32[4,4,16,512]{3,2,1,0:T(8,128)S(1)}, f32[4,4,16,512]{3,2,1,0:T(8,128)S(1)}, u32[]{:S(2)}, u32[]{:S(2)}) collective-permute-start(f32[4,4,16,512]{3,2,1,0:T(8,128)S(1)} %get-tuple-element.38.refs_1_), channel_id=1, source_target_pairs={{0,4},{4,8},{8,12},{12,16},{16,20},{20,24},{24,28},{1,5},{5,9},{9,... | collective-permute-start | bytes 1572872 | tf_op jit(solution)/shard_map/ppermute | solution.py:346
  127.0 25.7 %collective-permute-start.17 = (f32[4,4,16,512]{3,2,1,0:T(8,128)S(1)}, f32[4,4,16,512]{3,2,1,0:T(8,128)S(1)}, u32[]{:S(2)}, u32[]{:S(2)}) collective-permute-start(f32[4,4,16,512]{3,2,1,0:T(8,128)S(1)} %get-tuple-element.39.refs_4_), channel_id=1, source_target_pairs={{4,0},{8,4},{12,8},{16,12},{20,16},{24,20},{28,24},{5,1},{9,5},{13... | collective-permute-start | bytes 1572872 | tf_op jit(solution)/shard_map/ppermute | solution.py:347
  130.6 22.0 %collective-permute-start.16 = (f32[4,4,16,512]{3,2,1,0:T(8,128)S(1)}, f32[4,4,16,512]{3,2,1,0:T(8,128)S(1)}, u32[]{:S(2)}, u32[]{:S(2)}) collective-permute-start(f32[4,4,16,512]{3,2,1,0:T(8,128)S(1)} %get-tuple-element.39.refs_4_), channel_id=1, source_target_pairs={{0,4},{4,8},{8,12},{12,16},{16,20},{20,24},{24,28},{1,5},{5,9},{9,... | collective-permute-start | bytes 1572872 | tf_op jit(solution)/shard_map/ppermute | solution.py:346
  132.6 20.1 %collective-permute-start.26 = (f32[8,16,512]{2,1,0:T(8,128)S(1)}, f32[8,16,512]{2,1,0:T(8,128)S(1)}, u32[]{:S(2)}, u32[]{:S(2)}) collective-permute-start(f32[8,16,512]{2,1,0:T(8,128)S(1)} %constant_dynamic-update-slice_fusion.refs_7_), channel_id=1, source_target_pairs={{0,4},{4,8},{8,12},{12,16},{16,20},{20,24},{24,28},{1,5},{5,9},{9,... | collective-permute-start | bytes 786440 | tf_op jit(solution)/shard_map/ppermute | solution.py:346
  (9 other events, 49.8 us)
